TPU v7x, 512 devices: a whole 4x8x8 slice. The times are simulated.
512 devices in a mesh: row: 32 (over z_hi, y), col: 16 (over x, z_lo, core).
Axes of the slice: x: 4, y: 8, z: 8 (z_hi: 4, z_lo: 2; z = z_hi * 2 + z_lo), core: 2. Of those that a mesh axis runs over, the one named last changes fastest.
Arguments:
- sequence: bfloat16 [512, 1024], P('row'), may hold values from -6 to 6
- pair_state: bfloat16 [512, 512, 128], P('row', 'col'), may hold values from -6 to 6
- residue_mask: int32 [512], replicated, may hold values 0 or 1
- chain_index: int32 [512], replicated, may hold values from 0 to 3, never falling along the last dimension, each value on 1 to 256 neighbouring positions
- attention_in: bfloat16 [1024, 4, 1024], P(None, None, 'col'), may hold values from -0.1875 to 0.1875
- attention_out: bfloat16 [1024, 1024], P('col'), may hold values from -0.1875 to 0.1875
- bias_weight: bfloat16 [128, 32], replicated, may hold values from -40 to 40
- chain_bias: float32 [32], replicated, may hold values from -2 to 2
- outer_in: bfloat16 [1024, 128], replicated, may hold values from -0.1875 to 0.1875
- outer_out: bfloat16 [128, 128], replicated, may hold values from -0.5 to 0.5
- triangle_in: bfloat16 [128, 5, 128], replicated, may hold values from -0.5 to 0.5
- triangle_out: bfloat16 [128, 128], replicated, may hold values from -0.5 to 0.5
- transition_up: bfloat16 [128, 512], replicated, may hold values from -0.5 to 0.5
- transition_down: bfloat16 [512, 128], replicated, may hold values from -0.25 to 0.25
Outputs:
- sequence_out: bfloat16 [512, 1024], P('row')
- pair_out: bfloat16 [512, 512, 128], P('row', 'col')
Inputs may be any that keep to these rules, and one draw needn't show every extreme that they name: chain_index never falls along the residues; each chain holds at most 256 residues.
All inputs are finite; a program needn't handle non-finite values.
Results may differ from a plain program's by a relative error of at most 0.0095.
The roundings to bfloat16 on the way count: a program that leaves them out, or rounds other values in their place, can miss the bound.
Values may be sent and summed in bfloat16 or wider, within the bound.
No kernel may reach another device: no remote copies, remote signals or barrier semaphores. Data moves between devices by JAX's collectives and lax.ppermute only.
A program may use at most 64 MiB of HBM per device.

v0:
```python
import math

import jax
import jax.numpy as jnp
from jax import lax
from jax.sharding import Mesh
from jax.sharding import PartitionSpec as P

ROW = ("row_0", "row_1")


def in_one_piece(arrays, axis, dim, along):
    widths = [a.shape[along] for a in arrays]
    both = jnp.concatenate(arrays, axis=along)
    filled = lax.all_gather(both, axis, axis=dim, tiled=True)
    return tuple(jnp.split(filled, [sum(widths[:k]) for k in range(1, len(widths))], axis=along))


def from_everyone(value, axis):
    copies = jnp.broadcast_to(value, (lax.axis_size(axis), *value.shape))
    return lax.all_to_all(copies, axis, split_axis=0, concat_axis=0, tiled=True)


def over_copies(value, axis):
    everything = from_everyone(value, axis)
    return jnp.sum(everything, axis=0)


def laid_out(parts, dim):
    parts = jnp.moveaxis(parts, 0, dim)
    lengths = parts.shape
    return parts.reshape(*lengths[:dim], lengths[dim] * lengths[dim + 1], *lengths[dim + 2 :])


def gather_directly(value, axis, dim):
    return laid_out(from_everyone(value, axis), dim)


def gather_in_order(value, axes, order):
    parts = value[None]
    for k in order:
        parts = lax.all_gather(parts, axes[k], axis=0, tiled=True)
    current = [lax.axis_size(axes[k]) for k in reversed(order)]
    parts = parts.reshape(*current, *value.shape)
    turned = sorted(range(len(order)), key=lambda place: order[len(order) - 1 - place])
    return parts.transpose(*turned, *range(len(order), parts.ndim)).reshape(-1, *value.shape)


def gather_axes(value, axes, order, dim):
    return laid_out(gather_in_order(value, axes, order), dim)


def layer_norm(values):
    center = values - jnp.mean(values, axis=-1, keepdims=True)
    spread = jnp.mean(center * center, axis=-1, keepdims=True)
    return center * lax.rsqrt(spread + 1e-05)


def per_device(
    sequence,
    pair_state,
    residue_mask,
    chain_index,
    attention_in,
    attention_out,
    bias_weight,
    chain_bias,
    outer_in,
    outer_out,
    triangle_in,
    triangle_out,
    transition_up,
    transition_down,
):
    rows_here, cols_here, channels = pair_state.shape
    length_all = residue_mask.shape[0]
    row_index = lax.axis_index(ROW)
    col_index = lax.axis_index("col")
    row_start = row_index * rows_here
    col_start = col_index * cols_here
    pair_wide = pair_state.astype(jnp.float32)
    normed_pair = layer_norm(pair_wide).astype(jnp.bfloat16)
    bias_tile = jnp.einsum(
        "ijc,ch->hij", normed_pair, bias_weight, preferred_element_type=jnp.float32
    )
    pair_bias = lax.all_to_all(bias_tile, "col", split_axis=0, concat_axis=2, tiled=True)
    heads_here = pair_bias.shape[0]
    normed_seq = layer_norm(sequence.astype(jnp.float32)).astype(jnp.bfloat16)
    projected = jnp.einsum(
        "id,dpe->ipe", normed_seq, attention_in, preferred_element_type=jnp.float32
    )
    query = projected[:, 0].astype(jnp.bfloat16)
    key_rows = projected[:, 1].astype(jnp.bfloat16)
    value_rows = projected[:, 2].astype(jnp.bfloat16)
    gate = jax.nn.sigmoid(projected[:, 3])
    keys_all, values_all = in_one_piece((key_rows, value_rows), ROW, 0, 1)
    head_width = query.shape[1] // heads_here
    query_heads = query.reshape(rows_here, heads_here, head_width)
    key_heads = keys_all.reshape(length_all, heads_here, head_width)
    value_heads = values_all.reshape(length_all, heads_here, head_width)
    scale = 1.0 / math.sqrt(head_width)
    scores = (
        jnp.einsum("ihd,jhd->hij", query_heads, key_heads, preferred_element_type=jnp.float32)
        * scale
    )
    chain_rows = lax.dynamic_slice_in_dim(chain_index, row_start, rows_here, 0)
    same_chain = (chain_rows[:, None] == chain_index[None, :]).astype(jnp.float32)
    head_offset = lax.dynamic_slice_in_dim(chain_bias, col_index * heads_here, heads_here, 0)
    scores = scores + pair_bias + head_offset[:, None, None] * same_chain[None]
    positions = jnp.arange(length_all, dtype=jnp.int32)
    query_ids = row_start + jnp.arange(rows_here, dtype=jnp.int32)
    allowed = (residue_mask[None, :] == 1) | (query_ids[:, None] == positions[None, :])
    allowed = allowed[None]
    highest = jnp.max(jnp.where(allowed, scores, -jnp.inf), axis=-1, keepdims=True)
    raised = jnp.where(allowed, jnp.exp(scores - highest), 0.0)
    weights = (raised / jnp.sum(raised, axis=-1, keepdims=True)).astype(jnp.bfloat16)
    gathered = jnp.einsum(
        "hij,jhd->ihd", weights, value_heads, preferred_element_type=jnp.float32
    ).reshape(rows_here, -1)
    mixed = (gate * gathered).astype(jnp.bfloat16)
    head_terms = jnp.dot(mixed, attention_out, preferred_element_type=jnp.float32)
    update = over_copies(head_terms, "col")
    sequence_out = (sequence.astype(jnp.float32) + update).astype(jnp.bfloat16)
    normed_out = layer_norm(sequence_out.astype(jnp.float32)).astype(jnp.bfloat16)
    outer_rows = jnp.dot(normed_out, outer_in, preferred_element_type=jnp.float32).astype(
        jnp.bfloat16
    )
    half_width = outer_rows.shape[1] // 2
    right_all = gather_directly(outer_rows[:, half_width:], ROW, 0)
    right_side = lax.dynamic_slice_in_dim(right_all, col_start, cols_here, 0).astype(jnp.float32)
    left_side = outer_rows[:, :half_width].astype(jnp.float32)
    outer_feat = jnp.concatenate(
        [
            left_side[:, None, :] * right_side[None, :, :],
            left_side[:, None, :] - right_side[None, :, :],
        ],
        axis=-1,
    ).astype(jnp.bfloat16)
    pair_mid = pair_wide + jnp.dot(
        outer_feat.reshape(-1, 2 * half_width), outer_out, preferred_element_type=jnp.float32
    ).reshape(rows_here, cols_here, channels)
    normed_mid = layer_norm(pair_mid).astype(jnp.bfloat16)
    tri = jnp.dot(
        normed_mid.reshape(-1, channels),
        triangle_in.reshape(channels, -1),
        preferred_element_type=jnp.float32,
    ).reshape(rows_here, cols_here, 5, channels)
    live = residue_mask.astype(jnp.float32)
    row_live = lax.dynamic_slice_in_dim(live, row_start, rows_here, 0)
    col_live = lax.dynamic_slice_in_dim(live, col_start, cols_here, 0)
    pair_live = (row_live[:, None] * col_live[None, :])[:, :, None]
    left_op = (jax.nn.sigmoid(tri[:, :, 0]) * tri[:, :, 1] * pair_live).astype(jnp.bfloat16)
    right_op = (jax.nn.sigmoid(tri[:, :, 2]) * tri[:, :, 3] * pair_live).astype(jnp.bfloat16)
    out_gate = jax.nn.sigmoid(tri[:, :, 4])
    column_all = gather_axes(right_op, ROW, (0, 1), 0)
    crossed = lax.psum_scatter(
        jnp.einsum("jkc,ikc->jic", column_all, left_op, preferred_element_type=jnp.float32),
        "col",
        scatter_dimension=0,
        tiled=True,
    )
    product = jnp.transpose(crossed, (1, 0, 2))
    normed_product = layer_norm(product).astype(jnp.bfloat16)
    projected_product = jnp.dot(
        normed_product.reshape(-1, channels), triangle_out, preferred_element_type=jnp.float32
    ).reshape(rows_here, cols_here, channels)
    pair_late = pair_mid + out_gate * projected_product
    normed_late = layer_norm(pair_late).astype(jnp.bfloat16)
    hidden = jax.nn.relu(
        jnp.dot(
            normed_late.reshape(-1, channels), transition_up, preferred_element_type=jnp.float32
        )
    ).astype(jnp.bfloat16)
    lowered = jnp.dot(hidden, transition_down, preferred_element_type=jnp.float32).reshape(
        rows_here, cols_here, channels
    )
    pair_out = (pair_late + lowered).astype(jnp.bfloat16)
    return (sequence_out, pair_out)


def solution(mesh):
    finer = Mesh(mesh.devices.reshape(4, 8, mesh.shape["col"]), ("row_0", "row_1", "col"))
    placed = (
        P(ROW, None),
        P(ROW, "col", None),
        P(),
        P(),
        P(None, None, "col"),
        P("col", None),
        P(),
        P(),
        P(),
        P(),
        P(),
        P(),
        P(),
        P(),
    )
    return jax.shard_map(
        per_device,
        mesh=finer,
        in_specs=placed,
        out_specs=(P(ROW, None), P(ROW, "col", None)),
        check_vma=False,
    )
```

profile of v0, /device:TPU:1, one launch (start us, length us, event | category | flops | bytes accessed | tf_op | source)
XLA Modules:
  0.0 333.4 jit_solution(16700241843302141484)
XLA Ops:
  7.2 1.1 convert_reduce_fusion
  8.3 1.2 fusion.12
  9.5 1.2 convolution_bitcast_fusion.1
  10.7 0.2 copy.129
  10.9 0.8 reshape.298
  11.7 10.1 %all-to-all-start = ((f32[16,1,1024]{2,1,0:T(1,128)}), f32[16,1,1024]{2,1,0:T(1,128)S(1)}, u32[]{:S(2)}, u32[]{:S(2)}) async-start(f32[16,1,1024]{2,1,0:T(1,128)} %reshape.298), calls=%async_computation | async-start | bytes 131072 | tf_op jit(solution)/shard_map/all_to_all | solution.py:86
  21.8 0.7 broadcast_compare_fusion
  22.5 0.9 convert_reduce_fusion.1
  23.4 0.9 fusion.48
  24.4 0.8 dynamic_slice.16
  25.1 0.8 compare_convert_fusion
  25.9 1.1 fusion.92
  27.0 0.1 convert_element_type.95
  27.1 0.1 pad_maximum_fusion
  27.2 70.4 %all_gather.9 = bf16[512,128]{1,0:T(8,128)(2,1)S(1)} all-gather(bf16[16,128]{1,0:T(8,128)(2,1)S(1)} %pad_maximum_fusion), channel_id=1, replica_groups=mesh['row_0'=4,'row_1'=8,'col'=16] {'row_0','row_1'}, dimensions={0}, use_global_device_ids=true | all-gather | bytes 135168 | tf_op jit(solution)/shard_map/all_gather | solution.py:15
  97.6 0.1 fusion.90
  97.7 0.1 copy.127
  97.8 0.1 copy.126
  97.9 0.7 dynamic_slice.15
  98.7 0.5 broadcast.256
  99.2 0.8 reduce
  100.1 0.1 reshape.299
  100.2 0.2 copy.130
  100.3 0.1 all_to_all.22
  100.5 0.1 fusion.8
  100.6 0.2 fusion.93
  100.8 0.2 convolution_bitcast_fusion.2
  101.0 0.1 reshape.284
  101.1 0.1 fusion.75
  101.3 1.1 broadcast_in_dim.25
  102.4 20.0 %all-to-all-start.1 = ((f32[16,16,1024]{2,1,0:T(8,128)}), f32[16,16,1024]{2,1,0:T(8,128)S(1)}, u32[]{:S(2)}, u32[]{:S(2)}) async-start(f32[16,16,1024]{2,1,0:T(8,128)} %broadcast_in_dim.25), calls=%async_computation.1 | async-start | bytes 2097152 | tf_op jit(solution)/shard_map/all_to_all | solution.py:21
  122.4 0.1 dynamic_slice.18
  122.5 0.2 copy.132
  122.7 15.3 %all-to-all-done.1 = f32[16,16,1024]{2,1,0:T(8,128)S(1)} async-done(((f32[16,16,1024]{2,1,0:T(8,128)}), f32[16,16,1024]{2,1,0:T(8,128)S(1)}, u32[]{:S(2)}, u32[]{:S(2)}) %all-to-all-start.1) | async-done | bytes 1048608 | tf_op jit(solution)/shard_map/all_to_all | solution.py:21
  138.1 0.1 convert_reduce_fusion.2
  138.2 0.2 fusion.50
  138.4 0.2 convolution_convert_fusion
  138.6 0.1 slice_convert_fusion
  138.7 0.8 reshape.300
  139.5 3.9 %all-to-all-start.2 = ((bf16[32,2,512]{2,1,0:T(2,128)(2,1)}), bf16[32,2,512]{2,1,0:T(2,128)(2,1)S(1)}, u32[]{:S(2)}, u32[]{:S(2)}) async-start(bf16[32,2,512]{2,1,0:T(2,128)(2,1)} %reshape.300), calls=%async_computation.2 | async-start | bytes 131072 | tf_op jit(solution)/shard_map/all_to_all | solution.py:21
  143.5 11.2 %all-to-all-done.2 = bf16[32,2,512]{2,1,0:T(2,128)(2,1)S(1)} async-done(((bf16[32,2,512]{2,1,0:T(2,128)(2,1)}), bf16[32,2,512]{2,1,0:T(2,128)(2,1)S(1)}, u32[]{:S(2)}, u32[]{:S(2)}) %all-to-all-start.2) | async-done | bytes 65568 | tf_op jit(solution)/shard_map/all_to_all | solution.py:21
  154.7 0.1 reshape.301
  154.9 0.3 fusion.94
  155.3 0.3 multiply_reduce_fusion.2
  155.5 0.4 fusion.30
  155.9 0.1 fusion.16
  156.1 13.5 %all_gather.10 = bf16[4,16,32,128]{3,2,1,0:T(8,128)(2,1)} all-gather(bf16[1,16,32,128]{3,2,1,0:T(8,128)(2,1)S(1)} %fusion.16), channel_id=1, replica_groups=mesh['row_0'=4,'row_1'=8,'col'=16] {'row_0'}, dimensions={0}, use_global_device_ids=true | all-gather | bytes 655360 | tf_op jit(solution)/shard_map/all_gather | solution.py:42
  169.6 0.1 fusion.22
  169.8 0.4 copy.139
  170.2 52.9 %all-gather.2.cloned.1.call-done = bf16[32,16,32,128]{3,2,1,0:T(8,128)(2,1)} async-done(((bf16[4,16,32,128]{3,2,1,0:T(8,128)(2,1)}), bf16[32,16,32,128]{3,2,1,0:T(8,128)(2,1)}) %all-gather.2.cloned.1.call-update) | async-done | bytes 4194320 | tf_op jit(solution)/shard_map/all_gather | solution.py:42
  223.1 5.3 %copy.138 = bf16[4,8,16,32,128]{4,3,2,1,0:T(8,128)(2,1)} copy(bf16[4,8,16,32,128]{4,3,2,0,1:T(8,128)(2,1)} %bitcast.99) | data formatting | bytes 8388608 | tf_op jit(solution)/shard_map/transpose | solution.py:46
  228.4 8.6 %copy.140 = bf16[512,32,128]{0,1,2:T(8,128)(2,1)} copy(bf16[512,32,128]{2,1,0:T(8,128)(2,1)} %bitcast.98) | data formatting | bytes 8388608 | tf_op jit(solution)/shard_map/reshape;reshape | solution.py:32
  237.1 4.8 %convolution_bitcast_fusion = f32[512,16,128]{0,1,2:T(8,128)} fusion(bf16[16,32,128]{1,0,2:T(8,128)(2,1)S(1)} %copy.139, bf16[512,32,128]{0,1,2:T(8,128)(2,1)} %copy.140), kind=kOutput, calls=%fused_computation.1 | convolution fusion | flops 67108864 | bytes 8519680 | tf_op jit(solution)/shard_map/jkc,ikc->jic/dot_general | solution.py:157
  241.9 5.8 %copy.141 = f32[512,16,128]{2,1,0:T(8,128)} copy(f32[512,16,128]{0,1,2:T(8,128)} %convolution_bitcast_fusion) | data formatting | bytes 8388608 | tf_op jit(solution)/shard_map/jkc,ikc->jic/transpose | solution.py:157
  247.7 73.1 %reduce-scatter.2.cloned.1.call-done = f32[32,16,128]{2,1,0:T(8,128)} async-done(((f32[512,16,128]{2,1,0:T(8,128)}), f32[32,16,128]{2,1,0:T(8,128)}) %reduce-scatter.2.cloned.1.call-update) | async-done | bytes 262160 | tf_op jit(solution)/shard_map/reduce_scatter | solution.py:156
  320.8 1.1 bitcast_reduce_fusion
  322.0 0.1 copy.143
  322.1 1.2 multiply_reduce_fusion.1
  323.4 1.2 multiply_convert_fusion.1
  324.6 0.3 fusion.95
  324.9 0.3 multiply_reduce_fusion
  325.2 0.2 multiply_convert_fusion
  325.4 0.4 fusion.2
  325.8 0.7 add_convert_fusion
  (55 shorter events, 0.9 us)
Async XLA Ops:
  7.2 18.7 %copy-start = (bf16[1024,4,64]{0,2,1:T(8,128)(2,1)S(1)}, bf16[1024,4,64]{0,2,1:T(8,128)(2,1)}, u32[]{:S(2)}) copy-start(bf16[1024,4,64]{0,2,1:T(8,128)(2,1)} %param.18) | copy-start | bytes 1572868
  7.2 93.9 %copy-start.4 = (bf16[64,1024]{1,0:T(8,128)(2,1)S(1)}, bf16[64,1024]{1,0:T(8,128)(2,1)}, u32[]{:S(2)}) copy-start(bf16[64,1024]{1,0:T(8,128)(2,1)} %param.19) | copy-start | bytes 393220
  10.7 111.6 %copy-start.7 = (s32[512]{0:T(512)S(1)}, s32[512]{0:T(512)}, u32[]{:S(2)}) copy-start(s32[512]{0:T(512)} %param.16) | copy-start | bytes 6148
  10.7 111.8 %copy-start.3 = (bf16[128,5,128]{2,0,1:T(8,128)(2,1)S(1)}, bf16[128,5,128]{2,0,1:T(8,128)(2,1)}, u32[]{:S(2)}) copy-start(bf16[128,5,128]{2,0,1:T(8,128)(2,1)} %param.24) | copy-start | bytes 491524
  11.7 87.0 %all-to-all-start = ((f32[16,1,1024]{2,1,0:T(1,128)}), f32[16,1,1024]{2,1,0:T(1,128)S(1)}, u32[]{:S(2)}, u32[]{:S(2)}) async-start(f32[16,1,1024]{2,1,0:T(1,128)} %reshape.298), calls=%async_computation | async-start | bytes 131072 | tf_op jit(solution)/shard_map/all_to_all | solution.py:86
  27.0 111.1 %copy-start.2 = (bf16[16,1024]{1,0:T(8,128)(2,1)S(1)}, bf16[16,1024]{1,0:T(8,128)(2,1)}, u32[]{:S(2)}) copy-start(bf16[16,1024]{1,0:T(8,128)(2,1)} %param.14) | copy-start | bytes 98308
  27.0 111.5 %copy-start.8 = (bf16[1024,128]{1,0:T(8,128)(2,1)S(1)}, bf16[1024,128]{1,0:T(8,128)(2,1)}, u32[]{:S(2)}) copy-start(bf16[1024,128]{1,0:T(8,128)(2,1)} %param.22) | copy-start | bytes 786436
  100.0 54.8 %copy-start.1 = (bf16[16,32,128]{2,1,0:T(8,128)(2,1)S(1)}, bf16[16,32,128]{2,1,0:T(8,128)(2,1)}, u32[]{:S(2)}) copy-start(bf16[16,32,128]{2,1,0:T(8,128)(2,1)} %param.15) | copy-start | bytes 393220
  100.0 54.8 %copy-start.6 = (bf16[128,128]{1,0:T(8,128)(2,1)S(1)}, bf16[128,128]{1,0:T(8,128)(2,1)}, u32[]{:S(2)}) copy-start(bf16[128,128]{1,0:T(8,128)(2,1)} %param.23) | copy-start | bytes 98308
  102.4 35.6 %all-to-all-start.1 = ((f32[16,16,1024]{2,1,0:T(8,128)}), f32[16,16,1024]{2,1,0:T(8,128)S(1)}, u32[]{:S(2)}, u32[]{:S(2)}) async-start(f32[16,16,1024]{2,1,0:T(8,128)} %broadcast_in_dim.25), calls=%async_computation.1 | async-start | bytes 2097152 | tf_op jit(solution)/shard_map/all_to_all | solution.py:21
  138.2 90.2 %copy-start.5 = (bf16[16,1024]{1,0:T(8,128)(2,1)}, bf16[16,1024]{1,0:T(8,128)(2,1)S(1)}, u32[]{:S(2)}) copy-start(bf16[16,1024]{1,0:T(8,128)(2,1)S(1)} %get-tuple-element.3) | copy-start | bytes 98308
  139.5 15.1 %all-to-all-start.2 = ((bf16[32,2,512]{2,1,0:T(2,128)(2,1)}), bf16[32,2,512]{2,1,0:T(2,128)(2,1)S(1)}, u32[]{:S(2)}, u32[]{:S(2)}) async-start(bf16[32,2,512]{2,1,0:T(2,128)(2,1)} %reshape.300), calls=%async_computation.2 | async-start | bytes 131072 | tf_op jit(solution)/shard_map/all_to_all | solution.py:21
  143.4 79.7 %all-gather.2.cloned.1.call-start = ((), (), s32[]{:S(2)}) async-start(), calls=%async_computation.4 | async-start | bytes 4718592 | tf_op jit(solution)/shard_map/all_gather | solution.py:42
  169.6 151.3 %reduce-scatter.2.cloned.1.call-start = ((), (), s32[]{:S(2)}) async-start(), calls=%async_computation.5 | async-start | bytes 4456448 | tf_op jit(solution)/shard_map/reduce_scatter | solution.py:156
  247.7 76.9 %copy-start.11 = (bf16[128,128]{1,0:T(8,128)(2,1)S(1)}, bf16[128,128]{1,0:T(8,128)(2,1)}, u32[]{:S(2)}) copy-start(bf16[128,128]{1,0:T(8,128)(2,1)} %param.25) | copy-start | bytes 98308
  247.7 77.7 %copy-start.9 = (bf16[512,128]{1,0:T(8,128)(2,1)S(1)}, bf16[512,128]{1,0:T(8,128)(2,1)}, u32[]{:S(2)}) copy-start(bf16[512,128]{1,0:T(8,128)(2,1)} %param.27) | copy-start | bytes 393220
  247.7 77.7 %copy-start.10 = (bf16[128,512]{1,0:T(8,128)(2,1)S(1)}, bf16[128,512]{1,0:T(8,128)(2,1)}, u32[]{:S(2)}) copy-start(bf16[128,512]{1,0:T(8,128)(2,1)} %param.26) | copy-start | bytes 393220
Sparse Core Ops, SparseCore 0:
  169.7 53.3 all-gather.1
  247.9 72.9 reduce-scatter.1
where the time goes:
time: 336 us; the launch traced here: 333 us
  waiting for transfers between devices  152 us (45%)
  blocking collectives  83.9 us (25%)
  starting transfers between devices  34 us (10%)
  local copies, waits for them, and re-layouts  26.8 us (8%)
  between operations  14.4 us (4%)
  other arithmetic  12.4 us (4%)
  matrix products  9.29 us (3%)
    reduce_scatter x1, waiting for transfers between devices, per_device(): lax.psum_scatter(jnp.einsum('jkc,ikc->jic', column_all, left_op, preferre...  73.1 us
    all_gather x1, blocking collectives, in_one_piece(): filled = lax.all_gather(both, axis, axis=dim, tiled=True)  70.4 us
    all_gather x1, waiting for transfers between devices, gather_in_order(): parts = lax.all_gather(parts, axes[k], axis=0, tiled=True)  52.9 us
    all_to_all x2, waiting for transfers between devices, from_everyone(): return lax.all_to_all(copies, axis, split_axis=0, concat_axis=0, tiled=True)  26.5 us
    all_to_all x2, starting transfers between devices, from_everyone(): return lax.all_to_all(copies, axis, split_axis=0, concat_axis=0, tiled=True)  23.8 us
    all_gather x1, blocking collectives, gather_in_order(): parts = lax.all_gather(parts, axes[k], axis=0, tiled=True)  13.5 us
    all_to_all x1, starting transfers between devices, per_device(): lax.all_to_all(bias_tile, 'col', split_axis=0, concat_axis=2, tiled=True)  10.1 us
    another operation x1, local copies, waits for them, and re-layouts, laid_out(): parts.reshape(*lengths[:dim], lengths[dim] * lengths[dim + 1], *lengths[d...  8.64 us
  transfers between devices with their start and end apart: 5, of which 4 were waited for; matrix products, arithmetic and copies ran while one was open for 2% of the time, Pallas kernels for 0%

commit v1 on v0

v1 whole, which is shorter than its diff:
```python
import math

import jax
import jax.numpy as jnp
from jax import lax
from jax.sharding import Mesh
from jax.sharding import PartitionSpec as P

ROW = ("row_0", "row_1")
BF16 = jnp.bfloat16
F32 = jnp.float32


def exchange(blocks, axis):
    return lax.all_to_all(blocks, axis, split_axis=0, concat_axis=0, tiled=True)


def from_everyone(value, axis):
    copies = jnp.broadcast_to(value, (lax.axis_size(axis), *value.shape))
    return exchange(copies, axis)


def layer_norm(values, axis=-1):
    center = values - jnp.mean(values, axis=axis, keepdims=True)
    spread = jnp.mean(center * center, axis=axis, keepdims=True)
    return center * lax.rsqrt(spread + 1e-05)


def per_device(
    sequence,
    pair_state,
    residue_mask,
    chain_index,
    attention_in,
    attention_out,
    bias_weight,
    chain_bias,
    outer_in,
    outer_out,
    triangle_in,
    triangle_out,
    transition_up,
    transition_down,
):
    rows_here, cols_here, channels = pair_state.shape
    length_all = residue_mask.shape[0]
    pairs_here = rows_here * cols_here
    row_index = lax.axis_index(ROW)
    col_index = lax.axis_index("col")
    outer_rows_count = lax.axis_size("row_0")
    inner_rows_count = lax.axis_size("row_1")
    row_count = outer_rows_count * inner_rows_count
    col_count = lax.axis_size("col")
    row_start = row_index * rows_here
    col_start = col_index * cols_here

    normed_seq = layer_norm(sequence.astype(F32)).astype(BF16)
    projected = jnp.einsum("id,dpe->ipe", normed_seq, attention_in, preferred_element_type=F32)
    query = projected[:, 0].astype(BF16)
    key_values = projected[:, 1:3].astype(BF16).reshape(rows_here, -1)
    gate = jax.nn.sigmoid(projected[:, 3])
    key_values, pair_state = lax.optimization_barrier((key_values, pair_state))
    key_values_all = from_everyone(key_values, ROW).reshape(length_all, -1)

    pair_wide = pair_state.astype(F32)
    normed_pair = layer_norm(pair_wide).astype(BF16)
    bias_tile = jnp.einsum("ijc,ch->hij", normed_pair, bias_weight, preferred_element_type=F32)
    pair_bias = lax.all_to_all(bias_tile, "col", split_axis=0, concat_axis=2, tiled=True)
    heads_here = pair_bias.shape[0]

    width = query.shape[1]
    head_width = width // heads_here
    query_heads = query.reshape(rows_here, heads_here, head_width)
    key_heads = key_values_all[:, :width].reshape(length_all, heads_here, head_width)
    value_heads = key_values_all[:, width:].reshape(length_all, heads_here, head_width)
    scale = 1.0 / math.sqrt(head_width)
    scores = (
        jnp.einsum("ihd,jhd->hij", query_heads, key_heads, preferred_element_type=F32) * scale
    )
    chain_rows = lax.dynamic_slice_in_dim(chain_index, row_start, rows_here, 0)
    same_chain = (chain_rows[:, None] == chain_index[None, :]).astype(F32)
    head_offset = lax.dynamic_slice_in_dim(chain_bias, col_index * heads_here, heads_here, 0)
    scores = scores + pair_bias + head_offset[:, None, None] * same_chain[None]
    positions = jnp.arange(length_all, dtype=jnp.int32)
    query_ids = row_start + jnp.arange(rows_here, dtype=jnp.int32)
    allowed = (residue_mask[None, :] == 1) | (query_ids[:, None] == positions[None, :])
    allowed = allowed[None]
    highest = jnp.max(jnp.where(allowed, scores, -jnp.inf), axis=-1, keepdims=True)
    raised = jnp.where(allowed, jnp.exp(scores - highest), 0.0)
    weights = (raised / jnp.sum(raised, axis=-1, keepdims=True)).astype(BF16)
    gathered = jnp.einsum(
        "hij,jhd->ihd", weights, value_heads, preferred_element_type=F32
    ).reshape(rows_here, -1)
    mixed = (gate * gathered).astype(BF16)
    head_terms = jnp.dot(mixed, attention_out, preferred_element_type=F32).astype(BF16)
    update = jnp.sum(from_everyone(head_terms, "col").astype(F32), axis=0)
    sequence_out = (sequence.astype(F32) + update).astype(BF16)

    normed_out = layer_norm(sequence_out.astype(F32)).astype(BF16)
    outer_rows = jnp.dot(normed_out, outer_in, preferred_element_type=F32).astype(BF16)
    half_width = outer_rows.shape[1] // 2
    outer_all = from_everyone(outer_rows, ROW).reshape(length_all, -1)
    right_side = lax.dynamic_slice_in_dim(outer_all, col_start, cols_here, 0)
    right_side = right_side[:, half_width:].astype(F32)
    left_side = outer_rows[:, :half_width].astype(F32)
    outer_feat = jnp.concatenate(
        [
            left_side[:, None, :] * right_side[None, :, :],
            left_side[:, None, :] - right_side[None, :, :],
        ],
        axis=-1,
    ).astype(BF16)
    pair_mid = pair_wide.reshape(pairs_here, channels) + jnp.dot(
        outer_feat.reshape(pairs_here, 2 * half_width), outer_out, preferred_element_type=F32
    )
    normed_mid = layer_norm(pair_mid).astype(BF16)

    operand_in = triangle_in[:, :4].reshape(channels, 4 * channels)
    tri = lax.dot_general(
        operand_in, normed_mid, (((0,), (1,)), ((), ())), preferred_element_type=F32
    ).reshape(4, channels, pairs_here)
    live = residue_mask.astype(F32)
    row_live = lax.dynamic_slice_in_dim(live, row_start, rows_here, 0)
    col_live = lax.dynamic_slice_in_dim(live, col_start, cols_here, 0)
    pair_live = (row_live[:, None] * col_live[None, :]).reshape(1, pairs_here)
    left_op = (jax.nn.sigmoid(tri[0]) * tri[1] * pair_live).astype(BF16)
    right_op = (jax.nn.sigmoid(tri[2]) * tri[3] * pair_live).astype(BF16)
    out_gate = jax.nn.sigmoid(
        jnp.dot(normed_mid, triangle_in[:, 4], preferred_element_type=F32)
    )

    group = channels // col_count
    tiles = jnp.concatenate(
        [
            left_op.reshape(col_count, group, pairs_here),
            right_op.reshape(col_count, group, pairs_here),
        ],
        axis=1,
    )
    tiles = exchange(tiles, "col").reshape(col_count, 2, group, rows_here, cols_here)
    panels = jnp.transpose(tiles, (2, 1, 3, 0, 4)).reshape(group, 2 * rows_here, length_all)
    panels = exchange(panels, "row_1")
    lefts = panels[:, :rows_here].reshape(-1, length_all)
    rights = panels[:, rows_here:].reshape(-1, length_all)
    here = lax.axis_index("row_0")
    rights_all = jnp.zeros((outer_rows_count, *rights.shape), rights.dtype)
    for step in range(outer_rows_count):
        turn = [(p, (p + step) % outer_rows_count) for p in range(outer_rows_count)]
        arrived = lax.ppermute(rights, "row_0", turn) if step else rights
        origin = lax.rem(here - step + outer_rows_count, outer_rows_count)
        rights_all = lax.dynamic_update_slice_in_dim(rights_all, arrived[None], origin, 0)
    product = lax.dot_general(
        lefts,
        rights_all.reshape(-1, length_all),
        (((1,), (1,)), ((), ())),
        preferred_element_type=F32,
    ).astype(BF16)
    product = exchange(product.reshape(inner_rows_count, rows_here, length_all), "row_1")
    product = jnp.transpose(
        product.reshape(group, rows_here, col_count, cols_here), (2, 0, 1, 3)
    ).reshape(col_count, group, pairs_here)
    product = exchange(product, "col").reshape(channels, pairs_here)

    normed_product = layer_norm(product.astype(F32), axis=0).astype(BF16)
    projected_product = lax.dot_general(
        normed_product, triangle_out, (((0,), (0,)), ((), ())), preferred_element_type=F32
    )
    pair_late = pair_mid + out_gate * projected_product
    normed_late = layer_norm(pair_late).astype(BF16)
    hidden = jax.nn.relu(
        jnp.dot(normed_late, transition_up, preferred_element_type=F32)
    ).astype(BF16)
    lowered = jnp.dot(hidden, transition_down, preferred_element_type=F32)
    pair_out = (pair_late + lowered).astype(BF16).reshape(rows_here, cols_here, channels)
    return (sequence_out, pair_out)


def solution(mesh):
    finer = Mesh(mesh.devices.reshape(4, 8, mesh.shape["col"]), ("row_0", "row_1", "col"))
    placed = (
        P(ROW, None),
        P(ROW, "col", None),
        P(),
        P(),
        P(None, None, "col"),
        P("col", None),
        P(),
        P(),
        P(),
        P(),
        P(),
        P(),
        P(),
        P(),
    )
    return jax.shard_map(
        per_device,
        mesh=finer,
        in_specs=placed,
        out_specs=(P(ROW, None), P(ROW, "col", None)),
        check_vma=False,
    )
```

time: 336 us -> 162 us (0.48)
  waiting for transfers between devices: 152 us -> 53.1 us
  blocking collectives: 83.9 us -> 35.5 us
  starting transfers between devices: 34 us -> 47.5 us
  between operations: 14.4 us -> 1.07 us
  local copies, waits for them, and re-layouts: 26.8 us -> 15.3 us
  other arithmetic: 12.4 us -> 4.07 us
  matrix products: 9.29 us -> 4.29 us
    all_gather x2 -> x0, blocking collectives: 83.9 us -> none  [the longest x1 70.4 us: in_one_piece(): filled = lax.all_gather(both, axis, axis=dim, tiled=True)]
    reduce_scatter x1 -> x0, waiting for transfers between devices: 73.1 us -> none  [per_device(): lax.psum_scatter(jnp.einsum('jkc,ikc->jic', column_all, left_op, preferre...]
    all_gather x1 -> x0, waiting for transfers between devices: 52.9 us -> none  [gather_in_order(): parts = lax.all_gather(parts, axes[k], axis=0, tiled=True)]
    all_to_all x0 -> x3, blocking collectives: none -> 35.5 us  [exchange(): return lax.all_to_all(blocks, axis, split_axis=0, concat_axis=0, tiled=True)]
    ppermute x0 -> x3, waiting for transfers between devices: none -> 13.2 us  [per_device(): arrived = lax.ppermute(rights, 'row_0', turn) if step else rights]
    transpose x3, local copies, waits for them, and re-layouts: 11.2 us -> 0.83 us  [the longest x1 0.68 us: per_device(): jnp.transpose(tiles, (2, 1, 3, 0, 4))]
    ppermute x0 -> x3, starting transfers between devices: none -> 10.1 us  [per_device(): arrived = lax.ppermute(rights, 'row_0', turn) if step else rights]
    another operation x1 -> x0, local copies, waits for them, and re-layouts: 8.64 us -> none  [laid_out(): parts.reshape(*lengths[:dim], lengths[dim] * lengths[dim + 1], *lengths[d...]
  transfers between devices with their start and end apart: 5 -> 8, of which waited for: 4 -> 8; matrix products, arithmetic and copies ran while one was open for 2% -> 2% of each run, Pallas kernels for 0% -> 0%
where the time goes in v1:
time: 162 us; the launch traced here: 161 us
  waiting for transfers between devices  53.1 us (33%)
  starting transfers between devices  47.5 us (29%)
  blocking collectives  35.5 us (22%)
  local copies, waits for them, and re-layouts  15.3 us (9%)
  matrix products  4.29 us (3%)
  other arithmetic  4.07 us (3%)
    all_to_all x3, blocking collectives, exchange(): return lax.all_to_all(blocks, axis, split_axis=0, concat_axis=0, tiled=True)  35.5 us
    all_to_all x4, waiting for transfers between devices, exchange(): return lax.all_to_all(blocks, axis, split_axis=0, concat_axis=0, tiled=True)  34.1 us
    all_to_all x4, starting transfers between devices, exchange(): return lax.all_to_all(blocks, axis, split_axis=0, concat_axis=0, tiled=True)  27.2 us
    ppermute x3, waiting for transfers between devices, per_device(): arrived = lax.ppermute(rights, 'row_0', turn) if step else rights  13.2 us
    all_to_all x1, starting transfers between devices, per_device(): lax.all_to_all(bias_tile, 'col', split_axis=0, concat_axis=2, tiled=True)  10.3 us
    ppermute x3, starting transfers between devices, per_device(): arrived = lax.ppermute(rights, 'row_0', turn) if step else rights  10.1 us
    unnamed x33, local copies, waits for them, and re-layouts  6.33 us
    all_to_all x1, waiting for transfers between devices, per_device(): lax.all_to_all(bias_tile, 'col', split_axis=0, concat_axis=2, tiled=True)  5.84 us
  transfers between devices with their start and end apart: 8, of which 8 were waited for; matrix products, arithmetic and copies ran while one was open for 2% of the time, Pallas kernels for 0%

profile of v1, /device:TPU:1, one launch (start us, length us, event | category | flops | bytes accessed | tf_op | source)
XLA Modules:
  0.0 160.9 jit_solution(3261255225225528451)
XLA Ops:
  0.7 0.9 convert_reduce_fusion.3
  1.6 0.2 fusion.49
  1.8 0.3 fusion.92
  2.3 0.5 copy-done.1
  2.7 0.1 convert_reduce_fusion.2
  2.9 0.3 multiply_reduce_fusion.2
  3.2 0.7 copy-done.8
  3.8 0.3 convolution_bitcast_fusion.1
  4.2 0.2 copy.51
  4.3 0.8 reshape.304
  5.1 10.3 %all-to-all-start.1 = ((f32[16,1,1024]{2,1,0:T(1,128)}), f32[16,1,1024]{2,1,0:T(1,128)S(1)}, u32[]{:S(2)}, u32[]{:S(2)}) async-start(f32[16,1,1024]{2,1,0:T(1,128)} %reshape.304), calls=%async_computation.1 | async-start | bytes 131072 | tf_op jit(solution)/shard_map/all_to_all | solution.py:68
  15.4 5.8 %all-to-all-done.1 = f32[16,1,1024]{2,1,0:T(1,128)S(1)} async-done(((f32[16,1,1024]{2,1,0:T(1,128)}), f32[16,1,1024]{2,1,0:T(1,128)S(1)}, u32[]{:S(2)}, u32[]{:S(2)}) %all-to-all-start.1) | async-done | bytes 65568 | tf_op jit(solution)/shard_map/all_to_all | solution.py:68
  21.3 0.7 broadcast_in_dim.32
  21.9 12.2 %all-to-all-start = ((bf16[32,16,128]{2,1,0:T(8,128)(2,1)}), bf16[32,16,128]{2,1,0:T(8,128)(2,1)S(1)}, u32[]{:S(2)}, u32[]{:S(2)}) async-start(bf16[32,16,128]{2,1,0:T(8,128)(2,1)} %broadcast_in_dim.32), calls=%async_computation | async-start | bytes 262144 | tf_op jit(solution)/shard_map/all_to_all | solution.py:15
  34.3 0.6 copy-done.10
  35.0 0.7 copy-done.14
  35.8 0.5 broadcast.250
  36.3 0.8 reduce.2
  37.2 0.2 copy.52
  37.4 0.1 all_to_all.38
  37.5 8.2 %all-to-all-done = bf16[32,16,128]{2,1,0:T(8,128)(2,1)S(1)} async-done(((bf16[32,16,128]{2,1,0:T(8,128)(2,1)}), bf16[32,16,128]{2,1,0:T(8,128)(2,1)S(1)}, u32[]{:S(2)}, u32[]{:S(2)}) %all-to-all-start) | async-done | bytes 131104 | tf_op jit(solution)/shard_map/all_to_all | solution.py:15
  46.2 0.2 fusion.93
  46.4 0.2 convolution_bitcast_fusion.2
  46.7 0.6 copy-done.4
  47.3 0.1 convolution_convert_fusion.1
  47.4 0.9 broadcast_in_dim.36
  48.3 5.4 %all-to-all-start.2 = ((bf16[16,16,1024]{2,1,0:T(8,128)(2,1)}), bf16[16,16,1024]{2,1,0:T(8,128)(2,1)S(1)}, u32[]{:S(2)}, u32[]{:S(2)}) async-start(bf16[16,16,1024]{2,1,0:T(8,128)(2,1)} %broadcast_in_dim.36), calls=%async_computation.2 | async-start | bytes 1048576 | tf_op jit(solution)/shard_map/all_to_all | solution.py:15
  53.9 9.6 %all-to-all-done.2 = bf16[16,16,1024]{2,1,0:T(8,128)(2,1)S(1)} async-done(((bf16[16,16,1024]{2,1,0:T(8,128)(2,1)}), bf16[16,16,1024]{2,1,0:T(8,128)(2,1)S(1)}, u32[]{:S(2)}, u32[]{:S(2)}) %all-to-all-start.2) | async-done | bytes 524320 | tf_op jit(solution)/shard_map/all_to_all | solution.py:15
  63.7 0.2 fusion.51
  63.9 0.2 convolution_convert_fusion.2
  64.1 0.2 copy-done.5
  64.3 0.7 broadcast_in_dim.37
  65.0 3.9 %all-to-all-start.3 = ((bf16[32,16,128]{2,1,0:T(8,128)(2,1)}), bf16[32,16,128]{2,1,0:T(8,128)(2,1)S(1)}, u32[]{:S(2)}, u32[]{:S(2)}) async-start(bf16[32,16,128]{2,1,0:T(8,128)(2,1)} %broadcast_in_dim.37), calls=%async_computation.3 | async-start | bytes 262144 | tf_op jit(solution)/shard_map/all_to_all | solution.py:15
  68.9 0.9 slice-done
  70.0 10.5 %all-to-all-done.3 = bf16[32,16,128]{2,1,0:T(8,128)(2,1)S(1)} async-done(((bf16[32,16,128]{2,1,0:T(8,128)(2,1)}), bf16[32,16,128]{2,1,0:T(8,128)(2,1)S(1)}, u32[]{:S(2)}, u32[]{:S(2)}) %all-to-all-start.3) | async-done | bytes 131104 | tf_op jit(solution)/shard_map/all_to_all | solution.py:15
  80.6 0.7 copy-done.6
  81.3 0.4 fusion.94
  81.7 0.2 multiply_reduce_fusion.1
  82.0 0.5 convolution_bitcast_fusion
  82.4 0.1 fusion.28
  82.6 12.4 %all_to_all.53 = bf16[16,16,512]{2,1,0:T(8,128)(2,1)S(1)} all-to-all(bf16[16,16,512]{2,1,0:T(8,128)(2,1)S(1)} %pad_maximum_fusion), channel_id=1, replica_groups=mesh['row_0'=4,'row_1'=8,'col'=16] {'col'}, dimensions={0} | all-to-all | bytes 524288 | tf_op jit(solution)/shard_map/all_to_all | solution.py:15
  95.0 0.6 reshape.290
  95.6 0.7 copy.55
  96.3 1.0 reshape.291
  97.3 13.0 %all_to_all.54 = bf16[8,32,512]{2,1,0:T(8,128)(2,1)S(1)} all-to-all(bf16[8,32,512]{2,1,0:T(8,128)(2,1)S(1)} %reshape.291), channel_id=1, replica_groups=mesh['row_0'=4,'row_1'=8,'col'=16] {'row_1'}, dimensions={0} | all-to-all | bytes 524288 | tf_op jit(solution)/shard_map/all_to_all | solution.py:15
  110.3 2.5 %collective-permute-start = (bf16[128,512]{1,0:T(8,128)(2,1)S(1)}, bf16[128,512]{1,0:T(8,128)(2,1)S(1)}, u32[]{:S(2)}, u32[]{:S(2)}) collective-permute-start(bf16[128,512]{1,0:T(8,128)(2,1)S(1)} %bitcast.101), channel_id=1, source_target_pairs={{0,128},{128,256},{256,384},{384,0},{1,129},{129,257},{257,385},{3... | collective-permute-start | bytes 393224 | tf_op jit(solution)/shard_map/ppermute | solution.py:149
  112.9 3.6 %collective-permute-start.1 = (bf16[128,512]{1,0:T(8,128)(2,1)S(1)}, bf16[128,512]{1,0:T(8,128)(2,1)S(1)}, u32[]{:S(2)}, u32[]{:S(2)}) collective-permute-start(bf16[128,512]{1,0:T(8,128)(2,1)S(1)} %bitcast.102), channel_id=1, source_target_pairs={{0,256},{128,384},{256,0},{384,128},{1,257},{129,385},{257,1},{385... | collective-permute-start | bytes 393224 | tf_op jit(solution)/shard_map/ppermute | solution.py:149
  116.5 3.9 %collective-permute-start.2 = (bf16[128,512]{1,0:T(8,128)(2,1)S(1)}, bf16[128,512]{1,0:T(8,128)(2,1)S(1)}, u32[]{:S(2)}, u32[]{:S(2)}) collective-permute-start(bf16[128,512]{1,0:T(8,128)(2,1)S(1)} %bitcast.103), channel_id=1, source_target_pairs={{0,384},{128,0},{256,128},{384,256},{1,385},{129,1},{257,129},{385... | collective-permute-start | bytes 393224 | tf_op jit(solution)/shard_map/ppermute | solution.py:149
  120.5 1.3 collective-permute-done
  121.8 2.1 %collective-permute-done.1 = bf16[128,512]{1,0:T(8,128)(2,1)S(1)} collective-permute-done((bf16[128,512]{1,0:T(8,128)(2,1)S(1)}, bf16[128,512]{1,0:T(8,128)(2,1)S(1)}, u32[]{:S(2)}, u32[]{:S(2)}) %collective-permute-start.1) | collective-permute-done | bytes 131104 | tf_op jit(solution)/shard_map/ppermute | solution.py:149
  123.9 9.8 %collective-permute-done.2 = bf16[128,512]{1,0:T(8,128)(2,1)S(1)} collective-permute-done((bf16[128,512]{1,0:T(8,128)(2,1)S(1)}, bf16[128,512]{1,0:T(8,128)(2,1)S(1)}, u32[]{:S(2)}, u32[]{:S(2)}) %collective-permute-start.2) | collective-permute-done | bytes 131104 | tf_op jit(solution)/shard_map/ppermute | solution.py:149
  133.7 0.3 convolution_convert_fusion
  134.0 10.1 %all_to_all.55 = bf16[8,16,512]{2,1,0:T(8,128)(2,1)S(1)} all-to-all(bf16[8,16,512]{2,1,0:T(8,128)(2,1)S(1)} %bitcast.107), channel_id=1, replica_groups=mesh['row_0'=4,'row_1'=8,'col'=16] {'row_1'}, dimensions={0} | all-to-all | bytes 262144 | tf_op jit(solution)/shard_map/all_to_all | solution.py:15
  144.1 0.3 reshape.296
  144.4 0.1 copy.56
  144.6 1.1 reshape.297
  145.7 5.7 %all-to-all-start.7 = ((bf16[16,8,512]{2,1,0:T(8,128)(2,1)}), bf16[16,8,512]{2,1,0:T(8,128)(2,1)S(1)}, u32[]{:S(2)}, u32[]{:S(2)}) async-start(bf16[16,8,512]{2,1,0:T(8,128)(2,1)} %reshape.297), calls=%async_computation.7 | async-start | bytes 262144 | tf_op jit(solution)/shard_map/all_to_all | solution.py:15
  151.4 0.3 fusion.7
  151.7 5.9 %all-to-all-done.7 = bf16[16,8,512]{2,1,0:T(8,128)(2,1)S(1)} async-done(((bf16[16,8,512]{2,1,0:T(8,128)(2,1)}), bf16[16,8,512]{2,1,0:T(8,128)(2,1)S(1)}, u32[]{:S(2)}, u32[]{:S(2)}) %all-to-all-start.7) | async-done | bytes 131104 | tf_op jit(solution)/shard_map/all_to_all | solution.py:15
  157.7 0.7 copy-done.7
  158.4 0.3 fusion.95
  158.8 0.2 multiply_reduce_fusion
  159.0 0.6 copy-done.12
  159.7 1.1 fusion.8
  (72 shorter events, 2.3 us)
Async XLA Ops:
  0.6 1.2 copy-start
  0.6 1.0 copy-start.3
  1.8 0.9 copy-start.1
  3.1 0.7 copy-start.8
  5.1 10.3 %copy-start.9 = (s32[512]{0:T(512)S(1)}, s32[512]{0:T(512)}, u32[]{:S(2)}) copy-start(s32[512]{0:T(512)} %param.16) | copy-start | bytes 6148
  5.1 16.1 %all-to-all-start.1 = ((f32[16,1,1024]{2,1,0:T(1,128)}), f32[16,1,1024]{2,1,0:T(1,128)S(1)}, u32[]{:S(2)}, u32[]{:S(2)}) async-start(f32[16,1,1024]{2,1,0:T(1,128)} %reshape.304), calls=%async_computation.1 | async-start | bytes 131072 | tf_op jit(solution)/shard_map/all_to_all | solution.py:68
  21.9 23.8 %all-to-all-start = ((bf16[32,16,128]{2,1,0:T(8,128)(2,1)}), bf16[32,16,128]{2,1,0:T(8,128)(2,1)S(1)}, u32[]{:S(2)}, u32[]{:S(2)}) async-start(bf16[32,16,128]{2,1,0:T(8,128)(2,1)} %broadcast_in_dim.32), calls=%async_computation | async-start | bytes 262144 | tf_op jit(solution)/shard_map/all_to_all | solution.py:15
  34.2 0.7 copy-start.10
  35.0 0.7 copy-start.14
  46.4 0.9 copy-start.4
  48.3 15.2 %all-to-all-start.2 = ((bf16[16,16,1024]{2,1,0:T(8,128)(2,1)}), bf16[16,16,1024]{2,1,0:T(8,128)(2,1)S(1)}, u32[]{:S(2)}, u32[]{:S(2)}) async-start(bf16[16,16,1024]{2,1,0:T(8,128)(2,1)} %broadcast_in_dim.36), calls=%async_computation.2 | async-start | bytes 1048576 | tf_op jit(solution)/shard_map/all_to_all | solution.py:15
  53.9 10.0 %copy-start.11 = (bf16[1024,128]{1,0:T(8,128)(2,1)S(1)}, bf16[1024,128]{1,0:T(8,128)(2,1)}, u32[]{:S(2)}) copy-start(bf16[1024,128]{1,0:T(8,128)(2,1)} %param.22) | copy-start | bytes 786436
  63.7 0.6 copy-start.5
  65.0 15.5 %all-to-all-start.3 = ((bf16[32,16,128]{2,1,0:T(8,128)(2,1)}), bf16[32,16,128]{2,1,0:T(8,128)(2,1)S(1)}, u32[]{:S(2)}, u32[]{:S(2)}) async-start(bf16[32,16,128]{2,1,0:T(8,128)(2,1)} %broadcast_in_dim.37), calls=%async_computation.3 | async-start | bytes 262144 | tf_op jit(solution)/shard_map/all_to_all | solution.py:15
  68.9 0.9 slice-start
  80.6 0.8 copy-start.6
  110.3 11.5 %collective-permute-start = (bf16[128,512]{1,0:T(8,128)(2,1)S(1)}, bf16[128,512]{1,0:T(8,128)(2,1)S(1)}, u32[]{:S(2)}, u32[]{:S(2)}) collective-permute-start(bf16[128,512]{1,0:T(8,128)(2,1)S(1)} %bitcast.101), channel_id=1, source_target_pairs={{0,128},{128,256},{256,384},{384,0},{1,129},{129,257},{257,385},{3... | collective-permute-start | bytes 393224 | tf_op jit(solution)/shard_map/ppermute | solution.py:149
  112.9 11.0 %collective-permute-start.1 = (bf16[128,512]{1,0:T(8,128)(2,1)S(1)}, bf16[128,512]{1,0:T(8,128)(2,1)S(1)}, u32[]{:S(2)}, u32[]{:S(2)}) collective-permute-start(bf16[128,512]{1,0:T(8,128)(2,1)S(1)} %bitcast.102), channel_id=1, source_target_pairs={{0,256},{128,384},{256,0},{384,128},{1,257},{129,385},{257,1},{385... | collective-permute-start | bytes 393224 | tf_op jit(solution)/shard_map/ppermute | solution.py:149
  116.5 17.2 %collective-permute-start.2 = (bf16[128,512]{1,0:T(8,128)(2,1)S(1)}, bf16[128,512]{1,0:T(8,128)(2,1)S(1)}, u32[]{:S(2)}, u32[]{:S(2)}) collective-permute-start(bf16[128,512]{1,0:T(8,128)(2,1)S(1)} %bitcast.103), channel_id=1, source_target_pairs={{0,384},{128,0},{256,128},{384,256},{1,385},{129,1},{257,129},{385... | collective-permute-start | bytes 393224 | tf_op jit(solution)/shard_map/ppermute | solution.py:149
  145.7 5.7 %copy-start.2 = (bf16[128,5,128]{2,0,1:T(8,128)(2,1)S(1)}, bf16[128,5,128]{2,0,1:T(8,128)(2,1)}, u32[]{:S(2)}) copy-start(bf16[128,5,128]{2,0,1:T(8,128)(2,1)} %param.24) | copy-start | bytes 491524
  145.7 11.9 %all-to-all-start.7 = ((bf16[16,8,512]{2,1,0:T(8,128)(2,1)}), bf16[16,8,512]{2,1,0:T(8,128)(2,1)S(1)}, u32[]{:S(2)}, u32[]{:S(2)}) async-start(bf16[16,8,512]{2,1,0:T(8,128)(2,1)} %reshape.297), calls=%async_computation.7 | async-start | bytes 262144 | tf_op jit(solution)/shard_map/all_to_all | solution.py:15
  157.6 0.8 copy-start.7
  158.8 0.9 copy-start.12
  158.8 1.0 copy-start.13

commit v2 on v1

--- a/solution.py
+++ b/solution.py
@@ -9,6 +9,8 @@
 ROW = ("row_0", "row_1")
 BF16 = jnp.bfloat16
 F32 = jnp.float32
+K_PARTS = 2
+I_PARTS = 2
 
 
 def exchange(blocks, axis):
@@ -47,9 +49,7 @@
     pairs_here = rows_here * cols_here
     row_index = lax.axis_index(ROW)
     col_index = lax.axis_index("col")
-    outer_rows_count = lax.axis_size("row_0")
-    inner_rows_count = lax.axis_size("row_1")
-    row_count = outer_rows_count * inner_rows_count
+    row_count = lax.axis_size(ROW)
     col_count = lax.axis_size("col")
     row_start = row_index * rows_here
     col_start = col_index * cols_here
@@ -137,27 +137,28 @@
         ],
         axis=1,
     )
-    tiles = exchange(tiles, "col").reshape(col_count, 2, group, rows_here, cols_here)
-    panels = jnp.transpose(tiles, (2, 1, 3, 0, 4)).reshape(group, 2 * rows_here, length_all)
-    panels = exchange(panels, "row_1")
-    lefts = panels[:, :rows_here].reshape(-1, length_all)
-    rights = panels[:, rows_here:].reshape(-1, length_all)
-    here = lax.axis_index("row_0")
-    rights_all = jnp.zeros((outer_rows_count, *rights.shape), rights.dtype)
-    for step in range(outer_rows_count):
-        turn = [(p, (p + step) % outer_rows_count) for p in range(outer_rows_count)]
-        arrived = lax.ppermute(rights, "row_0", turn) if step else rights
-        origin = lax.rem(here - step + outer_rows_count, outer_rows_count)
-        rights_all = lax.dynamic_update_slice_in_dim(rights_all, arrived[None], origin, 0)
+    tiles = exchange(tiles, "col").reshape(K_PARTS, -1, 2, group, rows_here, cols_here)
+    panels = jnp.transpose(tiles, (2, 0, 3, 4, 1, 5)).reshape(
+        2, K_PARTS, 1, group, rows_here, length_all // K_PARTS
+    )
+    lefts = panels[0].reshape(K_PARTS, group, I_PARTS, rows_here // I_PARTS, -1)
+    lefts = jnp.swapaxes(lefts, 1, 2)
+    rights = jnp.broadcast_to(panels[1], (K_PARTS, I_PARTS, *panels.shape[3:]))
+    panels = jnp.concatenate([lefts, rights], axis=3)
+    panels = exchange(panels.reshape(row_count, -1, length_all // K_PARTS), ROW)
+    few = rows_here // I_PARTS
     product = lax.dot_general(
-        lefts,
-        rights_all.reshape(-1, length_all),
+        panels[:, :few].reshape(-1, length_all // K_PARTS),
+        panels[:, few:].reshape(-1, length_all // K_PARTS),
         (((1,), (1,)), ((), ())),
         preferred_element_type=F32,
     ).astype(BF16)
-    product = exchange(product.reshape(inner_rows_count, rows_here, length_all), "row_1")
+    product = exchange(product.reshape(row_count, few, length_all), ROW)
+    product = jnp.sum(
+        product.reshape(K_PARTS, I_PARTS, group, few, length_all).astype(F32), axis=0
+    ).astype(BF16)
     product = jnp.transpose(
-        product.reshape(group, rows_here, col_count, cols_here), (2, 0, 1, 3)
+        product.reshape(I_PARTS, group, few, col_count, cols_here), (3, 1, 0, 2, 4)
     ).reshape(col_count, group, pairs_here)
     product = exchange(product, "col").reshape(channels, pairs_here)
 

time: 162 us -> 153 us (0.944)
  blocking collectives: 35.5 us -> 48.7 us
  waiting for transfers between devices: 53.1 us -> 39.9 us
  starting transfers between devices: 47.5 us -> 39 us
    all_to_all x3, blocking collectives: 35.5 us -> 48.7 us  [exchange(): return lax.all_to_all(blocks, axis, split_axis=0, concat_axis=0, tiled=True)]
    ppermute x3 -> x0, waiting for transfers between devices: 13.2 us -> none  [per_device(): arrived = lax.ppermute(rights, 'row_0', turn) if step else rights]
    ppermute x3 -> x0, starting transfers between devices: 10.1 us -> none  [per_device(): arrived = lax.ppermute(rights, 'row_0', turn) if step else rights]
  transfers between devices with their start and end apart: 8 -> 5, of which waited for: 8 -> 5; matrix products, arithmetic and copies ran while one was open for 2% -> 2% of each run, Pallas kernels for 0% -> 0%
where the time goes in v2:
time: 153 us; the launch traced here: 152 us
  blocking collectives  48.7 us (32%)
  waiting for transfers between devices  39.9 us (26%)
  starting transfers between devices  39 us (25%)
  local copies, waits for them, and re-layouts  15.2 us (10%)
  matrix products  4.25 us (3%)
  other arithmetic  4.14 us (3%)
    all_to_all x3, blocking collectives, exchange(): return lax.all_to_all(blocks, axis, split_axis=0, concat_axis=0, tiled=True)  48.7 us
    all_to_all x4, waiting for transfers between devices, exchange(): return lax.all_to_all(blocks, axis, split_axis=0, concat_axis=0, tiled=True)  34 us
    all_to_all x4, starting transfers between devices, exchange(): return lax.all_to_all(blocks, axis, split_axis=0, concat_axis=0, tiled=True)  28.7 us
    all_to_all x1, starting transfers between devices, per_device(): lax.all_to_all(bias_tile, 'col', split_axis=0, concat_axis=2, tiled=True)  10.3 us
    unnamed x33, local copies, waits for them, and re-layouts  6.33 us
    all_to_all x1, waiting for transfers between devices, per_device(): lax.all_to_all(bias_tile, 'col', split_axis=0, concat_axis=2, tiled=True)  5.84 us
  transfers between devices with their start and end apart: 5, of which 5 were waited for; matrix products, arithmetic and copies ran while one was open for 2% of the time, Pallas kernels for 0%

profile of v2, /device:TPU:1, one launch (start us, length us, event | category | flops | bytes accessed | tf_op | source)
XLA Modules:
  0.0 152.2 jit_solution(1350504281802614018)
XLA Ops:
  0.7 0.9 convert_reduce_fusion.3
  1.6 0.2 fusion.50
  1.8 0.3 fusion.93
  2.3 0.5 copy-done.1
  2.7 0.1 convert_reduce_fusion.2
  2.9 0.3 multiply_reduce_fusion.2
  3.2 0.7 copy-done.8
  3.8 0.3 convolution_bitcast_fusion.1
  4.2 0.2 copy.57
  4.3 0.8 reshape.310
  5.1 10.3 %all-to-all-start.1 = ((f32[16,1,1024]{2,1,0:T(1,128)}), f32[16,1,1024]{2,1,0:T(1,128)S(1)}, u32[]{:S(2)}, u32[]{:S(2)}) async-start(f32[16,1,1024]{2,1,0:T(1,128)} %reshape.310), calls=%async_computation.1 | async-start | bytes 131072 | tf_op jit(solution)/shard_map/all_to_all | solution.py:68
  15.4 5.8 %all-to-all-done.1 = f32[16,1,1024]{2,1,0:T(1,128)S(1)} async-done(((f32[16,1,1024]{2,1,0:T(1,128)}), f32[16,1,1024]{2,1,0:T(1,128)S(1)}, u32[]{:S(2)}, u32[]{:S(2)}) %all-to-all-start.1) | async-done | bytes 65568 | tf_op jit(solution)/shard_map/all_to_all | solution.py:68
  21.3 0.7 broadcast_in_dim.28
  21.9 12.2 %all-to-all-start = ((bf16[32,16,128]{2,1,0:T(8,128)(2,1)}), bf16[32,16,128]{2,1,0:T(8,128)(2,1)S(1)}, u32[]{:S(2)}, u32[]{:S(2)}) async-start(bf16[32,16,128]{2,1,0:T(8,128)(2,1)} %broadcast_in_dim.28), calls=%async_computation | async-start | bytes 262144 | tf_op jit(solution)/shard_map/all_to_all | solution.py:17
  34.3 0.6 copy-done.10
  35.0 0.7 copy-done.14
  35.8 0.5 broadcast.246
  36.3 0.8 reduce.3
  37.2 0.2 copy.58
  37.4 0.1 all_to_all.38
  37.5 8.2 %all-to-all-done = bf16[32,16,128]{2,1,0:T(8,128)(2,1)S(1)} async-done(((bf16[32,16,128]{2,1,0:T(8,128)(2,1)}), bf16[32,16,128]{2,1,0:T(8,128)(2,1)S(1)}, u32[]{:S(2)}, u32[]{:S(2)}) %all-to-all-start) | async-done | bytes 131104 | tf_op jit(solution)/shard_map/all_to_all | solution.py:17
  46.1 0.1 fusion.14
  46.2 0.2 fusion.94
  46.4 0.2 convolution_bitcast_fusion.2
  46.7 0.6 copy-done.4
  47.3 0.1 convolution_convert_fusion.1
  47.4 0.9 broadcast_in_dim.32
  48.3 5.4 %all-to-all-start.2 = ((bf16[16,16,1024]{2,1,0:T(8,128)(2,1)}), bf16[16,16,1024]{2,1,0:T(8,128)(2,1)S(1)}, u32[]{:S(2)}, u32[]{:S(2)}) async-start(bf16[16,16,1024]{2,1,0:T(8,128)(2,1)} %broadcast_in_dim.32), calls=%async_computation.2 | async-start | bytes 1048576 | tf_op jit(solution)/shard_map/all_to_all | solution.py:17
  53.9 9.6 %all-to-all-done.2 = bf16[16,16,1024]{2,1,0:T(8,128)(2,1)S(1)} async-done(((bf16[16,16,1024]{2,1,0:T(8,128)(2,1)}), bf16[16,16,1024]{2,1,0:T(8,128)(2,1)S(1)}, u32[]{:S(2)}, u32[]{:S(2)}) %all-to-all-start.2) | async-done | bytes 524320 | tf_op jit(solution)/shard_map/all_to_all | solution.py:17
  63.6 0.1 convert_reduce_fusion.4
  63.7 0.2 fusion.52
  63.9 0.2 convolution_convert_fusion.2
  64.1 0.2 copy-done.5
  64.3 0.7 broadcast_in_dim.33
  65.0 3.9 %all-to-all-start.3 = ((bf16[32,16,128]{2,1,0:T(8,128)(2,1)}), bf16[32,16,128]{2,1,0:T(8,128)(2,1)S(1)}, u32[]{:S(2)}, u32[]{:S(2)}) async-start(bf16[32,16,128]{2,1,0:T(8,128)(2,1)} %broadcast_in_dim.33), calls=%async_computation.3 | async-start | bytes 262144 | tf_op jit(solution)/shard_map/all_to_all | solution.py:17
  68.9 0.9 slice-done
  69.8 0.1 copy.65
  70.0 10.5 %all-to-all-done.3 = bf16[32,16,128]{2,1,0:T(8,128)(2,1)S(1)} async-done(((bf16[32,16,128]{2,1,0:T(8,128)(2,1)}), bf16[32,16,128]{2,1,0:T(8,128)(2,1)S(1)}, u32[]{:S(2)}, u32[]{:S(2)}) %all-to-all-start.3) | async-done | bytes 131104 | tf_op jit(solution)/shard_map/all_to_all | solution.py:17
  80.6 0.7 copy-done.6
  81.3 0.4 fusion.95
  81.7 0.2 multiply_reduce_fusion.1
  82.0 0.5 convolution_bitcast_fusion
  82.4 0.1 fusion.29
  82.6 12.4 %all_to_all.53 = bf16[16,16,512]{2,1,0:T(8,128)(2,1)S(1)} all-to-all(bf16[16,16,512]{2,1,0:T(8,128)(2,1)S(1)} %pad_maximum_fusion.1), channel_id=1, replica_groups=mesh['row_0'=4,'row_1'=8,'col'=16] {'col'}, dimensions={0} | all-to-all | bytes 524288 | tf_op jit(solution)/shard_map/all_to_all | solution.py:17
  95.0 0.6 reshape.296
  95.6 0.3 fusion.91
  95.9 0.3 copy.62
  96.2 0.4 broadcast_in_dim.34
  96.6 0.3 copy.61
  97.0 0.4 reshape_squeeze.3
  97.4 17.7 %all_to_all.54 = bf16[32,24,256]{2,1,0:T(8,128)(2,1)S(1)} all-to-all(bf16[32,24,256]{2,1,0:T(8,128)(2,1)S(1)} %bitcast.100), channel_id=1, replica_groups=mesh['row_0'=4,'row_1'=8,'col'=16] {'row_0','row_1'}, dimensions={0} | all-to-all | bytes 786432 | tf_op jit(solution)/shard_map/all_to_all | solution.py:17
  115.1 0.3 fusion.3
  115.4 18.6 %all_to_all.55 = bf16[32,8,512]{2,1,0:T(8,128)(2,1)S(1)} all-to-all(bf16[32,8,512]{2,1,0:T(8,128)(2,1)S(1)} %fusion.3), channel_id=1, replica_groups=mesh['row_0'=4,'row_1'=8,'col'=16] {'row_0','row_1'}, dimensions={0} | all-to-all | bytes 524288 | tf_op jit(solution)/shard_map/all_to_all | solution.py:17
  134.0 0.3 reshape.302
  134.3 0.1 copy.64
  134.4 1.1 reshape.303
  135.6 7.2 %all-to-all-start.7 = ((bf16[16,8,512]{2,1,0:T(8,128)(2,1)}), bf16[16,8,512]{2,1,0:T(8,128)(2,1)S(1)}, u32[]{:S(2)}, u32[]{:S(2)}) async-start(bf16[16,8,512]{2,1,0:T(8,128)(2,1)} %reshape.303), calls=%async_computation.7 | async-start | bytes 262144 | tf_op jit(solution)/shard_map/all_to_all | solution.py:17
  142.8 0.3 fusion.8
  143.1 5.8 %all-to-all-done.7 = bf16[16,8,512]{2,1,0:T(8,128)(2,1)S(1)} async-done(((bf16[16,8,512]{2,1,0:T(8,128)(2,1)}), bf16[16,8,512]{2,1,0:T(8,128)(2,1)S(1)}, u32[]{:S(2)}, u32[]{:S(2)}) %all-to-all-start.7) | async-done | bytes 131104 | tf_op jit(solution)/shard_map/all_to_all | solution.py:17
  149.0 0.7 copy-done.7
  149.7 0.3 fusion.96
  150.1 0.2 multiply_reduce_fusion
  150.3 0.6 copy-done.12
  151.0 1.1 fusion.9
  (67 shorter events, 2.0 us)
Async XLA Ops:
  0.6 1.2 copy-start
  0.6 1.0 copy-start.3
  1.8 0.9 copy-start.1
  3.1 0.7 copy-start.8
  5.1 10.3 %copy-start.9 = (s32[512]{0:T(512)S(1)}, s32[512]{0:T(512)}, u32[]{:S(2)}) copy-start(s32[512]{0:T(512)} %param.16) | copy-start | bytes 6148
  5.1 16.1 %all-to-all-start.1 = ((f32[16,1,1024]{2,1,0:T(1,128)}), f32[16,1,1024]{2,1,0:T(1,128)S(1)}, u32[]{:S(2)}, u32[]{:S(2)}) async-start(f32[16,1,1024]{2,1,0:T(1,128)} %reshape.310), calls=%async_computation.1 | async-start | bytes 131072 | tf_op jit(solution)/shard_map/all_to_all | solution.py:68
  21.9 23.8 %all-to-all-start = ((bf16[32,16,128]{2,1,0:T(8,128)(2,1)}), bf16[32,16,128]{2,1,0:T(8,128)(2,1)S(1)}, u32[]{:S(2)}, u32[]{:S(2)}) async-start(bf16[32,16,128]{2,1,0:T(8,128)(2,1)} %broadcast_in_dim.28), calls=%async_computation | async-start | bytes 262144 | tf_op jit(solution)/shard_map/all_to_all | solution.py:17
  34.2 0.7 copy-start.10
  35.0 0.7 copy-start.14
  46.4 0.9 copy-start.4
  48.3 15.2 %all-to-all-start.2 = ((bf16[16,16,1024]{2,1,0:T(8,128)(2,1)}), bf16[16,16,1024]{2,1,0:T(8,128)(2,1)S(1)}, u32[]{:S(2)}, u32[]{:S(2)}) async-start(bf16[16,16,1024]{2,1,0:T(8,128)(2,1)} %broadcast_in_dim.32), calls=%async_computation.2 | async-start | bytes 1048576 | tf_op jit(solution)/shard_map/all_to_all | solution.py:17
  53.9 10.0 %copy-start.11 = (bf16[1024,128]{1,0:T(8,128)(2,1)S(1)}, bf16[1024,128]{1,0:T(8,128)(2,1)}, u32[]{:S(2)}) copy-start(bf16[1024,128]{1,0:T(8,128)(2,1)} %param.22) | copy-start | bytes 786436
  63.7 0.6 copy-start.5
  65.0 15.5 %all-to-all-start.3 = ((bf16[32,16,128]{2,1,0:T(8,128)(2,1)}), bf16[32,16,128]{2,1,0:T(8,128)(2,1)S(1)}, u32[]{:S(2)}, u32[]{:S(2)}) async-start(bf16[32,16,128]{2,1,0:T(8,128)(2,1)} %broadcast_in_dim.33), calls=%async_computation.3 | async-start | bytes 262144 | tf_op jit(solution)/shard_map/all_to_all | solution.py:17
  68.9 0.9 slice-start
  80.6 0.8 copy-start.6
  135.6 7.2 %copy-start.2 = (bf16[128,5,128]{2,0,1:T(8,128)(2,1)S(1)}, bf16[128,5,128]{2,0,1:T(8,128)(2,1)}, u32[]{:S(2)}) copy-start(bf16[128,5,128]{2,0,1:T(8,128)(2,1)} %param.24) | copy-start | bytes 491524
  135.6 13.3 %all-to-all-start.7 = ((bf16[16,8,512]{2,1,0:T(8,128)(2,1)}), bf16[16,8,512]{2,1,0:T(8,128)(2,1)S(1)}, u32[]{:S(2)}, u32[]{:S(2)}) async-start(bf16[16,8,512]{2,1,0:T(8,128)(2,1)} %reshape.303), calls=%async_computation.7 | async-start | bytes 262144 | tf_op jit(solution)/shard_map/all_to_all | solution.py:17
  148.9 0.8 copy-start.7
  150.1 0.9 copy-start.12
  150.1 1.0 copy-start.13

commit v3 on v2

--- a/solution.py
+++ b/solution.py
@@ -3,6 +3,8 @@
 import jax
 import jax.numpy as jnp
 from jax import lax
+from jax.experimental import pallas as pl
+from jax.experimental.pallas import tpu as pltpu
 from jax.sharding import Mesh
 from jax.sharding import PartitionSpec as P
 
@@ -26,6 +28,74 @@
     center = values - jnp.mean(values, axis=axis, keepdims=True)
     spread = jnp.mean(center * center, axis=axis, keepdims=True)
     return center * lax.rsqrt(spread + 1e-05)
+
+
+def local_kernel(body, out_shape, name, *operands, scalars=0):
+    spaces = [pltpu.SMEM if k < scalars else pltpu.VMEM for k in range(len(operands))]
+    held = [
+        x if space is pltpu.SMEM else pltpu.with_memory_space_constraint(x, space)
+        for x, space in zip(operands, spaces)
+    ]
+    return pl.pallas_call(
+        body,
+        out_shape=out_shape,
+        in_specs=[pl.BlockSpec(memory_space=space) for space in spaces],
+        out_specs=jax.tree.map(lambda _: pl.BlockSpec(memory_space=pltpu.VMEM), out_shape),
+        name=name,
+    )(*held)
+
+
+def mm(a, b, over_a, over_b):
+    return lax.dot_general(a, b, (((over_a,), (over_b,)), ((), ())), preferred_element_type=F32)
+
+
+def settle_body(terms, sequence, outer_in, sequence_out, left_twice, right_copies):
+    update = jnp.sum(terms[...].astype(F32), axis=0)
+    summed = (sequence[...].astype(F32) + update).astype(BF16)
+    sequence_out[...] = summed
+    normed = layer_norm(summed.astype(F32)).astype(BF16)
+    outer_rows = mm(normed, outer_in[...], 1, 0).astype(BF16).astype(F32)
+    rows, width = outer_rows.shape
+    half = width // 2
+    first = lax.broadcasted_iota(jnp.int32, (rows, width), 1) < half
+    turned = pltpu.roll(outer_rows, half, 1)
+    left_twice[...] = jnp.where(first, outer_rows, turned)
+    packed = jnp.where(first[: rows // 2], turned[: rows // 2], outer_rows[rows // 2 :])
+    right_copies[...] = jnp.broadcast_to(packed.astype(BF16)[None], right_copies.shape)
+
+
+def pair_body(start, rights, left_twice, pair, outer_out, gates_in, values_in, last_in, live, tiles, mid, out_gate):
+    rows, cols, channels = pair.shape
+    half = channels // 2
+    taken = rights[pl.ds(start[0], cols // rows)].astype(F32)
+    first = lax.broadcasted_iota(jnp.int32, (rows // 2, channels), 1) < half
+    pieces = []
+    for k in range(cols // rows):
+        turned = pltpu.roll(taken[k], half, 1)
+        pieces.append(jnp.where(first, taken[k], turned))
+        pieces.append(jnp.where(first, turned, taken[k]))
+    right_twice = jnp.concatenate(pieces, axis=0)
+    left = left_twice[...][:, None, :]
+    right = right_twice[None, :, :]
+    lane = lax.broadcasted_iota(jnp.int32, (rows, cols, channels), 2)
+    feat = jnp.where(lane < half, left * right, left - right).astype(BF16)
+    feat = feat.reshape(rows * cols, channels)
+    pair_mid = pair[...].astype(F32).reshape(rows * cols, channels) + mm(feat, outer_out[...], 1, 0)
+    mid[...] = pair_mid
+    normed = layer_norm(pair_mid).astype(BF16)
+    opened = jax.nn.sigmoid(mm(gates_in[...], normed, 1, 1))
+    operands = opened * mm(values_in[...], normed, 1, 1) * live[...]
+    tiles[...] = operands.astype(BF16).reshape(tiles.shape)
+    out_gate[...] = jax.nn.sigmoid(mm(normed, last_in[...], 1, 0))
+
+
+def tail_body(product, mid, out_gate, triangle_out, transition_up, transition_down, out):
+    normed_product = layer_norm(product[...].astype(F32), axis=0)
+    normed_product = jnp.transpose(normed_product).astype(BF16)
+    late = mid[...] + out_gate[...] * mm(normed_product, triangle_out[...], 1, 0)
+    normed_late = layer_norm(late).astype(BF16)
+    hidden = jnp.maximum(mm(normed_late, transition_up[...], 1, 0), 0.0).astype(BF16)
+    out[...] = (late + mm(hidden, transition_down[...], 1, 0)).astype(BF16)
 
 
 def per_device(
@@ -59,12 +129,54 @@
     query = projected[:, 0].astype(BF16)
     key_values = projected[:, 1:3].astype(BF16).reshape(rows_here, -1)
     gate = jax.nn.sigmoid(projected[:, 3])
-    key_values, pair_state = lax.optimization_barrier((key_values, pair_state))
     key_values_all = from_everyone(key_values, ROW).reshape(length_all, -1)
 
     pair_wide = pair_state.astype(F32)
     normed_pair = layer_norm(pair_wide).astype(BF16)
     bias_tile = jnp.einsum("ijc,ch->hij", normed_pair, bias_weight, preferred_element_type=F32)
+    one = (1 + jnp.minimum(col_index, 0)).astype(BF16)
+    attention_out, outer_in, outer_out = attention_out * one, outer_in * one, outer_out * one
+    triangle_out, transition_up = triangle_out * one, transition_up * one
+    transition_down = transition_down * one
+    group = channels // col_count
+    by_channel = jnp.transpose(triangle_in, (1, 2, 0)) * one
+    grouped = by_channel[:4].reshape(2, 2, col_count, group, channels)
+    gates_in = jnp.swapaxes(grouped[:, 0], 0, 1).reshape(2 * channels, channels)
+    values_in = jnp.swapaxes(grouped[:, 1], 0, 1).reshape(2 * channels, channels)
+    last_in = triangle_in[:, 4] * one
+    live = residue_mask.astype(F32)
+    row_live = lax.dynamic_slice_in_dim(live, row_start, rows_here, 0)
+    col_live = lax.dynamic_slice_in_dim(live, col_start, cols_here, 0)
+    pair_live = (row_live[:, None] * col_live[None, :]).reshape(1, pairs_here)
+    (
+        key_values_all,
+        bias_tile,
+        attention_out,
+        outer_in,
+        outer_out,
+        triangle_out,
+        transition_up,
+        transition_down,
+        gates_in,
+        values_in,
+        last_in,
+        pair_live,
+    ) = lax.optimization_barrier(
+        (
+            key_values_all,
+            bias_tile,
+            attention_out,
+            outer_in,
+            outer_out,
+            triangle_out,
+            transition_up,
+            transition_down,
+            gates_in,
+            values_in,
+            last_in,
+            pair_live,
+        )
+    )
     pair_bias = lax.all_to_all(bias_tile, "col", split_axis=0, concat_axis=2, tiled=True)
     heads_here = pair_bias.shape[0]
 
@@ -93,50 +205,41 @@
     ).reshape(rows_here, -1)
     mixed = (gate * gathered).astype(BF16)
     head_terms = jnp.dot(mixed, attention_out, preferred_element_type=F32).astype(BF16)
-    update = jnp.sum(from_everyone(head_terms, "col").astype(F32), axis=0)
-    sequence_out = (sequence.astype(F32) + update).astype(BF16)
-
-    normed_out = layer_norm(sequence_out.astype(F32)).astype(BF16)
-    outer_rows = jnp.dot(normed_out, outer_in, preferred_element_type=F32).astype(BF16)
-    half_width = outer_rows.shape[1] // 2
-    outer_all = from_everyone(outer_rows, ROW).reshape(length_all, -1)
-    right_side = lax.dynamic_slice_in_dim(outer_all, col_start, cols_here, 0)
-    right_side = right_side[:, half_width:].astype(F32)
-    left_side = outer_rows[:, :half_width].astype(F32)
-    outer_feat = jnp.concatenate(
-        [
-            left_side[:, None, :] * right_side[None, :, :],
-            left_side[:, None, :] - right_side[None, :, :],
-        ],
-        axis=-1,
-    ).astype(BF16)
-    pair_mid = pair_wide.reshape(pairs_here, channels) + jnp.dot(
-        outer_feat.reshape(pairs_here, 2 * half_width), outer_out, preferred_element_type=F32
-    )
-    normed_mid = layer_norm(pair_mid).astype(BF16)
-
-    operand_in = triangle_in[:, :4].reshape(channels, 4 * channels)
-    tri = lax.dot_general(
-        operand_in, normed_mid, (((0,), (1,)), ((), ())), preferred_element_type=F32
-    ).reshape(4, channels, pairs_here)
-    live = residue_mask.astype(F32)
-    row_live = lax.dynamic_slice_in_dim(live, row_start, rows_here, 0)
-    col_live = lax.dynamic_slice_in_dim(live, col_start, cols_here, 0)
-    pair_live = (row_live[:, None] * col_live[None, :]).reshape(1, pairs_here)
-    left_op = (jax.nn.sigmoid(tri[0]) * tri[1] * pair_live).astype(BF16)
-    right_op = (jax.nn.sigmoid(tri[2]) * tri[3] * pair_live).astype(BF16)
-    out_gate = jax.nn.sigmoid(
-        jnp.dot(normed_mid, triangle_in[:, 4], preferred_element_type=F32)
-    )
-
-    group = channels // col_count
-    tiles = jnp.concatenate(
-        [
-            left_op.reshape(col_count, group, pairs_here),
-            right_op.reshape(col_count, group, pairs_here),
-        ],
-        axis=1,
-    )
+    terms = from_everyone(head_terms, "col")
+    width = outer_in.shape[1]
+    sequence_out, left_twice, right_copies = local_kernel(
+        settle_body,
+        (
+            jax.ShapeDtypeStruct(sequence.shape, BF16),
+            pltpu.VMEM((rows_here, width), F32),
+            pltpu.VMEM((row_count, rows_here // 2, width), BF16),
+        ),
+        "settle",
+        terms,
+        sequence,
+        outer_in,
+    )
+    rights = exchange(right_copies, ROW)
+    tiles, pair_mid, out_gate = local_kernel(
+        pair_body,
+        (
+            pltpu.VMEM((col_count, 2 * group, pairs_here), BF16),
+            pltpu.VMEM((pairs_here, channels), F32),
+            pltpu.VMEM((pairs_here, channels), F32),
+        ),
+        "pair",
+        (col_index * (cols_here // rows_here)).reshape(1),
+        rights,
+        left_twice,
+        pair_state,
+        outer_out,
+        gates_in,
+        values_in,
+        last_in,
+        pair_live,
+        scalars=1,
+    )
+
     tiles = exchange(tiles, "col").reshape(K_PARTS, -1, 2, group, rows_here, cols_here)
     panels = jnp.transpose(tiles, (2, 0, 3, 4, 1, 5)).reshape(
         2, K_PARTS, 1, group, rows_here, length_all // K_PARTS
@@ -162,17 +265,17 @@
     ).reshape(col_count, group, pairs_here)
     product = exchange(product, "col").reshape(channels, pairs_here)
 
-    normed_product = layer_norm(product.astype(F32), axis=0).astype(BF16)
-    projected_product = lax.dot_general(
-        normed_product, triangle_out, (((0,), (0,)), ((), ())), preferred_element_type=F32
-    )
-    pair_late = pair_mid + out_gate * projected_product
-    normed_late = layer_norm(pair_late).astype(BF16)
-    hidden = jax.nn.relu(
-        jnp.dot(normed_late, transition_up, preferred_element_type=F32)
-    ).astype(BF16)
-    lowered = jnp.dot(hidden, transition_down, preferred_element_type=F32)
-    pair_out = (pair_late + lowered).astype(BF16).reshape(rows_here, cols_here, channels)
+    pair_out = local_kernel(
+        tail_body,
+        jax.ShapeDtypeStruct((pairs_here, channels), BF16),
+        "tail",
+        product,
+        pair_mid,
+        out_gate,
+        triangle_out,
+        transition_up,
+        transition_down,
+    ).reshape(rows_here, cols_here, channels)
     return (sequence_out, pair_out)
 
 

time: 153 us -> 148 us (0.967)
  blocking collectives: 48.7 us -> 92.7 us
  waiting for transfers between devices: 39.9 us -> 8.96 us
  starting transfers between devices: 39 us -> 23.9 us
  Pallas kernels: 0 us -> 3.12 us
  matrix products: 4.25 us -> 1.39 us
  local copies, waits for them, and re-layouts: 15.2 us -> 13.6 us
    all_to_all x3 -> x6, blocking collectives: 48.7 us -> 92.7 us  [exchange(): return lax.all_to_all(blocks, axis, split_axis=0, concat_axis=0, tiled=True)]
    all_to_all x4 -> x1, waiting for transfers between devices: 34 us -> 3.46 us  [exchange(): return lax.all_to_all(blocks, axis, split_axis=0, concat_axis=0, tiled=True)]
    all_to_all x4 -> x1, starting transfers between devices: 28.7 us -> 16.6 us  [exchange(): return lax.all_to_all(blocks, axis, split_axis=0, concat_axis=0, tiled=True)]
    pallas_call x0 -> x3, Pallas kernels: none -> 3.12 us  [local_kernel(): pl.pallas_call(body, out_shape=out_shape, in_specs=[pl.BlockSpec(memory_s...]
    all_to_all x1, starting transfers between devices: 10.3 us -> 7.26 us  [per_device(): lax.all_to_all(bias_tile, 'col', split_axis=0, concat_axis=2, tiled=True)]
    dot_general x6 -> x0, matrix products: 2.86 us -> none  [the longest x1 1.14 us: per_device(): lowered = jnp.dot(hidden, transition_down, preferred_element_type=F32)]
    unnamed x33 -> x31, local copies, waits for them, and re-layouts: 6.33 us -> 7.35 us
  transfers between devices with their start and end apart: 5 -> 2, of which waited for: 5 -> 2; matrix products, arithmetic and copies ran while one was open for 2% -> 1% of each run, Pallas kernels for 0% -> 0%
where the time goes in v3:
time: 148 us
  blocking collectives  92.7 us (63%)
  starting transfers between devices  23.9 us (16%)
  local copies, waits for them, and re-layouts  13.6 us (9%)
  waiting for transfers between devices  8.96 us (6%)
  Pallas kernels  3.12 us (2%)
  other arithmetic  2.92 us (2%)
    all_to_all x6, blocking collectives, exchange(): return lax.all_to_all(blocks, axis, split_axis=0, concat_axis=0, tiled=True)  92.7 us
    all_to_all x1, starting transfers between devices, exchange(): return lax.all_to_all(blocks, axis, split_axis=0, concat_axis=0, tiled=True)  16.6 us
    unnamed x31, local copies, waits for them, and re-layouts  7.35 us
    all_to_all x1, starting transfers between devices, per_device(): lax.all_to_all(bias_tile, 'col', split_axis=0, concat_axis=2, tiled=True)  7.26 us
    all_to_all x1, waiting for transfers between devices, per_device(): lax.all_to_all(bias_tile, 'col', split_axis=0, concat_axis=2, tiled=True)  5.5 us
    all_to_all x1, waiting for transfers between devices, exchange(): return lax.all_to_all(blocks, axis, split_axis=0, concat_axis=0, tiled=True)  3.46 us
    pallas_call x3, Pallas kernels, local_kernel(): pl.pallas_call(body, out_shape=out_shape, in_specs=[pl.BlockSpec(memory_s...  3.12 us
  transfers between devices with their start and end apart: 2, of which 2 were waited for; matrix products, arithmetic and copies ran while one was open for 1% of the time, Pallas kernels for 0%

profile of v3, /device:TPU:1, one launch (start us, length us, event | category | flops | bytes accessed | tf_op | source)
XLA Modules:
  0.0 147.6 jit_solution(2744299204063302112)
XLA Ops:
  0.7 0.9 convert_reduce_fusion.1
  1.6 0.2 fusion.17
  1.8 0.3 fusion.49
  2.2 0.1 reshape.198
  2.3 0.7 broadcast_in_dim.26
  2.9 16.6 %all-to-all-start = ((bf16[32,16,128]{2,1,0:T(8,128)(2,1)}), bf16[32,16,128]{2,1,0:T(8,128)(2,1)S(1)}, u32[]{:S(2)}, u32[]{:S(2)}) async-start(bf16[32,16,128]{2,1,0:T(8,128)(2,1)} %broadcast_in_dim.26), calls=%async_computation | async-start | bytes 262144 | tf_op jit(solution)/shard_map/all_to_all | solution.py:19
  19.6 0.7 copy-done.11
  20.3 0.7 copy-done.12
  21.0 0.1 dynamic_slice.15
  21.0 0.1 dynamic_slice.12
  21.1 0.1 dynamic_slice.13
  21.2 0.1 convert_reduce_fusion
  21.4 0.3 fusion.9
  21.6 0.1 compare_convert_fusion
  21.7 0.4 copy-done.4
  22.1 0.2 copy.48
  22.3 0.7 copy-done.5
  23.0 0.9 copy-done.6
  23.9 0.9 copy-done.7
  24.9 0.1 fusion.26
  25.0 0.6 copy-done.8
  25.7 0.7 copy-done.10
  26.4 0.3 convolution_bitcast_fusion
  26.7 0.1 broadcast_multiply_fusion.6
  26.8 0.1 mul.161.live
  26.8 0.1 convert_element_type.51
  27.0 0.6 copy-done.13
  27.6 0.1 dynamic_slice.14
  27.7 3.5 %all-to-all-done = bf16[32,16,128]{2,1,0:T(8,128)(2,1)S(1)} async-done(((bf16[32,16,128]{2,1,0:T(8,128)(2,1)}), bf16[32,16,128]{2,1,0:T(8,128)(2,1)S(1)}, u32[]{:S(2)}, u32[]{:S(2)}) %all-to-all-start) | async-done | bytes 131104 | tf_op jit(solution)/shard_map/all_to_all | solution.py:19
  31.2 0.2 copy.54
  31.3 0.8 reshape.219
  32.1 7.3 %all-to-all-start.1 = ((f32[16,1,1024]{2,1,0:T(1,128)}), f32[16,1,1024]{2,1,0:T(1,128)S(1)}, u32[]{:S(2)}, u32[]{:S(2)}) async-start(f32[16,1,1024]{2,1,0:T(1,128)} %reshape.219), calls=%async_computation.1 | async-start | bytes 131072 | tf_op jit(solution)/shard_map/all_to_all | solution.py:180
  39.4 0.1 fusion.48
  39.5 0.1 copy.52
  39.6 0.1 copy.51
  39.7 5.5 %all-to-all-done.1 = f32[16,1,1024]{2,1,0:T(1,128)S(1)} async-done(((f32[16,1,1024]{2,1,0:T(1,128)}), f32[16,1,1024]{2,1,0:T(1,128)S(1)}, u32[]{:S(2)}, u32[]{:S(2)}) %all-to-all-start.1) | async-done | bytes 65568 | tf_op jit(solution)/shard_map/all_to_all | solution.py:180
  45.2 0.5 broadcast.122
  45.7 0.8 reduce.1
  46.5 0.1 reshape.220
  46.7 0.2 copy.55
  46.8 0.1 all_to_all.38
  47.0 0.1 fusion.6
  47.1 0.2 fusion.50
  47.3 0.2 convolution_bitcast_fusion.1
  47.5 0.1 reshape.205
  47.6 0.1 convolution_convert_fusion.1
  47.8 12.6 %all_to_all.53.terms = bf16[16,16,1024]{2,1,0:T(8,128)(2,1)S(1)} all-to-all(bf16[16,16,1024]{2,1,0:T(8,128)(2,1)S(1)} %broadcast_in_dim.51), channel_id=1, replica_groups=mesh['row_0'=4,'row_1'=8,'col'=16] {'col'}, dimensions={0} | all-to-all | bytes 1048576 | tf_op jit(solution)/shard_map/all_to_all | solution.py:19
  60.4 0.7 settle.1
  61.2 18.5 %all_to_all.54.rights = bf16[32,8,128]{2,1,0:T(8,128)(2,1)S(1)} all-to-all(bf16[32,8,128]{2,1,0:T(8,128)(2,1)S(1)} %get-tuple-element.25), channel_id=1, replica_groups=mesh['row_0'=4,'row_1'=8,'col'=16] {'row_0','row_1'}, dimensions={0} | all-to-all | bytes 131072 | tf_op jit(solution)/shard_map/all_to_all | solution.py:19
  79.7 0.8 pair.2
  80.5 12.3 %all_to_all.55 = bf16[16,16,512]{2,1,0:T(8,128)(2,1)S(1)} all-to-all(bf16[16,16,512]{2,1,0:T(8,128)(2,1)S(1)} %get-tuple-element.32), channel_id=1, replica_groups=mesh['row_0'=4,'row_1'=8,'col'=16] {'col'}, dimensions={0} | all-to-all | bytes 524288 | tf_op jit(solution)/shard_map/all_to_all | solution.py:19
  92.7 0.6 reshape.207
  93.3 1.2 copy.65
  94.6 0.1 fusion.47
  94.7 0.4 reshape_squeeze.3
  95.0 0.4 broadcast_in_dim.52
  95.4 17.7 %all_to_all.56 = bf16[32,24,256]{2,1,0:T(8,128)(2,1)S(1)} all-to-all(bf16[32,24,256]{2,1,0:T(8,128)(2,1)S(1)} %bitcast.81), channel_id=1, replica_groups=mesh['row_0'=4,'row_1'=8,'col'=16] {'row_0','row_1'}, dimensions={0} | all-to-all | bytes 786432 | tf_op jit(solution)/shard_map/all_to_all | solution.py:19
  113.2 0.3 fusion.1
  113.4 18.6 %all_to_all.57 = bf16[32,8,512]{2,1,0:T(8,128)(2,1)S(1)} all-to-all(bf16[32,8,512]{2,1,0:T(8,128)(2,1)S(1)} %fusion.1), channel_id=1, replica_groups=mesh['row_0'=4,'row_1'=8,'col'=16] {'row_0','row_1'}, dimensions={0} | all-to-all | bytes 524288 | tf_op jit(solution)/shard_map/all_to_all | solution.py:19
  132.0 0.3 reshape.213
  132.3 0.1 copy.59
  132.5 0.5 reshape.214
  132.9 13.0 %all_to_all.58 = bf16[16,8,512]{2,1,0:T(8,128)(2,1)S(1)} all-to-all(bf16[16,8,512]{2,1,0:T(8,128)(2,1)S(1)} %reshape.214), channel_id=1, replica_groups=mesh['row_0'=4,'row_1'=8,'col'=16] {'col'}, dimensions={0} | all-to-all | bytes 262144 | tf_op jit(solution)/shard_map/all_to_all | solution.py:19
  146.0 1.6 %tail.1 = bf16[512,128]{1,0:T(8,128)(2,1)} custom-call(bf16[128,512]{1,0:T(8,128)(2,1)S(1)} %bitcast.76, f32[512,128]{1,0:T(8,128)S(1)} %get-tuple-element.33.mid, f32[512,128]{1,0:T(8,128)S(1)} %get-tuple-element.34.out_gate, bf16[128,128]{1,0:T(8,128)(2,1)S(1)} %get-tuple-element.35.triangle_out, ...), custom_call_target="tpu_custom_call" | custom-call | tf_op jit(solution)/shard_map/tail/pallas_call | solution.py:39
  (46 shorter events, 0.5 us)
Async XLA Ops:
  0.6 1.2 copy-start
  0.6 1.0 copy-start.2
  2.9 18.2 %copy-start.1 = (bf16[16,32,128]{2,1,0:T(8,128)(2,1)S(1)}, bf16[16,32,128]{2,1,0:T(8,128)(2,1)}, u32[]{:S(2)}) copy-start(bf16[16,32,128]{2,1,0:T(8,128)(2,1)} %pair.3) | copy-start | bytes 393220
  2.9 28.2 %all-to-all-start = ((bf16[32,16,128]{2,1,0:T(8,128)(2,1)}), bf16[32,16,128]{2,1,0:T(8,128)(2,1)S(1)}, u32[]{:S(2)}, u32[]{:S(2)}) async-start(bf16[32,16,128]{2,1,0:T(8,128)(2,1)} %broadcast_in_dim.26), calls=%async_computation | async-start | bytes 262144 | tf_op jit(solution)/shard_map/all_to_all | solution.py:19
  19.6 0.7 copy-start.11
  20.3 0.7 copy-start.12
  21.2 0.9 copy-start.4
  22.1 0.9 copy-start.5
  23.0 0.9 copy-start.6
  23.9 0.9 copy-start.7
  24.9 0.8 copy-start.8
  24.9 0.8 copy-start.9
  25.7 0.7 copy-start.10
  26.7 1.0 copy-start.3
  27.0 0.7 copy-start.13
  32.1 13.1 %all-to-all-start.1 = ((f32[16,1,1024]{2,1,0:T(1,128)}), f32[16,1,1024]{2,1,0:T(1,128)S(1)}, u32[]{:S(2)}, u32[]{:S(2)}) async-start(f32[16,1,1024]{2,1,0:T(1,128)} %reshape.219), calls=%async_computation.1 | async-start | bytes 131072 | tf_op jit(solution)/shard_map/all_to_all | solution.py:180

commit v4 on v3

--- a/solution.py
+++ b/solution.py
@@ -13,6 +13,8 @@
 F32 = jnp.float32
 K_PARTS = 2
 I_PARTS = 2
+LANES = 128
+GROUPS = 4
 
 
 def exchange(blocks, axis):
@@ -30,7 +32,7 @@
     return center * lax.rsqrt(spread + 1e-05)
 
 
-def local_kernel(body, out_shape, name, *operands, scalars=0):
+def local_kernel(body, out_shape, name, *operands, scalars=0, scratch=()):
     spaces = [pltpu.SMEM if k < scalars else pltpu.VMEM for k in range(len(operands))]
     held = [
         x if space is pltpu.SMEM else pltpu.with_memory_space_constraint(x, space)
@@ -41,12 +43,160 @@
         out_shape=out_shape,
         in_specs=[pl.BlockSpec(memory_space=space) for space in spaces],
         out_specs=jax.tree.map(lambda _: pl.BlockSpec(memory_space=pltpu.VMEM), out_shape),
+        scratch_shapes=scratch,
         name=name,
     )(*held)
 
 
 def mm(a, b, over_a, over_b):
     return lax.dot_general(a, b, (((over_a,), (over_b,)), ((), ())), preferred_element_type=F32)
+
+
+def turn_lanes(value, groups):
+    steps = groups % GROUPS
+    return pltpu.roll(value, steps * (LANES // GROUPS), 1) if steps else value
+
+
+def regroup(pick, shape):
+    group = lax.broadcasted_iota(jnp.int32, shape, 1) // (LANES // GROUPS)
+    tile = pick(0)
+    for k in range(1, GROUPS):
+        tile = jnp.where(group == k, pick(k), tile)
+    return tile
+
+
+def project_body(sequence, weights, key_values, query, gate):
+    normed = layer_norm(sequence[...].astype(F32)).astype(BF16)
+    projected = mm(normed, weights[...], 1, 1)
+    rows = projected.shape[0]
+    head, rest = projected[:, :LANES], projected[:, LANES:]
+    first = lax.broadcasted_iota(jnp.int32, (rows, LANES), 1) < LANES // 2
+    both = jnp.where(first, pltpu.roll(head, LANES // 2, 1), pltpu.roll(rest, LANES // 2, 1))
+    key_values[...] = jnp.broadcast_to(both.astype(BF16)[None], key_values.shape)
+    query[...] = jnp.where(first, head, 0.0).astype(BF16).astype(F32)
+    gate[...] = jnp.where(first, 0.0, jax.nn.sigmoid(rest))
+
+
+def bias_body(pair, bias_in, blocks):
+    rows, cols, channels = pair.shape
+    wide = pair[...].astype(F32)
+    turned = jnp.concatenate([wide[GROUPS * (p % GROUPS) + p // GROUPS] for p in range(rows)], axis=0)
+    normed = layer_norm(turned).astype(BF16)
+    bias = mm(bias_in[...], normed, 1, 1)
+    count = blocks.shape[0]
+    for h in range(2):
+        for t in range(GROUPS):
+            part = bias[h * count : (h + 1) * count, t * LANES : (t + 1) * LANES]
+            blocks[:, h * GROUPS + t, :] = part
+
+
+def attention_body(
+    start, offsets, blocks, key_values, query, gate, mask, chain, attention_out, copies, spread, joined
+):
+    count, eight, _ = blocks.shape
+    four = eight // 2
+    length = count * (LANES // GROUPS)
+    rows = query.shape[0]
+    lane = lax.broadcasted_iota(jnp.int32, (four, LANES), 1)
+    for g in range(GROUPS):
+        taken = query[g * four : (g + 1) * four, :]
+        for h in range(2):
+            own = (lane >= h * (LANES // 4)) & (lane < (h + 1) * (LANES // 4))
+            spread[g * eight + h * four : g * eight + (h + 1) * four, :] = jnp.where(own, taken, 0.0)
+    everyone = key_values[...].reshape(length, LANES)
+    raw = mm(spread[...].astype(BF16), everyone, 1, 1)
+    raw = raw * (1.0 / math.sqrt(LANES // 4))
+    position = lax.broadcasted_iota(jnp.int32, (eight, length), 1)
+    row = lax.broadcasted_iota(jnp.int32, (eight, length), 0)
+    chains = jnp.broadcast_to(chain[...], (eight, length))
+    kept = jnp.broadcast_to(mask[...], (eight, length)) == 1
+    offset = jnp.where(row < four, offsets[0], offsets[1])
+    weights = []
+    for g in range(GROUPS):
+        pieces = []
+        for tile in range(count // GROUPS):
+            pieces.append(
+                regroup(
+                    lambda k, tile=tile, g=g: turn_lanes(blocks[GROUPS * tile + k], k - g),
+                    (eight, LANES),
+                )
+            )
+        bias = jnp.concatenate(pieces, axis=1)
+        here = position == start[0] + g * four + row % four
+        own_chain = jnp.sum(jnp.where(here, chains, 0).astype(F32), axis=1, keepdims=True)
+        same = chains.astype(F32) == own_chain
+        scores = raw[g * eight : (g + 1) * eight] + bias + jnp.where(same, offset, 0.0)
+        allowed = kept | here
+        highest = jnp.max(jnp.where(allowed, scores, -jnp.inf), axis=1, keepdims=True)
+        raised = jnp.where(allowed, jnp.exp(scores - highest), 0.0)
+        weights.append(raised / jnp.sum(raised, axis=1, keepdims=True))
+    mixed = mm(jnp.concatenate(weights, axis=0).astype(BF16), everyone, 1, 0)
+    for g in range(GROUPS):
+        upper = mixed[g * eight : g * eight + four]
+        lower = mixed[g * eight + four : (g + 1) * eight]
+        joined[g * four : (g + 1) * four, :] = jnp.where(lane < LANES * 3 // 4, upper, lower)
+    gated = pltpu.roll(gate[...] * joined[...], LANES // 2, 1)[:, : LANES // 2].astype(BF16)
+    terms = mm(gated, attention_out[...], 1, 0).astype(BF16)
+    copies[...] = jnp.broadcast_to(terms[None], copies.shape)
+
+
+def spread_body(tiles, order, panels):
+    count, chans, pairs = tiles.shape
+    rows = pairs // (LANES // GROUPS)
+    per = count // GROUPS
+    by_row = []
+    for i in range(rows):
+        at, g = i // GROUPS * LANES, i % GROUPS
+        by_row.append(
+            jnp.concatenate(
+                [
+                    regroup(
+                        lambda k, tile=tile, g=g, at=at: turn_lanes(
+                            tiles[GROUPS * tile + k, :, at : at + LANES].astype(F32), k - g
+                        ),
+                        (chans, LANES),
+                    )
+                    for tile in range(per)
+                ],
+                axis=1,
+            )
+        )
+    turned = mm(order[...], jnp.concatenate(by_row, axis=0).astype(BF16), 1, 0).astype(BF16)
+    half = chans // 2
+    few = rows // I_PARTS
+    wide = turned.shape[1] // K_PARTS
+    for k in range(K_PARTS):
+        for i in range(I_PARTS):
+            for c in range(half):
+                block = (k * I_PARTS + i) * half + c
+                at = c * rows + i * few
+                panels[block, :few, :] = turned[at : at + few, k * wide : (k + 1) * wide]
+                at = (half + c) * rows
+                panels[block, few:, :] = turned[at : at + rows, k * wide : (k + 1) * wide]
+
+
+def gather_body(parts, order, blocks):
+    total, few, length = parts.shape
+    count, group, pairs = blocks.shape
+    rows = pairs // (LANES // GROUPS)
+    summed = mm(order[...], parts[...].reshape(total * few, length), 1, 0)
+    for q in range(count):
+        tile, s = q // GROUPS, q % GROUPS
+        pieces = []
+        for t in range(rows // GROUPS):
+            pieces.append(
+                regroup(
+                    lambda k, t=t, tile=tile, s=s: turn_lanes(
+                        summed[
+                            (GROUPS * t + k) * group : (GROUPS * t + k + 1) * group,
+                            tile * LANES : (tile + 1) * LANES,
+                        ],
+                        k - s,
+                    ),
+                    (group, LANES),
+                )
+            )
+        blocks[q] = jnp.concatenate(pieces, axis=1).astype(BF16)
 
 
 def settle_body(terms, sequence, outer_in, sequence_out, left_twice, right_copies):
@@ -124,33 +274,63 @@
     row_start = row_index * rows_here
     col_start = col_index * cols_here
 
-    normed_seq = layer_norm(sequence.astype(F32)).astype(BF16)
-    projected = jnp.einsum("id,dpe->ipe", normed_seq, attention_in, preferred_element_type=F32)
-    query = projected[:, 0].astype(BF16)
-    key_values = projected[:, 1:3].astype(BF16).reshape(rows_here, -1)
-    gate = jax.nn.sigmoid(projected[:, 3])
-    key_values_all = from_everyone(key_values, ROW).reshape(length_all, -1)
-
-    pair_wide = pair_state.astype(F32)
-    normed_pair = layer_norm(pair_wide).astype(BF16)
-    bias_tile = jnp.einsum("ijc,ch->hij", normed_pair, bias_weight, preferred_element_type=F32)
+    group = channels // col_count
+    heads_here = bias_weight.shape[1] // col_count
+
+    weights = jnp.transpose(attention_in, (1, 2, 0)).reshape(-1, sequence.shape[1])
+    key_values, query, gate = local_kernel(
+        project_body,
+        (
+            pltpu.VMEM((row_count, rows_here, LANES), BF16),
+            pltpu.VMEM((rows_here, LANES), F32),
+            pltpu.VMEM((rows_here, LANES), F32),
+        ),
+        "project",
+        sequence,
+        weights,
+    )
+    key_values_all = exchange(key_values, ROW)
+
+    bias_in = jnp.transpose(bias_weight.reshape(channels, col_count, heads_here), (2, 1, 0))
+    bias_blocks = local_kernel(
+        bias_body,
+        pltpu.VMEM((col_count, heads_here * GROUPS, LANES), F32),
+        "bias",
+        pair_state,
+        bias_in.reshape(-1, channels),
+    )
+
     one = (1 + jnp.minimum(col_index, 0)).astype(BF16)
     attention_out, outer_in, outer_out = attention_out * one, outer_in * one, outer_out * one
     triangle_out, transition_up = triangle_out * one, transition_up * one
     transition_down = transition_down * one
-    group = channels // col_count
     by_channel = jnp.transpose(triangle_in, (1, 2, 0)) * one
     grouped = by_channel[:4].reshape(2, 2, col_count, group, channels)
     gates_in = jnp.swapaxes(grouped[:, 0], 0, 1).reshape(2 * channels, channels)
     values_in = jnp.swapaxes(grouped[:, 1], 0, 1).reshape(2 * channels, channels)
     last_in = triangle_in[:, 4] * one
+    rows_of = jnp.arange(2 * group * rows_here)
+    spread_order = jax.nn.one_hot(
+        rows_of % rows_here * (2 * group) + rows_of // rows_here, 2 * group * rows_here, dtype=BF16
+    )
+    few = rows_here // I_PARTS
+    rows_of = jnp.arange(rows_here * group)
+    source = (rows_of // group // few * group + rows_of % group) * few + rows_of // group % few
+    gather_order = jnp.tile(
+        jax.nn.one_hot(source, rows_here * group, dtype=BF16), (1, K_PARTS)
+    )
+    spread_order, gather_order = spread_order * one, gather_order * one
+    whole = 1 + jnp.minimum(col_index, 0)
+    mask_row = residue_mask.reshape(1, -1) * whole
+    chain_row = chain_index.reshape(1, -1) * whole
+    head_offset = lax.dynamic_slice_in_dim(chain_bias, col_index * heads_here, heads_here, 0)
     live = residue_mask.astype(F32)
     row_live = lax.dynamic_slice_in_dim(live, row_start, rows_here, 0)
     col_live = lax.dynamic_slice_in_dim(live, col_start, cols_here, 0)
     pair_live = (row_live[:, None] * col_live[None, :]).reshape(1, pairs_here)
     (
         key_values_all,
-        bias_tile,
+        bias_blocks,
         attention_out,
         outer_in,
         outer_out,
@@ -161,10 +341,14 @@
         values_in,
         last_in,
         pair_live,
+        spread_order,
+        gather_order,
+        mask_row,
+        chain_row,
     ) = lax.optimization_barrier(
         (
             key_values_all,
-            bias_tile,
+            bias_blocks,
             attention_out,
             outer_in,
             outer_out,
@@ -175,37 +359,33 @@
             values_in,
             last_in,
             pair_live,
+            spread_order,
+            gather_order,
+            mask_row,
+            chain_row,
         )
     )
-    pair_bias = lax.all_to_all(bias_tile, "col", split_axis=0, concat_axis=2, tiled=True)
-    heads_here = pair_bias.shape[0]
-
-    width = query.shape[1]
-    head_width = width // heads_here
-    query_heads = query.reshape(rows_here, heads_here, head_width)
-    key_heads = key_values_all[:, :width].reshape(length_all, heads_here, head_width)
-    value_heads = key_values_all[:, width:].reshape(length_all, heads_here, head_width)
-    scale = 1.0 / math.sqrt(head_width)
-    scores = (
-        jnp.einsum("ihd,jhd->hij", query_heads, key_heads, preferred_element_type=F32) * scale
-    )
-    chain_rows = lax.dynamic_slice_in_dim(chain_index, row_start, rows_here, 0)
-    same_chain = (chain_rows[:, None] == chain_index[None, :]).astype(F32)
-    head_offset = lax.dynamic_slice_in_dim(chain_bias, col_index * heads_here, heads_here, 0)
-    scores = scores + pair_bias + head_offset[:, None, None] * same_chain[None]
-    positions = jnp.arange(length_all, dtype=jnp.int32)
-    query_ids = row_start + jnp.arange(rows_here, dtype=jnp.int32)
-    allowed = (residue_mask[None, :] == 1) | (query_ids[:, None] == positions[None, :])
-    allowed = allowed[None]
-    highest = jnp.max(jnp.where(allowed, scores, -jnp.inf), axis=-1, keepdims=True)
-    raised = jnp.where(allowed, jnp.exp(scores - highest), 0.0)
-    weights = (raised / jnp.sum(raised, axis=-1, keepdims=True)).astype(BF16)
-    gathered = jnp.einsum(
-        "hij,jhd->ihd", weights, value_heads, preferred_element_type=F32
-    ).reshape(rows_here, -1)
-    mixed = (gate * gathered).astype(BF16)
-    head_terms = jnp.dot(mixed, attention_out, preferred_element_type=F32).astype(BF16)
-    terms = from_everyone(head_terms, "col")
+    bias_blocks = exchange(bias_blocks, "col")
+    terms = local_kernel(
+        attention_body,
+        pltpu.VMEM((col_count, *sequence.shape), BF16),
+        "attention",
+        row_start.reshape(1),
+        head_offset,
+        bias_blocks,
+        key_values_all,
+        query,
+        gate,
+        mask_row,
+        chain_row,
+        attention_out,
+        scalars=2,
+        scratch=(
+            pltpu.VMEM((heads_here * rows_here, LANES), F32),
+            pltpu.VMEM((rows_here, LANES), F32),
+        ),
+    )
+    terms = exchange(terms, "col")
     width = outer_in.shape[1]
     sequence_out, left_twice, right_copies = local_kernel(
         settle_body,
@@ -240,16 +420,15 @@
         scalars=1,
     )
 
-    tiles = exchange(tiles, "col").reshape(K_PARTS, -1, 2, group, rows_here, cols_here)
-    panels = jnp.transpose(tiles, (2, 0, 3, 4, 1, 5)).reshape(
-        2, K_PARTS, 1, group, rows_here, length_all // K_PARTS
-    )
-    lefts = panels[0].reshape(K_PARTS, group, I_PARTS, rows_here // I_PARTS, -1)
-    lefts = jnp.swapaxes(lefts, 1, 2)
-    rights = jnp.broadcast_to(panels[1], (K_PARTS, I_PARTS, *panels.shape[3:]))
-    panels = jnp.concatenate([lefts, rights], axis=3)
-    panels = exchange(panels.reshape(row_count, -1, length_all // K_PARTS), ROW)
-    few = rows_here // I_PARTS
+    tiles = exchange(tiles, "col")
+    panels = local_kernel(
+        spread_body,
+        pltpu.VMEM((row_count, few + rows_here, length_all // K_PARTS), BF16),
+        "spread",
+        tiles,
+        spread_order,
+    )
+    panels = exchange(panels, ROW)
     product = lax.dot_general(
         panels[:, :few].reshape(-1, length_all // K_PARTS),
         panels[:, few:].reshape(-1, length_all // K_PARTS),
@@ -257,12 +436,13 @@
         preferred_element_type=F32,
     ).astype(BF16)
     product = exchange(product.reshape(row_count, few, length_all), ROW)
-    product = jnp.sum(
-        product.reshape(K_PARTS, I_PARTS, group, few, length_all).astype(F32), axis=0
-    ).astype(BF16)
-    product = jnp.transpose(
-        product.reshape(I_PARTS, group, few, col_count, cols_here), (3, 1, 0, 2, 4)
-    ).reshape(col_count, group, pairs_here)
+    product = local_kernel(
+        gather_body,
+        pltpu.VMEM((col_count, group, pairs_here), BF16),
+        "gather",
+        product,
+        gather_order,
+    )
     product = exchange(product, "col").reshape(channels, pairs_here)
 
     pair_out = local_kernel(

time: 148 us -> 144 us (0.973)
  Pallas kernels: 3.12 us -> 7.4 us
  local copies, waits for them, and re-layouts: 13.6 us -> 9.58 us
  other arithmetic: 2.92 us -> 0.37 us
    all_to_all x1 -> x0, starting transfers between devices: 7.26 us -> none  [per_device(): lax.all_to_all(bias_tile, 'col', split_axis=0, concat_axis=2, tiled=True)]
    all_to_all x1 -> x2, starting transfers between devices: 16.6 us -> 23.9 us  [exchange(): return lax.all_to_all(blocks, axis, split_axis=0, concat_axis=0, tiled=True)]
    all_to_all x1 -> x0, waiting for transfers between devices: 5.5 us -> none  [per_device(): lax.all_to_all(bias_tile, 'col', split_axis=0, concat_axis=2, tiled=True)]
    all_to_all x1 -> x2, waiting for transfers between devices: 3.46 us -> 8.1 us  [exchange(): return lax.all_to_all(blocks, axis, split_axis=0, concat_axis=0, tiled=True)]
    pallas_call x3 -> x8, Pallas kernels: 3.12 us -> 7.4 us  [local_kernel(): pl.pallas_call(body, out_shape=out_shape, in_specs=[pl.BlockSpec(memory_s...]
    reshape x6 -> x1, local copies, waits for them, and re-layouts: 2.71 us -> 0.01 us  [per_device(): bias_weight.reshape(channels, col_count, heads_here)]
    reduce_sum x5 -> x0, other arithmetic: 1.57 us -> none  [the longest x2 1.08 us: layer_norm(): center = values - jnp.mean(values, axis=axis, keepdims=True)]
    unnamed x31 -> x32, local copies, waits for them, and re-layouts: 7.35 us -> 8.58 us
  transfers between devices with their start and end apart: 2 -> 2, of which waited for: 2 -> 2; matrix products, arithmetic and copies ran while one was open for 1% -> 1% of each run, Pallas kernels for 0% -> 1%
where the time goes in v4:
time: 144 us; the launch traced here: 143 us
  blocking collectives  92.6 us (64%)
  starting transfers between devices  23.9 us (17%)
  local copies, waits for them, and re-layouts  9.58 us (7%)
  waiting for transfers between devices  8.1 us (6%)
  Pallas kernels  7.4 us (5%)
    all_to_all x6, blocking collectives, exchange(): return lax.all_to_all(blocks, axis, split_axis=0, concat_axis=0, tiled=True)  92.6 us
    all_to_all x2, starting transfers between devices, exchange(): return lax.all_to_all(blocks, axis, split_axis=0, concat_axis=0, tiled=True)  23.9 us
    unnamed x32, local copies, waits for them, and re-layouts  8.58 us
    all_to_all x2, waiting for transfers between devices, exchange(): return lax.all_to_all(blocks, axis, split_axis=0, concat_axis=0, tiled=True)  8.1 us
    pallas_call x8, Pallas kernels, local_kernel(): pl.pallas_call(body, out_shape=out_shape, in_specs=[pl.BlockSpec(memory_s...  7.4 us
  transfers between devices with their start and end apart: 2, of which 2 were waited for; matrix products, arithmetic and copies ran while one was open for 1% of the time, Pallas kernels for 1%

profile of v4, /device:TPU:1, one launch (start us, length us, event | category | flops | bytes accessed | tf_op | source)
XLA Modules:
  0.0 143.1 jit_solution(6122082319832185147)
XLA Ops:
  0.6 0.0 copy-start
  0.6 1.0 copy-done
  1.7 0.0 copy-start.2
  1.7 0.8 copy-done.2
  2.4 1.1 project.1
  3.5 0.0 copy-start.5
  3.5 16.6 %all-to-all-start = ((bf16[32,16,128]{2,1,0:T(8,128)(2,1)}), bf16[32,16,128]{2,1,0:T(8,128)(2,1)S(1)}, u32[]{:S(2)}, u32[]{:S(2)}) async-start(bf16[32,16,128]{2,1,0:T(8,128)(2,1)} %get-tuple-element.27), calls=%async_computation | async-start | bytes 262144 | tf_op jit(solution)/shard_map/all_to_all | solution.py:21
  20.2 0.0 copy-start.12
  20.2 0.7 copy-done.12
  20.9 0.1 dynamic_slice.11
  21.0 0.1 dynamic_slice.10
  21.0 0.0 copy-done.5
  21.0 0.2 copy.20
  21.2 0.0 copy-start.6
  21.2 0.1 fusion.2
  21.3 0.1 fusion.1.order
  21.4 0.7 copy-done.6
  22.1 0.0 copy-start.7
  22.1 0.9 copy-done.7
  23.0 0.0 copy-start.8
  23.0 0.9 copy-done.8
  24.0 0.0 copy-start.9
  24.0 0.0 copy-start.10
  24.0 0.1 broadcast_multiply_fusion.6
  24.1 0.6 copy-done.9
  24.8 0.0 copy-done.10
  24.8 0.0 copy-start.13
  24.8 0.7 copy-done.13
  25.5 0.0 copy-start.11
  25.5 0.1 mul.164.live
  25.5 0.6 copy-done.11
  26.2 0.0 copy-start.1
  26.2 0.0 copy-start.4
  26.3 0.8 copy-done.1
  27.1 1.0 bias.1
  28.1 0.0 copy-done.4
  28.2 3.6 %all-to-all-done.key_values = bf16[32,16,128]{2,1,0:T(8,128)(2,1)S(1)} async-done(((bf16[32,16,128]{2,1,0:T(8,128)(2,1)}), bf16[32,16,128]{2,1,0:T(8,128)(2,1)S(1)}, u32[]{:S(2)}, u32[]{:S(2)}) %all-to-all-start) | async-done | bytes 131104 | tf_op jit(solution)/shard_map/all_to_all | solution.py:21
  31.8 7.3 %all-to-all-start.1 = ((f32[16,8,128]{2,1,0:T(8,128)}), f32[16,8,128]{2,1,0:T(8,128)S(1)}, u32[]{:S(2)}, u32[]{:S(2)}) async-start(f32[16,8,128]{2,1,0:T(8,128)} %bias.1), calls=%async_computation.1 | async-start | bytes 131072 | tf_op jit(solution)/shard_map/all_to_all | solution.py:21
  39.0 0.0 copy-start.14
  39.0 0.6 copy-done.14
  39.7 0.7 dynamic_slice.9.offsets
  40.3 4.5 %all-to-all-done.1.blocks = f32[16,8,128]{2,1,0:T(8,128)S(1)} async-done(((f32[16,8,128]{2,1,0:T(8,128)}), f32[16,8,128]{2,1,0:T(8,128)S(1)}, u32[]{:S(2)}, u32[]{:S(2)}) %all-to-all-start.1) | async-done | bytes 65568 | tf_op jit(solution)/shard_map/all_to_all | solution.py:21
  44.8 1.4 attention.1
  46.2 0.0 copy-start.3
  46.2 12.6 %all_to_all.40.terms = bf16[16,16,1024]{2,1,0:T(8,128)(2,1)S(1)} all-to-all(bf16[16,16,1024]{2,1,0:T(8,128)(2,1)S(1)} %attention.1), channel_id=1, replica_groups=mesh['row_0'=4,'row_1'=8,'col'=16] {'col'}, dimensions={0} | all-to-all | bytes 1048576 | tf_op jit(solution)/shard_map/all_to_all | solution.py:21
  58.9 0.0 copy-done.3
  58.9 0.7 settle.1
  59.6 18.4 %all_to_all.41.rights = bf16[32,8,128]{2,1,0:T(8,128)(2,1)S(1)} all-to-all(bf16[32,8,128]{2,1,0:T(8,128)(2,1)S(1)} %get-tuple-element.37), channel_id=1, replica_groups=mesh['row_0'=4,'row_1'=8,'col'=16] {'row_0','row_1'}, dimensions={0} | all-to-all | bytes 131072 | tf_op jit(solution)/shard_map/all_to_all | solution.py:21
  78.0 0.8 pair.4
  78.8 12.3 %all_to_all.42.tiles = bf16[16,16,512]{2,1,0:T(8,128)(2,1)S(1)} all-to-all(bf16[16,16,512]{2,1,0:T(8,128)(2,1)S(1)} %get-tuple-element.44), channel_id=1, replica_groups=mesh['row_0'=4,'row_1'=8,'col'=16] {'col'}, dimensions={0} | all-to-all | bytes 524288 | tf_op jit(solution)/shard_map/all_to_all | solution.py:21
  91.0 0.5 spread.1
  91.5 17.7 %all_to_all.43 = bf16[32,24,256]{2,1,0:T(8,128)(2,1)S(1)} all-to-all(bf16[32,24,256]{2,1,0:T(8,128)(2,1)S(1)} %spread.1), channel_id=1, replica_groups=mesh['row_0'=4,'row_1'=8,'col'=16] {'row_0','row_1'}, dimensions={0} | all-to-all | bytes 786432 | tf_op jit(solution)/shard_map/all_to_all | solution.py:21
  109.2 0.3 fusion
  109.5 18.6 %all_to_all.44.parts = bf16[32,8,512]{2,1,0:T(8,128)(2,1)S(1)} all-to-all(bf16[32,8,512]{2,1,0:T(8,128)(2,1)S(1)} %fusion), channel_id=1, replica_groups=mesh['row_0'=4,'row_1'=8,'col'=16] {'row_0','row_1'}, dimensions={0} | all-to-all | bytes 524288 | tf_op jit(solution)/shard_map/all_to_all | solution.py:21
  128.1 0.3 gather.1
  128.4 13.0 %all_to_all.45 = bf16[16,8,512]{2,1,0:T(8,128)(2,1)S(1)} all-to-all(bf16[16,8,512]{2,1,0:T(8,128)(2,1)S(1)} %gather.1), channel_id=1, replica_groups=mesh['row_0'=4,'row_1'=8,'col'=16] {'col'}, dimensions={0} | all-to-all | bytes 262144 | tf_op jit(solution)/shard_map/all_to_all | solution.py:21
  141.4 1.6 %tail.1 = bf16[512,128]{1,0:T(8,128)(2,1)} custom-call(bf16[128,512]{1,0:T(8,128)(2,1)S(1)} %bitcast.39, f32[512,128]{1,0:T(8,128)S(1)} %get-tuple-element.47.mid, f32[512,128]{1,0:T(8,128)S(1)} %get-tuple-element.48.out_gate, bf16[128,128]{1,0:T(8,128)(2,1)S(1)} %get-tuple-element.49.triangle_out, ...), custom_call_target="tpu_custom_call" | custom-call | tf_op jit(solution)/shard_map/tail/pallas_call | solution.py:41
  (19 shorter events, 0.2 us)
Async XLA Ops:
  0.6 1.0 copy-start
  1.7 0.8 copy-start.2
  3.5 17.5 %copy-start.5 = (bf16[128,5,128]{2,0,1:T(8,128)(2,1)S(1)}, bf16[128,5,128]{2,0,1:T(8,128)(2,1)}, u32[]{:S(2)}) copy-start(bf16[128,5,128]{2,0,1:T(8,128)(2,1)} %param.24) | copy-start | bytes 491524
  3.5 28.2 %all-to-all-start = ((bf16[32,16,128]{2,1,0:T(8,128)(2,1)}), bf16[32,16,128]{2,1,0:T(8,128)(2,1)S(1)}, u32[]{:S(2)}, u32[]{:S(2)}) async-start(bf16[32,16,128]{2,1,0:T(8,128)(2,1)} %get-tuple-element.27), calls=%async_computation | async-start | bytes 262144 | tf_op jit(solution)/shard_map/all_to_all | solution.py:21
  20.2 0.7 copy-start.12
  21.2 0.9 copy-start.6
  22.1 0.9 copy-start.7
  23.0 0.9 copy-start.8
  24.0 0.8 copy-start.9
  24.0 0.8 copy-start.10
  24.8 0.7 copy-start.13
  25.5 0.7 copy-start.11
  26.2 0.9 copy-start.1
  26.2 1.9 %copy-start.4 = (bf16[1024,128]{1,0:T(8,128)(2,1)S(1)}, bf16[1024,128]{1,0:T(8,128)(2,1)}, u32[]{:S(2)}) copy-start(bf16[1024,128]{1,0:T(8,128)(2,1)} %param.22) | copy-start | bytes 786436
  31.8 13.1 %all-to-all-start.1 = ((f32[16,8,128]{2,1,0:T(8,128)}), f32[16,8,128]{2,1,0:T(8,128)S(1)}, u32[]{:S(2)}, u32[]{:S(2)}) async-start(f32[16,8,128]{2,1,0:T(8,128)} %bias.1), calls=%async_computation.1 | async-start | bytes 131072 | tf_op jit(solution)/shard_map/all_to_all | solution.py:21
  39.0 0.7 copy-start.14
  46.2 12.6 %copy-start.3 = (bf16[16,1024]{1,0:T(8,128)(2,1)S(1)}, bf16[16,1024]{1,0:T(8,128)(2,1)}, u32[]{:S(2)}) copy-start(bf16[16,1024]{1,0:T(8,128)(2,1)} %sequence.3) | copy-start | bytes 98308

commit v5 on v4

--- a/solution.py
+++ b/solution.py
@@ -13,6 +13,17 @@
 F32 = jnp.float32
 K_PARTS = 2
 I_PARTS = 2
+KEPT = (
+    "pair",
+    "mask",
+    "chain",
+    "attention_out",
+    "outer_in",
+    "outer_out",
+    "triangle_out",
+    "transition_up",
+    "transition_down",
+)
 LANES = 128
 GROUPS = 4
 
@@ -32,20 +43,32 @@
     return center * lax.rsqrt(spread + 1e-05)
 
 
-def local_kernel(body, out_shape, name, *operands, scalars=0, scratch=()):
-    spaces = [pltpu.SMEM if k < scalars else pltpu.VMEM for k in range(len(operands))]
+def local_kernel(body, out_shape, name, *operands, scalars=0, scratch=(), far=False, out_space=None):
+    space = pltpu.HBM if far else pltpu.VMEM
+    spaces = [pltpu.SMEM if k < scalars else space for k in range(len(operands))]
     held = [
-        x if space is pltpu.SMEM else pltpu.with_memory_space_constraint(x, space)
+        pltpu.with_memory_space_constraint(x, space) if space is pltpu.VMEM else x
         for x, space in zip(operands, spaces)
     ]
+    out_space = out_space or pltpu.VMEM
     return pl.pallas_call(
         body,
         out_shape=out_shape,
         in_specs=[pl.BlockSpec(memory_space=space) for space in spaces],
-        out_specs=jax.tree.map(lambda _: pl.BlockSpec(memory_space=pltpu.VMEM), out_shape),
+        out_specs=jax.tree.map(lambda _: pl.BlockSpec(memory_space=out_space), out_shape),
         scratch_shapes=scratch,
         name=name,
     )(*held)
+
+
+def fetch(sources, targets, arrived):
+    copies = [
+        pltpu.make_async_copy(source, target, arrived.at[k])
+        for k, (source, target) in enumerate(zip(sources, targets))
+    ]
+    for copy in copies:
+        copy.start()
+    return copies
 
 
 def mm(a, b, over_a, over_b):
@@ -65,9 +88,12 @@
     return tile
 
 
-def project_body(sequence, weights, key_values, query, gate):
-    normed = layer_norm(sequence[...].astype(F32)).astype(BF16)
-    projected = mm(normed, weights[...], 1, 1)
+def project_body(sequence, weights, key_values, query, gate, near, held, arrived):
+    first_copy, second_copy = fetch((sequence, weights), (near, held), arrived)
+    first_copy.wait()
+    normed = layer_norm(near[...].astype(F32)).astype(BF16)
+    second_copy.wait()
+    projected = mm(normed, held[...], 1, 1)
     rows = projected.shape[0]
     head, rest = projected[:, :LANES], projected[:, LANES:]
     first = lax.broadcasted_iota(jnp.int32, (rows, LANES), 1) < LANES // 2
@@ -77,21 +103,65 @@
     gate[...] = jnp.where(first, 0.0, jax.nn.sigmoid(rest))
 
 
-def bias_body(pair, bias_in, blocks):
-    rows, cols, channels = pair.shape
-    wide = pair[...].astype(F32)
+def prepare_body(row_start, col_start, *refs):
+    count = len(KEPT)
+    sources, targets = refs[: count + 2], refs[count + 2 : 2 * count + 2]
+    blocks, gates_in, values_in, last_in, live, spread_order, gather_order = refs[2 * count + 2 : -4]
+    bias_near, triangle_near, turned_bias, arrived = refs[-4:]
+    copies = fetch(sources, (*targets, bias_near, triangle_near), arrived)
+    near = dict(zip(KEPT, targets))
+    landed = dict(zip((*KEPT, "bias_in", "triangle"), copies))
+
+    size = spread_order.shape[0]
+    n = lax.broadcasted_iota(jnp.int32, spread_order.shape, 0)
+    m = lax.broadcasted_iota(jnp.int32, spread_order.shape, 1)
+    rows = live.shape[1] // (LANES // GROUPS)
+    wanted = n % rows * (size // rows) + n // rows
+    spread_order[...] = jnp.where(m == wanted, 1.0, 0.0).astype(BF16)
+    size = gather_order.shape[0]
+    group, few = size // rows, rows // I_PARTS
+    n = lax.broadcasted_iota(jnp.int32, gather_order.shape, 0)
+    m = lax.broadcasted_iota(jnp.int32, gather_order.shape, 1)
+    i, c = n // group, n % group
+    wanted = (i // few * group + c) * few + i % few
+    gather_order[...] = jnp.where(m % size == wanted, 1.0, 0.0).astype(BF16)
+
+    landed["pair"].wait()
+    landed["bias_in"].wait()
+    wide = near["pair"][...].astype(F32)
     turned = jnp.concatenate([wide[GROUPS * (p % GROUPS) + p // GROUPS] for p in range(rows)], axis=0)
     normed = layer_norm(turned).astype(BF16)
-    bias = mm(bias_in[...], normed, 1, 1)
-    count = blocks.shape[0]
-    for h in range(2):
-        for t in range(GROUPS):
-            part = bias[h * count : (h + 1) * count, t * LANES : (t + 1) * LANES]
-            blocks[:, h * GROUPS + t, :] = part
+    bias = mm(bias_near[...], normed, 1, 1)
+    columns = blocks.shape[0]
+    for t in range(GROUPS):
+        turned_bias[t] = bias[:, t * LANES : (t + 1) * LANES]
+        for h in range(2):
+            blocks[:, h * GROUPS + t, :] = turned_bias[t, pl.ds(h, columns, stride=2), :]
+
+    landed["mask"].wait()
+    mask = near["mask"][...].astype(F32).astype(BF16)
+    length = mask.shape[1]
+    residue = lax.broadcasted_iota(jnp.int32, (length, live.shape[1]), 0)
+    pair = lax.broadcasted_iota(jnp.int32, (length, live.shape[1]), 1)
+    of_row = jnp.where(residue == row_start[0] + pair // (LANES // GROUPS), 1.0, 0.0).astype(BF16)
+    of_col = jnp.where(residue == col_start[0] + pair % (LANES // GROUPS), 1.0, 0.0).astype(BF16)
+    mask = jnp.broadcast_to(mask, (8, length))
+    live[...] = (mm(mask, of_row, 1, 0) * mm(mask, of_col, 1, 0))[:1]
+
+    landed["triangle"].wait()
+    half = gates_in.shape[1] // 2
+    for k, target in enumerate((gates_in, values_in, gates_in, values_in)):
+        side = half * (k // 2)
+        across = jnp.transpose(triangle_near[k].astype(F32)).astype(BF16)
+        target[:, side : side + half, :] = across.reshape(target.shape[0], half, LANES)
+    last_in[...] = triangle_near[4]
+    for name in KEPT:
+        if name not in ("pair", "mask"):
+            landed[name].wait()
 
 
 def attention_body(
-    start, offsets, blocks, key_values, query, gate, mask, chain, attention_out, copies, spread, joined
+    start, col, offsets, blocks, key_values, query, gate, mask, chain, attention_out, copies, spread, joined
 ):
     count, eight, _ = blocks.shape
     four = eight // 2
@@ -110,7 +180,7 @@
     row = lax.broadcasted_iota(jnp.int32, (eight, length), 0)
     chains = jnp.broadcast_to(chain[...], (eight, length))
     kept = jnp.broadcast_to(mask[...], (eight, length)) == 1
-    offset = jnp.where(row < four, offsets[0], offsets[1])
+    offset = jnp.where(row < four, offsets[2 * col[0]], offsets[2 * col[0] + 1])
     weights = []
     for g in range(GROUPS):
         pieces = []
@@ -214,10 +284,10 @@
     right_copies[...] = jnp.broadcast_to(packed.astype(BF16)[None], right_copies.shape)
 
 
-def pair_body(start, rights, left_twice, pair, outer_out, gates_in, values_in, last_in, live, tiles, mid, out_gate):
+def pair_body(col, rights, left_twice, pair, outer_out, gates_in, values_in, last_in, live, tiles, mid, out_gate):
     rows, cols, channels = pair.shape
     half = channels // 2
-    taken = rights[pl.ds(start[0], cols // rows)].astype(F32)
+    taken = rights[pl.ds(col[0] * (cols // rows), cols // rows)].astype(F32)
     first = lax.broadcasted_iota(jnp.int32, (rows // 2, channels), 1) < half
     pieces = []
     for k in range(cols // rows):
@@ -233,19 +303,28 @@
     pair_mid = pair[...].astype(F32).reshape(rows * cols, channels) + mm(feat, outer_out[...], 1, 0)
     mid[...] = pair_mid
     normed = layer_norm(pair_mid).astype(BF16)
-    opened = jax.nn.sigmoid(mm(gates_in[...], normed, 1, 1))
-    operands = opened * mm(values_in[...], normed, 1, 1) * live[...]
+    flat = (-1, channels)
+    opened = jax.nn.sigmoid(mm(gates_in[...].reshape(flat), normed, 1, 1))
+    operands = opened * mm(values_in[...].reshape(flat), normed, 1, 1) * live[...]
     tiles[...] = operands.astype(BF16).reshape(tiles.shape)
     out_gate[...] = jax.nn.sigmoid(mm(normed, last_in[...], 1, 0))
 
 
-def tail_body(product, mid, out_gate, triangle_out, transition_up, transition_down, out):
-    normed_product = layer_norm(product[...].astype(F32), axis=0)
-    normed_product = jnp.transpose(normed_product).astype(BF16)
-    late = mid[...] + out_gate[...] * mm(normed_product, triangle_out[...], 1, 0)
-    normed_late = layer_norm(late).astype(BF16)
-    hidden = jnp.maximum(mm(normed_late, transition_up[...], 1, 0), 0.0).astype(BF16)
-    out[...] = (late + mm(hidden, transition_down[...], 1, 0)).astype(BF16)
+def tail_body(product, mid, out_gate, triangle_out, transition_up, transition_down, out, held, left):
+    pairs = mid.shape[0]
+    copies = []
+    for k in range(pairs // LANES):
+        here = pl.ds(k * LANES, LANES)
+        normed_product = layer_norm(product[:, here].astype(F32), axis=0)
+        normed_product = jnp.transpose(normed_product).astype(BF16)
+        late = mid[here] + out_gate[here] * mm(normed_product, triangle_out[...], 1, 0)
+        normed_late = layer_norm(late).astype(BF16)
+        hidden = jnp.maximum(mm(normed_late, transition_up[...], 1, 0), 0.0).astype(BF16)
+        held[here] = (late + mm(hidden, transition_down[...], 1, 0)).astype(BF16)
+        copies.append(pltpu.make_async_copy(held.at[here], out.at[here], left.at[k]))
+        copies[-1].start()
+    for copy in copies:
+        copy.wait()
 
 
 def per_device(
@@ -278,108 +357,83 @@
     heads_here = bias_weight.shape[1] // col_count
 
     weights = jnp.transpose(attention_in, (1, 2, 0)).reshape(-1, sequence.shape[1])
-    key_values, query, gate = local_kernel(
+    key_values, query, gate, sequence_near = local_kernel(
         project_body,
         (
             pltpu.VMEM((row_count, rows_here, LANES), BF16),
             pltpu.VMEM((rows_here, LANES), F32),
             pltpu.VMEM((rows_here, LANES), F32),
+            pltpu.VMEM(sequence.shape, BF16),
         ),
         "project",
         sequence,
         weights,
+        scratch=(pltpu.VMEM(weights.shape, BF16), pltpu.SemaphoreType.DMA((2,))),
+        far=True,
     )
     key_values_all = exchange(key_values, ROW)
 
-    bias_in = jnp.transpose(bias_weight.reshape(channels, col_count, heads_here), (2, 1, 0))
-    bias_blocks = local_kernel(
-        bias_body,
-        pltpu.VMEM((col_count, heads_here * GROUPS, LANES), F32),
-        "bias",
-        pair_state,
-        bias_in.reshape(-1, channels),
-    )
-
-    one = (1 + jnp.minimum(col_index, 0)).astype(BF16)
-    attention_out, outer_in, outer_out = attention_out * one, outer_in * one, outer_out * one
-    triangle_out, transition_up = triangle_out * one, transition_up * one
-    transition_down = transition_down * one
-    by_channel = jnp.transpose(triangle_in, (1, 2, 0)) * one
-    grouped = by_channel[:4].reshape(2, 2, col_count, group, channels)
-    gates_in = jnp.swapaxes(grouped[:, 0], 0, 1).reshape(2 * channels, channels)
-    values_in = jnp.swapaxes(grouped[:, 1], 0, 1).reshape(2 * channels, channels)
-    last_in = triangle_in[:, 4] * one
-    rows_of = jnp.arange(2 * group * rows_here)
-    spread_order = jax.nn.one_hot(
-        rows_of % rows_here * (2 * group) + rows_of // rows_here, 2 * group * rows_here, dtype=BF16
+    bias_in = jnp.transpose(bias_weight)
+    triangle = jnp.transpose(triangle_in, (1, 0, 2))
+    kept = dict(
+        pair=pair_state,
+        mask=residue_mask.reshape(1, -1),
+        chain=chain_index.reshape(1, -1),
+        attention_out=attention_out,
+        outer_in=outer_in,
+        outer_out=outer_out,
+        triangle_out=triangle_out,
+        transition_up=transition_up,
+        transition_down=transition_down,
     )
     few = rows_here // I_PARTS
-    rows_of = jnp.arange(rows_here * group)
-    source = (rows_of // group // few * group + rows_of % group) * few + rows_of // group % few
-    gather_order = jnp.tile(
-        jax.nn.one_hot(source, rows_here * group, dtype=BF16), (1, K_PARTS)
-    )
-    spread_order, gather_order = spread_order * one, gather_order * one
-    whole = 1 + jnp.minimum(col_index, 0)
-    mask_row = residue_mask.reshape(1, -1) * whole
-    chain_row = chain_index.reshape(1, -1) * whole
-    head_offset = lax.dynamic_slice_in_dim(chain_bias, col_index * heads_here, heads_here, 0)
-    live = residue_mask.astype(F32)
-    row_live = lax.dynamic_slice_in_dim(live, row_start, rows_here, 0)
-    col_live = lax.dynamic_slice_in_dim(live, col_start, cols_here, 0)
-    pair_live = (row_live[:, None] * col_live[None, :]).reshape(1, pairs_here)
-    (
-        key_values_all,
-        bias_blocks,
-        attention_out,
-        outer_in,
-        outer_out,
-        triangle_out,
-        transition_up,
-        transition_down,
-        gates_in,
-        values_in,
-        last_in,
-        pair_live,
-        spread_order,
-        gather_order,
-        mask_row,
-        chain_row,
-    ) = lax.optimization_barrier(
+    near = local_kernel(
+        prepare_body,
         (
-            key_values_all,
-            bias_blocks,
-            attention_out,
-            outer_in,
-            outer_out,
-            triangle_out,
-            transition_up,
-            transition_down,
-            gates_in,
-            values_in,
-            last_in,
-            pair_live,
-            spread_order,
-            gather_order,
-            mask_row,
-            chain_row,
-        )
-    )
+            *[pltpu.VMEM(kept[k].shape, kept[k].dtype) for k in KEPT],
+            pltpu.VMEM((col_count, heads_here * GROUPS, LANES), F32),
+            pltpu.VMEM((col_count, 2 * group, channels), BF16),
+            pltpu.VMEM((col_count, 2 * group, channels), BF16),
+            pltpu.VMEM((channels, channels), BF16),
+            pltpu.VMEM((1, pairs_here), F32),
+            pltpu.VMEM((2 * group * rows_here,) * 2, BF16),
+            pltpu.VMEM((group * rows_here, K_PARTS * group * rows_here), BF16),
+        ),
+        "prepare",
+        row_start.reshape(1),
+        col_start.reshape(1),
+        *[kept[k] for k in KEPT],
+        bias_in,
+        triangle,
+        scalars=2,
+        scratch=(
+            pltpu.VMEM(bias_in.shape, BF16),
+            pltpu.VMEM(triangle.shape, BF16),
+            pltpu.VMEM((GROUPS, bias_in.shape[0], LANES), F32),
+            pltpu.SemaphoreType.DMA((len(KEPT) + 2,)),
+        ),
+        far=True,
+    )
+    near, made = dict(zip(KEPT, near)), near[len(KEPT) :]
+    bias_blocks, gates_in, values_in, last_in, pair_live, spread_order, gather_order = made
+
+    key_values_all, bias_blocks = lax.optimization_barrier((key_values_all, bias_blocks))
     bias_blocks = exchange(bias_blocks, "col")
     terms = local_kernel(
         attention_body,
         pltpu.VMEM((col_count, *sequence.shape), BF16),
         "attention",
         row_start.reshape(1),
-        head_offset,
+        col_index.reshape(1),
+        chain_bias,
         bias_blocks,
         key_values_all,
         query,
         gate,
-        mask_row,
-        chain_row,
-        attention_out,
-        scalars=2,
+        near["mask"],
+        near["chain"],
+        near["attention_out"],
+        scalars=3,
         scratch=(
             pltpu.VMEM((heads_here * rows_here, LANES), F32),
             pltpu.VMEM((rows_here, LANES), F32),
@@ -396,8 +450,8 @@
         ),
         "settle",
         terms,
-        sequence,
-        outer_in,
+        sequence_near,
+        near["outer_in"],
     )
     rights = exchange(right_copies, ROW)
     tiles, pair_mid, out_gate = local_kernel(
@@ -408,11 +462,11 @@
             pltpu.VMEM((pairs_here, channels), F32),
         ),
         "pair",
-        (col_index * (cols_here // rows_here)).reshape(1),
+        col_index.reshape(1),
         rights,
         left_twice,
-        pair_state,
-        outer_out,
+        near["pair"],
+        near["outer_out"],
         gates_in,
         values_in,
         last_in,
@@ -452,9 +506,14 @@
         product,
         pair_mid,
         out_gate,
-        triangle_out,
-        transition_up,
-        transition_down,
+        near["triangle_out"],
+        near["transition_up"],
+        near["transition_down"],
+        scratch=(
+            pltpu.VMEM((pairs_here, channels), BF16),
+            pltpu.SemaphoreType.DMA((pairs_here // LANES,)),
+        ),
+        out_space=pltpu.HBM,
     ).reshape(rows_here, cols_here, channels)
     return (sequence_out, pair_out)
 

time: 144 us -> 139 us (0.965)
  local copies, waits for them, and re-layouts: 9.58 us -> 0.02 us
  blocking collectives: 92.6 us -> 101 us
  starting transfers between devices: 23.9 us -> 16.5 us
  Pallas kernels: 7.4 us -> 10.4 us
  waiting for transfers between devices: 8.1 us -> 9.64 us
    unnamed x32 -> x0, local copies, waits for them, and re-layouts: 8.58 us -> none
    all_to_all x6 -> x7, blocking collectives: 92.6 us -> 101 us  [exchange(): return lax.all_to_all(blocks, axis, split_axis=0, concat_axis=0, tiled=True)]
    all_to_all x2 -> x1, starting transfers between devices: 23.9 us -> 16.5 us  [exchange(): return lax.all_to_all(blocks, axis, split_axis=0, concat_axis=0, tiled=True)]
    pallas_call x8, Pallas kernels: 7.4 us -> 10.4 us  [local_kernel(): pl.pallas_call(body, out_shape=out_shape, in_specs=[pl.BlockSpec(memory_s...]
    all_to_all x2 -> x1, waiting for transfers between devices: 8.1 us -> 9.64 us  [exchange(): return lax.all_to_all(blocks, axis, split_axis=0, concat_axis=0, tiled=True)]
  transfers between devices with their start and end apart: 2 -> 1, of which waited for: 2 -> 1; matrix products, arithmetic and copies ran while one was open for 1% -> 0% of each run, Pallas kernels for 1% -> 1%
where the time goes in v5:
time: 139 us
  blocking collectives  101 us (73%)
  starting transfers between devices  16.5 us (12%)
  Pallas kernels  10.4 us (7%)
  waiting for transfers between devices  9.64 us (7%)
    all_to_all x7, blocking collectives, exchange(): return lax.all_to_all(blocks, axis, split_axis=0, concat_axis=0, tiled=True)  101 us
    all_to_all x1, starting transfers between devices, exchange(): return lax.all_to_all(blocks, axis, split_axis=0, concat_axis=0, tiled=True)  16.5 us
    pallas_call x8, Pallas kernels, local_kernel(): pl.pallas_call(body, out_shape=out_shape, in_specs=[pl.BlockSpec(memory_s...  10.4 us
    all_to_all x1, waiting for transfers between devices, exchange(): return lax.all_to_all(blocks, axis, split_axis=0, concat_axis=0, tiled=True)  9.64 us
  transfers between devices with their start and end apart: 1, of which 1 were waited for; matrix products, arithmetic and copies ran while one was open for 0% of the time, Pallas kernels for 1%

profile of v5, /device:TPU:1, one launch (start us, length us, event | category | flops | bytes accessed | tf_op | source)
XLA Modules:
  0.0 138.6 jit_solution(18265848919118821676)
XLA Ops:
  0.6 2.1 %project.1 = (bf16[32,16,128]{2,1,0:T(8,128)(2,1)}, f32[16,128]{1,0:T(8,128)S(1)}, f32[16,128]{1,0:T(8,128)S(1)}, bf16[16,1024]{1,0:T(8,128)(2,1)S(1)}) custom-call(bf16[16,1024]{1,0:T(8,128)(2,1)} %sequence.1, bf16[256,1024]{1,0:T(8,128)(2,1)} %bitcast.21), custom_call_target="tpu_custom_call" | custom-call | tf_op jit(solution)/shard_map/project/pallas_call | solution.py:54
  2.7 16.5 %all-to-all-start = ((bf16[32,16,128]{2,1,0:T(8,128)(2,1)}), bf16[32,16,128]{2,1,0:T(8,128)(2,1)S(1)}, u32[]{:S(2)}, u32[]{:S(2)}) async-start(bf16[32,16,128]{2,1,0:T(8,128)(2,1)} %get-tuple-element.30), calls=%async_computation | async-start | bytes 262144 | tf_op jit(solution)/shard_map/all_to_all | solution.py:32
  19.2 1.9 %prepare.1 = (bf16[16,32,128]{2,1,0:T(8,128)(2,1)S(1)}, s32[1,512]{1,0:T(1,128)S(1)}, s32[1,512]{1,0:T(1,128)S(1)}, bf16[64,1024]{1,0:T(8,128)(2,1)S(1)}, bf16[1...) custom-call(s32[1]{0:T(128)} %bitcast.row_start.start, ...), custom_call_target="tpu_custom_call" | custom-call | tf_op jit(solution)/shard_map/prepare/pallas_call | solution.py:54
  21.2 9.6 %all-to-all-done.key_values = bf16[32,16,128]{2,1,0:T(8,128)(2,1)S(1)} async-done(((bf16[32,16,128]{2,1,0:T(8,128)(2,1)}), bf16[32,16,128]{2,1,0:T(8,128)(2,1)S(1)}, u32[]{:S(2)}, u32[]{:S(2)}) %all-to-all-start) | async-done | bytes 131104 | tf_op jit(solution)/shard_map/all_to_all | solution.py:32
  30.8 12.9 %all_to_all.40.blocks = f32[16,8,128]{2,1,0:T(8,128)S(1)} all-to-all(f32[16,8,128]{2,1,0:T(8,128)S(1)} %get-tuple-element.32), channel_id=1, replica_groups=mesh['row_0'=4,'row_1'=8,'col'=16] {'col'}, dimensions={0} | all-to-all | bytes 131072 | tf_op jit(solution)/shard_map/all_to_all | solution.py:32
  43.7 1.4 attention.1
  45.1 12.6 %all_to_all.41.terms = bf16[16,16,1024]{2,1,0:T(8,128)(2,1)S(1)} all-to-all(bf16[16,16,1024]{2,1,0:T(8,128)(2,1)S(1)} %attention.1), channel_id=1, replica_groups=mesh['row_0'=4,'row_1'=8,'col'=16] {'col'}, dimensions={0} | all-to-all | bytes 1048576 | tf_op jit(solution)/shard_map/all_to_all | solution.py:32
  57.7 0.7 settle.1
  58.4 14.2 %all_to_all.42.rights = bf16[32,8,128]{2,1,0:T(8,128)(2,1)S(1)} all-to-all(bf16[32,8,128]{2,1,0:T(8,128)(2,1)S(1)} %get-tuple-element.42), channel_id=1, replica_groups=mesh['row_0'=4,'row_1'=8,'col'=16] {'row_0','row_1'}, dimensions={0} | all-to-all | bytes 131072 | tf_op jit(solution)/shard_map/all_to_all | solution.py:32
  72.6 0.8 pair.1
  73.4 12.1 %all_to_all.43.tiles = bf16[16,16,512]{2,1,0:T(8,128)(2,1)S(1)} all-to-all(bf16[16,16,512]{2,1,0:T(8,128)(2,1)S(1)} %get-tuple-element.50), channel_id=1, replica_groups=mesh['row_0'=4,'row_1'=8,'col'=16] {'col'}, dimensions={0} | all-to-all | bytes 524288 | tf_op jit(solution)/shard_map/all_to_all | solution.py:32
  85.5 0.5 spread.1
  86.0 17.7 %all_to_all.44 = bf16[32,24,256]{2,1,0:T(8,128)(2,1)S(1)} all-to-all(bf16[32,24,256]{2,1,0:T(8,128)(2,1)S(1)} %spread.1), channel_id=1, replica_groups=mesh['row_0'=4,'row_1'=8,'col'=16] {'row_0','row_1'}, dimensions={0} | all-to-all | bytes 786432 | tf_op jit(solution)/shard_map/all_to_all | solution.py:32
  103.7 0.3 fusion
  104.0 18.6 %all_to_all.45.parts = bf16[32,8,512]{2,1,0:T(8,128)(2,1)S(1)} all-to-all(bf16[32,8,512]{2,1,0:T(8,128)(2,1)S(1)} %fusion), channel_id=1, replica_groups=mesh['row_0'=4,'row_1'=8,'col'=16] {'row_0','row_1'}, dimensions={0} | all-to-all | bytes 524288 | tf_op jit(solution)/shard_map/all_to_all | solution.py:32
  122.6 0.3 gather.1
  122.9 13.0 %all_to_all.46 = bf16[16,8,512]{2,1,0:T(8,128)(2,1)S(1)} all-to-all(bf16[16,8,512]{2,1,0:T(8,128)(2,1)S(1)} %gather.1), channel_id=1, replica_groups=mesh['row_0'=4,'row_1'=8,'col'=16] {'col'}, dimensions={0} | all-to-all | bytes 262144 | tf_op jit(solution)/shard_map/all_to_all | solution.py:32
  135.9 2.7 %tail.1 = bf16[512,128]{1,0:T(8,128)(2,1)} custom-call(bf16[128,512]{1,0:T(8,128)(2,1)S(1)} %bitcast.19, f32[512,128]{1,0:T(8,128)S(1)} %get-tuple-element.53.mid, f32[512,128]{1,0:T(8,128)S(1)} %get-tuple-element.54.out_gate, bf16[128,128]{1,0:T(8,128)(2,1)S(1)} %get-tuple-element.55.triangle_out, bf16[128,512]{1,0:T(8,128)(2,1)S(1)} %get-tuple-element.56.transition_up, ...), custom_call_target="tpu_custom_call" | custom-call | tf_op jit(solution)/shard_map/tail/pallas_call | solution.py:54
  (1 shorter events, 0.0 us)
Async XLA Ops:
  2.7 28.1 %all-to-all-start = ((bf16[32,16,128]{2,1,0:T(8,128)(2,1)}), bf16[32,16,128]{2,1,0:T(8,128)(2,1)S(1)}, u32[]{:S(2)}, u32[]{:S(2)}) async-start(bf16[32,16,128]{2,1,0:T(8,128)(2,1)} %get-tuple-element.30), calls=%async_computation | async-start | bytes 262144 | tf_op jit(solution)/shard_map/all_to_all | solution.py:32

commit v6 on v5

--- a/solution.py
+++ b/solution.py
@@ -13,10 +13,9 @@
 F32 = jnp.float32
 K_PARTS = 2
 I_PARTS = 2
+TAIL_PARTS = 2
 KEPT = (
     "pair",
-    "mask",
-    "chain",
     "attention_out",
     "outer_in",
     "outer_out",
@@ -43,19 +42,21 @@
     return center * lax.rsqrt(spread + 1e-05)
 
 
-def local_kernel(body, out_shape, name, *operands, scalars=0, scratch=(), far=False, out_space=None):
+def local_kernel(body, out_shape, name, *operands, scalars=0, scratch=(), far=False):
     space = pltpu.HBM if far else pltpu.VMEM
     spaces = [pltpu.SMEM if k < scalars else space for k in range(len(operands))]
     held = [
         pltpu.with_memory_space_constraint(x, space) if space is pltpu.VMEM else x
         for x, space in zip(operands, spaces)
     ]
-    out_space = out_space or pltpu.VMEM
+    in_hbm = lambda x: isinstance(x, jax.ShapeDtypeStruct)
     return pl.pallas_call(
         body,
         out_shape=out_shape,
         in_specs=[pl.BlockSpec(memory_space=space) for space in spaces],
-        out_specs=jax.tree.map(lambda _: pl.BlockSpec(memory_space=out_space), out_shape),
+        out_specs=jax.tree.map(
+            lambda x: pl.BlockSpec(memory_space=pltpu.HBM if in_hbm(x) else pltpu.VMEM), out_shape
+        ),
         scratch_shapes=scratch,
         name=name,
     )(*held)
@@ -89,13 +90,20 @@
 
 
 def project_body(sequence, weights, key_values, query, gate, near, held, arrived):
-    first_copy, second_copy = fetch((sequence, weights), (near, held), arrived)
+    halves = [pl.ds(k * LANES, LANES) for k in range(2)]
+    first_copy, *weight_copies = fetch(
+        (sequence, *[weights.at[half] for half in halves]),
+        (near, *[held.at[half] for half in halves]),
+        arrived,
+    )
     first_copy.wait()
     normed = layer_norm(near[...].astype(F32)).astype(BF16)
-    second_copy.wait()
-    projected = mm(normed, held[...], 1, 1)
-    rows = projected.shape[0]
-    head, rest = projected[:, :LANES], projected[:, LANES:]
+    projected = []
+    for half, copy in zip(halves, weight_copies):
+        copy.wait()
+        projected.append(mm(normed, held[half], 1, 1))
+    head, rest = projected
+    rows = head.shape[0]
     first = lax.broadcasted_iota(jnp.int32, (rows, LANES), 1) < LANES // 2
     both = jnp.where(first, pltpu.roll(head, LANES // 2, 1), pltpu.roll(rest, LANES // 2, 1))
     key_values[...] = jnp.broadcast_to(both.astype(BF16)[None], key_values.shape)
@@ -103,14 +111,18 @@
     gate[...] = jnp.where(first, 0.0, jax.nn.sigmoid(rest))
 
 
-def prepare_body(row_start, col_start, *refs):
+def prepare_body(row_start, col, chain_bias, *refs):
     count = len(KEPT)
-    sources, targets = refs[: count + 2], refs[count + 2 : 2 * count + 2]
-    blocks, gates_in, values_in, last_in, live, spread_order, gather_order = refs[2 * count + 2 : -4]
-    bias_near, triangle_near, turned_bias, arrived = refs[-4:]
-    copies = fetch(sources, (*targets, bias_near, triangle_near), arrived)
+    sources, targets = refs[: count + 4], refs[count + 4 : 2 * count + 4]
+    blocks, gates_in, values_in, last_in, live, spread_order, gather_order, extra, pick = refs[
+        2 * count + 4 : -6
+    ]
+    mask_near, chain_near, bias_near, triangle_near, turned_bias, arrived = refs[-6:]
+    copies = fetch(
+        sources, (*targets, mask_near, chain_near, bias_near, triangle_near), arrived
+    )
     near = dict(zip(KEPT, targets))
-    landed = dict(zip((*KEPT, "bias_in", "triangle"), copies))
+    landed = dict(zip((*KEPT, "mask", "chain", "bias_in", "triangle"), copies))
 
     size = spread_order.shape[0]
     n = lax.broadcasted_iota(jnp.int32, spread_order.shape, 0)
@@ -126,6 +138,10 @@
     wanted = (i // few * group + c) * few + i % few
     gather_order[...] = jnp.where(m % size == wanted, 1.0, 0.0).astype(BF16)
 
+    n = lax.broadcasted_iota(jnp.int32, pick.shape, 0)
+    m = lax.broadcasted_iota(jnp.int32, pick.shape, 1)
+    pick[...] = jnp.where(m == col[0] * pick.shape[0] + n, 1.0, 0.0).astype(BF16)
+
     landed["pair"].wait()
     landed["bias_in"].wait()
     wide = near["pair"][...].astype(F32)
@@ -139,14 +155,28 @@
             blocks[:, h * GROUPS + t, :] = turned_bias[t, pl.ds(h, columns, stride=2), :]
 
     landed["mask"].wait()
-    mask = near["mask"][...].astype(F32).astype(BF16)
+    mask = mask_near[...].astype(F32).astype(BF16)
     length = mask.shape[1]
     residue = lax.broadcasted_iota(jnp.int32, (length, live.shape[1]), 0)
     pair = lax.broadcasted_iota(jnp.int32, (length, live.shape[1]), 1)
     of_row = jnp.where(residue == row_start[0] + pair // (LANES // GROUPS), 1.0, 0.0).astype(BF16)
-    of_col = jnp.where(residue == col_start[0] + pair % (LANES // GROUPS), 1.0, 0.0).astype(BF16)
+    of_col = jnp.where(residue == col[0] * (LANES // GROUPS) + pair % (LANES // GROUPS), 1.0, 0.0).astype(BF16)
     mask = jnp.broadcast_to(mask, (8, length))
     live[...] = (mm(mask, of_row, 1, 0) * mm(mask, of_col, 1, 0))[:1]
+
+    landed["chain"].wait()
+    eight = blocks.shape[1]
+    four = eight // 2
+    position = lax.broadcasted_iota(jnp.int32, (eight, length), 1)
+    row = lax.broadcasted_iota(jnp.int32, (eight, length), 0)
+    chains = jnp.broadcast_to(chain_near[...].astype(F32), (eight, length))
+    kept = jnp.broadcast_to(mask_near[...], (eight, length)) == 1
+    offset = jnp.where(row < four, chain_bias[2 * col[0]], chain_bias[2 * col[0] + 1])
+    for g in range(GROUPS):
+        here = position == row_start[0] + g * four + row % four
+        own_chain = jnp.sum(jnp.where(here, chains, 0.0), axis=1, keepdims=True)
+        added = jnp.where(chains == own_chain, offset, 0.0)
+        extra[g * eight : (g + 1) * eight, :] = jnp.where(kept | here, added, -jnp.inf)
 
     landed["triangle"].wait()
     half = gates_in.shape[1] // 2
@@ -156,17 +186,14 @@
         target[:, side : side + half, :] = across.reshape(target.shape[0], half, LANES)
     last_in[...] = triangle_near[4]
     for name in KEPT:
-        if name not in ("pair", "mask"):
+        if name != "pair":
             landed[name].wait()
 
 
-def attention_body(
-    start, col, offsets, blocks, key_values, query, gate, mask, chain, attention_out, copies, spread, joined
-):
+def attention_body(blocks, extra, key_values, query, gate, attention_out, copies, spread, joined):
     count, eight, _ = blocks.shape
     four = eight // 2
     length = count * (LANES // GROUPS)
-    rows = query.shape[0]
     lane = lax.broadcasted_iota(jnp.int32, (four, LANES), 1)
     for g in range(GROUPS):
         taken = query[g * four : (g + 1) * four, :]
@@ -176,12 +203,7 @@
     everyone = key_values[...].reshape(length, LANES)
     raw = mm(spread[...].astype(BF16), everyone, 1, 1)
     raw = raw * (1.0 / math.sqrt(LANES // 4))
-    position = lax.broadcasted_iota(jnp.int32, (eight, length), 1)
-    row = lax.broadcasted_iota(jnp.int32, (eight, length), 0)
-    chains = jnp.broadcast_to(chain[...], (eight, length))
-    kept = jnp.broadcast_to(mask[...], (eight, length)) == 1
-    offset = jnp.where(row < four, offsets[2 * col[0]], offsets[2 * col[0] + 1])
-    weights = []
+    biases = []
     for g in range(GROUPS):
         pieces = []
         for tile in range(count // GROUPS):
@@ -191,15 +213,10 @@
                     (eight, LANES),
                 )
             )
-        bias = jnp.concatenate(pieces, axis=1)
-        here = position == start[0] + g * four + row % four
-        own_chain = jnp.sum(jnp.where(here, chains, 0).astype(F32), axis=1, keepdims=True)
-        same = chains.astype(F32) == own_chain
-        scores = raw[g * eight : (g + 1) * eight] + bias + jnp.where(same, offset, 0.0)
-        allowed = kept | here
-        highest = jnp.max(jnp.where(allowed, scores, -jnp.inf), axis=1, keepdims=True)
-        raised = jnp.where(allowed, jnp.exp(scores - highest), 0.0)
-        weights.append(raised / jnp.sum(raised, axis=1, keepdims=True))
+        biases.append(jnp.concatenate(pieces, axis=1))
+    scores = raw + jnp.concatenate(biases, axis=0) + extra[...]
+    raised = jnp.exp(scores - jnp.max(scores, axis=1, keepdims=True))
+    weights = [raised / jnp.sum(raised, axis=1, keepdims=True)]
     mixed = mm(jnp.concatenate(weights, axis=0).astype(BF16), everyone, 1, 0)
     for g in range(GROUPS):
         upper = mixed[g * eight : g * eight + four]
@@ -284,10 +301,29 @@
     right_copies[...] = jnp.broadcast_to(packed.astype(BF16)[None], right_copies.shape)
 
 
-def pair_body(col, rights, left_twice, pair, outer_out, gates_in, values_in, last_in, live, tiles, mid, out_gate):
+def pair_body(
+    sequence_near,
+    rights,
+    pick,
+    left_twice,
+    pair,
+    outer_out,
+    gates_in,
+    values_in,
+    last_in,
+    live,
+    sequence_out,
+    tiles,
+    mid,
+    out_gate,
+    left,
+):
+    sent = pltpu.make_async_copy(sequence_near, sequence_out, left.at[0])
+    sent.start()
     rows, cols, channels = pair.shape
     half = channels // 2
-    taken = rights[pl.ds(col[0] * (cols // rows), cols // rows)].astype(F32)
+    taken = mm(pick[...], rights[...].reshape(-1, channels), 1, 0)
+    taken = taken.reshape(cols // rows, rows // 2, channels)
     first = lax.broadcasted_iota(jnp.int32, (rows // 2, channels), 1) < half
     pieces = []
     for k in range(cols // rows):
@@ -308,19 +344,20 @@
     operands = opened * mm(values_in[...].reshape(flat), normed, 1, 1) * live[...]
     tiles[...] = operands.astype(BF16).reshape(tiles.shape)
     out_gate[...] = jax.nn.sigmoid(mm(normed, last_in[...], 1, 0))
+    sent.wait()
 
 
 def tail_body(product, mid, out_gate, triangle_out, transition_up, transition_down, out, held, left):
-    pairs = mid.shape[0]
+    normed_product = layer_norm(product[...].astype(F32), axis=0)
+    normed_product = jnp.transpose(normed_product).astype(BF16)
+    late = mid[...] + out_gate[...] * mm(normed_product, triangle_out[...], 1, 0)
+    normed_late = layer_norm(late).astype(BF16)
+    hidden = jnp.maximum(mm(normed_late, transition_up[...], 1, 0), 0.0).astype(BF16)
     copies = []
-    for k in range(pairs // LANES):
-        here = pl.ds(k * LANES, LANES)
-        normed_product = layer_norm(product[:, here].astype(F32), axis=0)
-        normed_product = jnp.transpose(normed_product).astype(BF16)
-        late = mid[here] + out_gate[here] * mm(normed_product, triangle_out[...], 1, 0)
-        normed_late = layer_norm(late).astype(BF16)
-        hidden = jnp.maximum(mm(normed_late, transition_up[...], 1, 0), 0.0).astype(BF16)
-        held[here] = (late + mm(hidden, transition_down[...], 1, 0)).astype(BF16)
+    part = mid.shape[0] // TAIL_PARTS
+    for k in range(TAIL_PARTS):
+        here = slice(k * part, (k + 1) * part)
+        held[here] = (late[here] + mm(hidden[here], transition_down[...], 1, 0)).astype(BF16)
         copies.append(pltpu.make_async_copy(held.at[here], out.at[here], left.at[k]))
         copies[-1].start()
     for copy in copies:
@@ -351,7 +388,6 @@
     row_count = lax.axis_size(ROW)
     col_count = lax.axis_size("col")
     row_start = row_index * rows_here
-    col_start = col_index * cols_here
 
     group = channels // col_count
     heads_here = bias_weight.shape[1] // col_count
@@ -368,7 +404,7 @@
         "project",
         sequence,
         weights,
-        scratch=(pltpu.VMEM(weights.shape, BF16), pltpu.SemaphoreType.DMA((2,))),
+        scratch=(pltpu.VMEM(weights.shape, BF16), pltpu.SemaphoreType.DMA((3,))),
         far=True,
     )
     key_values_all = exchange(key_values, ROW)
@@ -377,8 +413,6 @@
     triangle = jnp.transpose(triangle_in, (1, 0, 2))
     kept = dict(
         pair=pair_state,
-        mask=residue_mask.reshape(1, -1),
-        chain=chain_index.reshape(1, -1),
         attention_out=attention_out,
         outer_in=outer_in,
         outer_out=outer_out,
@@ -398,24 +432,31 @@
             pltpu.VMEM((1, pairs_here), F32),
             pltpu.VMEM((2 * group * rows_here,) * 2, BF16),
             pltpu.VMEM((group * rows_here, K_PARTS * group * rows_here), BF16),
+            pltpu.VMEM((heads_here * rows_here, length_all), F32),
+            pltpu.VMEM((cols_here // 2, length_all // 2), BF16),
         ),
         "prepare",
         row_start.reshape(1),
-        col_start.reshape(1),
+        col_index.reshape(1),
+        chain_bias,
         *[kept[k] for k in KEPT],
+        residue_mask.reshape(1, -1),
+        chain_index.reshape(1, -1),
         bias_in,
         triangle,
-        scalars=2,
+        scalars=3,
         scratch=(
+            pltpu.VMEM((1, length_all), jnp.int32),
+            pltpu.VMEM((1, length_all), jnp.int32),
             pltpu.VMEM(bias_in.shape, BF16),
             pltpu.VMEM(triangle.shape, BF16),
             pltpu.VMEM((GROUPS, bias_in.shape[0], LANES), F32),
-            pltpu.SemaphoreType.DMA((len(KEPT) + 2,)),
+            pltpu.SemaphoreType.DMA((len(KEPT) + 4,)),
         ),
         far=True,
     )
     near, made = dict(zip(KEPT, near)), near[len(KEPT) :]
-    bias_blocks, gates_in, values_in, last_in, pair_live, spread_order, gather_order = made
+    bias_blocks, gates_in, values_in, last_in, pair_live, spread_order, gather_order, extra, pick = made
 
     key_values_all, bias_blocks = lax.optimization_barrier((key_values_all, bias_blocks))
     bias_blocks = exchange(bias_blocks, "col")
@@ -423,17 +464,12 @@
         attention_body,
         pltpu.VMEM((col_count, *sequence.shape), BF16),
         "attention",
-        row_start.reshape(1),
-        col_index.reshape(1),
-        chain_bias,
         bias_blocks,
+        extra,
         key_values_all,
         query,
         gate,
-        near["mask"],
-        near["chain"],
         near["attention_out"],
-        scalars=3,
         scratch=(
             pltpu.VMEM((heads_here * rows_here, LANES), F32),
             pltpu.VMEM((rows_here, LANES), F32),
@@ -441,10 +477,10 @@
     )
     terms = exchange(terms, "col")
     width = outer_in.shape[1]
-    sequence_out, left_twice, right_copies = local_kernel(
+    sequence_summed, left_twice, right_copies = local_kernel(
         settle_body,
         (
-            jax.ShapeDtypeStruct(sequence.shape, BF16),
+            pltpu.VMEM(sequence.shape, BF16),
             pltpu.VMEM((rows_here, width), F32),
             pltpu.VMEM((row_count, rows_here // 2, width), BF16),
         ),
@@ -454,16 +490,18 @@
         near["outer_in"],
     )
     rights = exchange(right_copies, ROW)
-    tiles, pair_mid, out_gate = local_kernel(
+    sequence_out, tiles, pair_mid, out_gate = local_kernel(
         pair_body,
         (
+            jax.ShapeDtypeStruct(sequence.shape, BF16),
             pltpu.VMEM((col_count, 2 * group, pairs_here), BF16),
             pltpu.VMEM((pairs_here, channels), F32),
             pltpu.VMEM((pairs_here, channels), F32),
         ),
         "pair",
-        col_index.reshape(1),
+        sequence_summed,
         rights,
+        pick,
         left_twice,
         near["pair"],
         near["outer_out"],
@@ -471,7 +509,7 @@
         values_in,
         last_in,
         pair_live,
-        scalars=1,
+        scratch=(pltpu.SemaphoreType.DMA((1,)),),
     )
 
     tiles = exchange(tiles, "col")
@@ -511,9 +549,8 @@
         near["transition_down"],
         scratch=(
             pltpu.VMEM((pairs_here, channels), BF16),
-            pltpu.SemaphoreType.DMA((pairs_here // LANES,)),
-        ),
-        out_space=pltpu.HBM,
+            pltpu.SemaphoreType.DMA((TAIL_PARTS,)),
+        ),
     ).reshape(rows_here, cols_here, channels)
     return (sequence_out, pair_out)
 

time: 139 us -> 137 us (0.986)
  transfers between devices with their start and end apart: 1 -> 1, of which waited for: 1 -> 1; matrix products, arithmetic and copies ran while one was open for 0% -> 0% of each run, Pallas kernels for 1% -> 2%
where the time goes in v6:
time: 137 us
  blocking collectives  101 us (74%)
  starting transfers between devices  16.5 us (12%)
  Pallas kernels  9.5 us (7%)
  waiting for transfers between devices  8.84 us (6%)
    all_to_all x7, blocking collectives, exchange(): return lax.all_to_all(blocks, axis, split_axis=0, concat_axis=0, tiled=True)  101 us
    all_to_all x1, starting transfers between devices, exchange(): return lax.all_to_all(blocks, axis, split_axis=0, concat_axis=0, tiled=True)  16.5 us
    pallas_call x8, Pallas kernels, local_kernel(): pl.pallas_call(body, out_shape=out_shape, in_specs=[pl.BlockSpec(memory_s...  9.5 us
    all_to_all x1, waiting for transfers between devices, exchange(): return lax.all_to_all(blocks, axis, split_axis=0, concat_axis=0, tiled=True)  8.84 us
  transfers between devices with their start and end apart: 1, of which 1 were waited for; matrix products, arithmetic and copies ran while one was open for 0% of the time, Pallas kernels for 2%

profile of v6, /device:TPU:1, one launch (start us, length us, event | category | flops | bytes accessed | tf_op | source)
XLA Modules:
  0.0 137.0 jit_solution(13501979921078760109)
XLA Ops:
  0.6 2.2 %project.1 = (bf16[32,16,128]{2,1,0:T(8,128)(2,1)}, f32[16,128]{1,0:T(8,128)S(1)}, f32[16,128]{1,0:T(8,128)S(1)}, bf16[16,1024]{1,0:T(8,128)(2,1)S(1)}) custom-call(bf16[16,1024]{1,0:T(8,128)(2,1)} %sequence.1, bf16[256,1024]{1,0:T(8,128)(2,1)} %bitcast.20), custom_call_target="tpu_custom_call" | custom-call | tf_op jit(solution)/shard_map/project/pallas_call | solution.py:53
  2.9 16.5 %all-to-all-start = ((bf16[32,16,128]{2,1,0:T(8,128)(2,1)}), bf16[32,16,128]{2,1,0:T(8,128)(2,1)S(1)}, u32[]{:S(2)}, u32[]{:S(2)}) async-start(bf16[32,16,128]{2,1,0:T(8,128)(2,1)} %get-tuple-element.31), calls=%async_computation | async-start | bytes 262144 | tf_op jit(solution)/shard_map/all_to_all | solution.py:31
  19.4 2.7 %prepare.1 = (bf16[16,32,128]{2,1,0:T(8,128)(2,1)S(1)}, bf16[64,1024]{1,0:T(8,128)(2,1)S(1)}, bf16[1024,128]{1,0:T(8,128)(2,1)S(1)}, bf16[128,128]{1,0:T(8,128)(...) custom-call(s32[1]{0:T(128)} %bitcast.2.row_start, ...), custom_call_target="tpu_custom_call" | custom-call | tf_op jit(solution)/shard_map/prepare/pallas_call | solution.py:53
  22.1 8.8 %all-to-all-done.key_values = bf16[32,16,128]{2,1,0:T(8,128)(2,1)S(1)} async-done(((bf16[32,16,128]{2,1,0:T(8,128)(2,1)}), bf16[32,16,128]{2,1,0:T(8,128)(2,1)S(1)}, u32[]{:S(2)}, u32[]{:S(2)}) %all-to-all-start) | async-done | bytes 131104 | tf_op jit(solution)/shard_map/all_to_all | solution.py:31
  31.0 12.9 %all_to_all.40.blocks = f32[16,8,128]{2,1,0:T(8,128)S(1)} all-to-all(f32[16,8,128]{2,1,0:T(8,128)S(1)} %get-tuple-element.33), channel_id=1, replica_groups=mesh['row_0'=4,'row_1'=8,'col'=16] {'col'}, dimensions={0} | all-to-all | bytes 131072 | tf_op jit(solution)/shard_map/all_to_all | solution.py:31
  43.8 0.7 attention.1
  44.5 12.6 %all_to_all.41.terms = bf16[16,16,1024]{2,1,0:T(8,128)(2,1)S(1)} all-to-all(bf16[16,16,1024]{2,1,0:T(8,128)(2,1)S(1)} %attention.1), channel_id=1, replica_groups=mesh['row_0'=4,'row_1'=8,'col'=16] {'col'}, dimensions={0} | all-to-all | bytes 1048576 | tf_op jit(solution)/shard_map/all_to_all | solution.py:31
  57.2 0.5 settle.1
  57.6 14.2 %all_to_all.42.rights = bf16[32,8,128]{2,1,0:T(8,128)(2,1)S(1)} all-to-all(bf16[32,8,128]{2,1,0:T(8,128)(2,1)S(1)} %get-tuple-element.42), channel_id=1, replica_groups=mesh['row_0'=4,'row_1'=8,'col'=16] {'row_0','row_1'}, dimensions={0} | all-to-all | bytes 131072 | tf_op jit(solution)/shard_map/all_to_all | solution.py:31
  71.9 0.9 pair.1
  72.8 12.1 %all_to_all.43.tiles = bf16[16,16,512]{2,1,0:T(8,128)(2,1)S(1)} all-to-all(bf16[16,16,512]{2,1,0:T(8,128)(2,1)S(1)} %get-tuple-element.52), channel_id=1, replica_groups=mesh['row_0'=4,'row_1'=8,'col'=16] {'col'}, dimensions={0} | all-to-all | bytes 524288 | tf_op jit(solution)/shard_map/all_to_all | solution.py:31
  84.9 0.5 spread.1
  85.4 17.7 %all_to_all.44 = bf16[32,24,256]{2,1,0:T(8,128)(2,1)S(1)} all-to-all(bf16[32,24,256]{2,1,0:T(8,128)(2,1)S(1)} %spread.1), channel_id=1, replica_groups=mesh['row_0'=4,'row_1'=8,'col'=16] {'row_0','row_1'}, dimensions={0} | all-to-all | bytes 786432 | tf_op jit(solution)/shard_map/all_to_all | solution.py:31
  103.1 0.3 fusion
  103.4 18.6 %all_to_all.45.parts = bf16[32,8,512]{2,1,0:T(8,128)(2,1)S(1)} all-to-all(bf16[32,8,512]{2,1,0:T(8,128)(2,1)S(1)} %fusion), channel_id=1, replica_groups=mesh['row_0'=4,'row_1'=8,'col'=16] {'row_0','row_1'}, dimensions={0} | all-to-all | bytes 524288 | tf_op jit(solution)/shard_map/all_to_all | solution.py:31
  122.0 0.3 gather.1
  122.3 13.0 %all_to_all.46 = bf16[16,8,512]{2,1,0:T(8,128)(2,1)S(1)} all-to-all(bf16[16,8,512]{2,1,0:T(8,128)(2,1)S(1)} %gather.1), channel_id=1, replica_groups=mesh['row_0'=4,'row_1'=8,'col'=16] {'col'}, dimensions={0} | all-to-all | bytes 262144 | tf_op jit(solution)/shard_map/all_to_all | solution.py:31
  135.3 1.6 %tail.1 = bf16[512,128]{1,0:T(8,128)(2,1)} custom-call(bf16[128,512]{1,0:T(8,128)(2,1)S(1)} %bitcast.18, f32[512,128]{1,0:T(8,128)S(1)} %get-tuple-element.55.mid, f32[512,128]{1,0:T(8,128)S(1)} %get-tuple-element.56.out_gate, bf16[128,128]{1,0:T(8,128)(2,1)S(1)} %get-tuple-element.57.triangle_out, bf16[128,512]{1,0:T(8,128)(2,1)S(1)} %get-tuple-element.58.transition_up, ...), custom_call_target="tpu_custom_call" | custom-call | tf_op jit(solution)/shard_map/tail/pallas_call | solution.py:53
  (1 shorter events, 0.0 us)
Async XLA Ops:
  2.9 28.1 %all-to-all-start = ((bf16[32,16,128]{2,1,0:T(8,128)(2,1)}), bf16[32,16,128]{2,1,0:T(8,128)(2,1)S(1)}, u32[]{:S(2)}, u32[]{:S(2)}) async-start(bf16[32,16,128]{2,1,0:T(8,128)(2,1)} %get-tuple-element.31), calls=%async_computation | async-start | bytes 262144 | tf_op jit(solution)/shard_map/all_to_all | solution.py:31

commit v7 on v6

--- a/solution.py
+++ b/solution.py
@@ -9,11 +9,13 @@
 from jax.sharding import PartitionSpec as P
 
 ROW = ("row_0", "row_1")
+ROW_TURN = 20
+COL_TURN = 1
 BF16 = jnp.bfloat16
 F32 = jnp.float32
 K_PARTS = 2
 I_PARTS = 2
-TAIL_PARTS = 2
+TAIL_PARTS = 4
 KEPT = (
     "pair",
     "attention_out",
@@ -28,12 +30,14 @@
 
 
 def exchange(blocks, axis):
-    return lax.all_to_all(blocks, axis, split_axis=0, concat_axis=0, tiled=True)
-
-
-def from_everyone(value, axis):
-    copies = jnp.broadcast_to(value, (lax.axis_size(axis), *value.shape))
-    return exchange(copies, axis)
+    rows, cols = lax.axis_size(ROW), lax.axis_size("col")
+    if axis == "col":
+        groups = [[r * cols + (p ^ COL_TURN) for p in range(cols)] for r in range(rows)]
+    else:
+        groups = [[(p ^ ROW_TURN) * cols + q for p in range(rows)] for q in range(cols)]
+    return lax.all_to_all(
+        blocks, (*ROW, "col"), split_axis=0, concat_axis=0, tiled=True, axis_index_groups=groups
+    )
 
 
 def layer_norm(values, axis=-1):
@@ -140,14 +144,18 @@
 
     n = lax.broadcasted_iota(jnp.int32, pick.shape, 0)
     m = lax.broadcasted_iota(jnp.int32, pick.shape, 1)
-    pick[...] = jnp.where(m == col[0] * pick.shape[0] + n, 1.0, 0.0).astype(BF16)
+    pick[...] = jnp.where(m == (col[0] ^ (ROW_TURN // 2)) * pick.shape[0] + n, 1.0, 0.0).astype(BF16)
 
     landed["pair"].wait()
     landed["bias_in"].wait()
     wide = near["pair"][...].astype(F32)
     turned = jnp.concatenate([wide[GROUPS * (p % GROUPS) + p // GROUPS] for p in range(rows)], axis=0)
     normed = layer_norm(turned).astype(BF16)
-    bias = mm(bias_near[...], normed, 1, 1)
+    heads = bias_near.shape[0]
+    n = lax.broadcasted_iota(jnp.int32, (heads, heads), 0)
+    m = lax.broadcasted_iota(jnp.int32, (heads, heads), 1)
+    by_place = jnp.where(m == n ^ (2 * COL_TURN), 1.0, 0.0).astype(BF16)
+    bias = mm(mm(by_place, bias_near[...], 1, 0).astype(BF16), normed, 1, 1)
     columns = blocks.shape[0]
     for t in range(GROUPS):
         turned_bias[t] = bias[:, t * LANES : (t + 1) * LANES]
@@ -200,7 +208,7 @@
         for h in range(2):
             own = (lane >= h * (LANES // 4)) & (lane < (h + 1) * (LANES // 4))
             spread[g * eight + h * four : g * eight + (h + 1) * four, :] = jnp.where(own, taken, 0.0)
-    everyone = key_values[...].reshape(length, LANES)
+    everyone = jnp.concatenate([key_values[r ^ ROW_TURN] for r in range(key_values.shape[0])], axis=0)
     raw = mm(spread[...].astype(BF16), everyone, 1, 1)
     raw = raw * (1.0 / math.sqrt(LANES // 4))
     biases = []
@@ -209,7 +217,7 @@
         for tile in range(count // GROUPS):
             pieces.append(
                 regroup(
-                    lambda k, tile=tile, g=g: turn_lanes(blocks[GROUPS * tile + k], k - g),
+                    lambda k, tile=tile, g=g: turn_lanes(blocks[(GROUPS * tile + k) ^ COL_TURN], k - g),
                     (eight, LANES),
                 )
             )
@@ -239,7 +247,7 @@
                 [
                     regroup(
                         lambda k, tile=tile, g=g, at=at: turn_lanes(
-                            tiles[GROUPS * tile + k, :, at : at + LANES].astype(F32), k - g
+                            tiles[(GROUPS * tile + k) ^ COL_TURN, :, at : at + LANES].astype(F32), k - g
                         ),
                         (chans, LANES),
                     )
@@ -268,7 +276,8 @@
     rows = pairs // (LANES // GROUPS)
     summed = mm(order[...], parts[...].reshape(total * few, length), 1, 0)
     for q in range(count):
-        tile, s = q // GROUPS, q % GROUPS
+        place = q ^ COL_TURN ^ (ROW_TURN // 2)
+        tile, s = place // GROUPS, place % GROUPS
         pieces = []
         for t in range(rows // GROUPS):
             pieces.append(
@@ -302,7 +311,6 @@
 
 
 def pair_body(
-    sequence_near,
     rights,
     pick,
     left_twice,
@@ -312,14 +320,10 @@
     values_in,
     last_in,
     live,
-    sequence_out,
     tiles,
     mid,
     out_gate,
-    left,
 ):
-    sent = pltpu.make_async_copy(sequence_near, sequence_out, left.at[0])
-    sent.start()
     rows, cols, channels = pair.shape
     half = channels // 2
     taken = mm(pick[...], rights[...].reshape(-1, channels), 1, 0)
@@ -344,16 +348,28 @@
     operands = opened * mm(values_in[...].reshape(flat), normed, 1, 1) * live[...]
     tiles[...] = operands.astype(BF16).reshape(tiles.shape)
     out_gate[...] = jax.nn.sigmoid(mm(normed, last_in[...], 1, 0))
-    sent.wait()
-
-
-def tail_body(product, mid, out_gate, triangle_out, transition_up, transition_down, out, held, left):
+
+
+def tail_body(
+    sequence_near,
+    product,
+    mid,
+    out_gate,
+    triangle_out,
+    transition_up,
+    transition_down,
+    sequence_out,
+    out,
+    held,
+    left,
+):
+    copies = [pltpu.make_async_copy(sequence_near, sequence_out, left.at[TAIL_PARTS])]
+    copies[0].start()
     normed_product = layer_norm(product[...].astype(F32), axis=0)
     normed_product = jnp.transpose(normed_product).astype(BF16)
     late = mid[...] + out_gate[...] * mm(normed_product, triangle_out[...], 1, 0)
     normed_late = layer_norm(late).astype(BF16)
     hidden = jnp.maximum(mm(normed_late, transition_up[...], 1, 0), 0.0).astype(BF16)
-    copies = []
     part = mid.shape[0] // TAIL_PARTS
     for k in range(TAIL_PARTS):
         here = slice(k * part, (k + 1) * part)
@@ -490,16 +506,14 @@
         near["outer_in"],
     )
     rights = exchange(right_copies, ROW)
-    sequence_out, tiles, pair_mid, out_gate = local_kernel(
+    tiles, pair_mid, out_gate = local_kernel(
         pair_body,
         (
-            jax.ShapeDtypeStruct(sequence.shape, BF16),
             pltpu.VMEM((col_count, 2 * group, pairs_here), BF16),
             pltpu.VMEM((pairs_here, channels), F32),
             pltpu.VMEM((pairs_here, channels), F32),
         ),
         "pair",
-        sequence_summed,
         rights,
         pick,
         left_twice,
@@ -509,7 +523,6 @@
         values_in,
         last_in,
         pair_live,
-        scratch=(pltpu.SemaphoreType.DMA((1,)),),
     )
 
     tiles = exchange(tiles, "col")
@@ -537,10 +550,14 @@
     )
     product = exchange(product, "col").reshape(channels, pairs_here)
 
-    pair_out = local_kernel(
+    sequence_out, pair_out = local_kernel(
         tail_body,
-        jax.ShapeDtypeStruct((pairs_here, channels), BF16),
+        (
+            jax.ShapeDtypeStruct(sequence.shape, BF16),
+            jax.ShapeDtypeStruct((pairs_here, channels), BF16),
+        ),
         "tail",
+        sequence_summed,
         product,
         pair_mid,
         out_gate,
@@ -549,9 +566,10 @@
         near["transition_down"],
         scratch=(
             pltpu.VMEM((pairs_here, channels), BF16),
-            pltpu.SemaphoreType.DMA((TAIL_PARTS,)),
-        ),
-    ).reshape(rows_here, cols_here, channels)
+            pltpu.SemaphoreType.DMA((TAIL_PARTS + 1,)),
+        ),
+    )
+    pair_out = pair_out.reshape(rows_here, cols_here, channels)
     return (sequence_out, pair_out)
 
 

time: 137 us -> 130 us (0.949)
  waiting for transfers between devices: 8.84 us -> 0.51 us
  starting transfers between devices: 16.5 us -> 18.7 us
    all_to_all x1, waiting for transfers between devices: 8.84 us -> 0.51 us  [exchange(): lax.all_to_all(blocks, (*ROW, 'col'), split_axis=0, concat_axis=0, tiled=...]
    all_to_all x1, starting transfers between devices: 16.5 us -> 18.7 us  [exchange(): lax.all_to_all(blocks, (*ROW, 'col'), split_axis=0, concat_axis=0, tiled=...]
where the time goes in v7:
time: 130 us
  blocking collectives  99.9 us (77%)
  starting transfers between devices  18.7 us (14%)
  Pallas kernels  9.53 us (7%)
    all_to_all x7, blocking collectives, exchange(): lax.all_to_all(blocks, (*ROW, 'col'), split_axis=0, concat_axis=0, tiled=...  99.9 us
    all_to_all x1, starting transfers between devices, exchange(): lax.all_to_all(blocks, (*ROW, 'col'), split_axis=0, concat_axis=0, tiled=...  18.7 us
    pallas_call x8, Pallas kernels, local_kernel(): pl.pallas_call(body, out_shape=out_shape, in_specs=[pl.BlockSpec(memory_s...  9.53 us
  transfers between devices with their start and end apart: 1, of which 1 were waited for; matrix products, arithmetic and copies ran while one was open for 0% of the time, Pallas kernels for 2%

profile of v7, /device:TPU:1, one launch (start us, length us, event | category | flops | bytes accessed | tf_op | source)
XLA Modules:
  0.0 129.7 jit_solution(6257331511303721978)
XLA Ops:
  0.6 2.2 %project.1 = (bf16[32,16,128]{2,1,0:T(8,128)(2,1)}, f32[16,128]{1,0:T(8,128)S(1)}, f32[16,128]{1,0:T(8,128)S(1)}, bf16[16,1024]{1,0:T(8,128)(2,1)S(1)}) custom-call(bf16[16,1024]{1,0:T(8,128)(2,1)} %sequence.1, bf16[256,1024]{1,0:T(8,128)(2,1)} %bitcast.20), custom_call_target="tpu_custom_call" | custom-call | tf_op jit(solution)/shard_map/project/pallas_call | solution.py:57
  2.9 18.7 %all-to-all-start = ((bf16[32,16,128]{2,1,0:T(8,128)(2,1)}), bf16[32,16,128]{2,1,0:T(8,128)(2,1)S(1)}, u32[]{:S(2)}, u32[]{:S(2)}) async-start(bf16[32,16,128]{2,1,0:T(8,128)(2,1)} %get-tuple-element.32), calls=%async_computation | async-start | bytes 262144 | tf_op jit(solution)/shard_map/all_to_all | solution.py:38
  21.6 2.7 %prepare.1 = (bf16[16,32,128]{2,1,0:T(8,128)(2,1)S(1)}, bf16[64,1024]{1,0:T(8,128)(2,1)S(1)}, bf16[1024,128]{1,0:T(8,128)(2,1)S(1)}, bf16[128,128]{1,0:T(8,128)(...) custom-call(s32[1]{0:T(128)} %bitcast.2.row_start, ...), custom_call_target="tpu_custom_call" | custom-call | tf_op jit(solution)/shard_map/prepare/pallas_call | solution.py:57
  24.3 0.5 all-to-all-done.key_values
  24.8 12.2 %all_to_all.40.blocks = f32[16,8,128]{2,1,0:T(8,128)S(1)} all-to-all(f32[16,8,128]{2,1,0:T(8,128)S(1)} %get-tuple-element.34), channel_id=1, replica_groups={{1,0,3,2,5,4,7,6,9,8,11,10,13,12,15,14},{17,16,19,18,21,20,23,22,25,24,..., dimensions={0} | all-to-all | bytes 131072 | tf_op jit(solution)/shard_map/all_to_all | solution.py:38
  37.0 0.7 attention.1
  37.7 12.3 %all_to_all.41.terms = bf16[16,16,1024]{2,1,0:T(8,128)(2,1)S(1)} all-to-all(bf16[16,16,1024]{2,1,0:T(8,128)(2,1)S(1)} %attention.1), channel_id=1, replica_groups={{1,0,3,2,5,4,7,6,9,8,11,10,13,12,15,14},{17,16,19,18,21,20,23,22,25,24,..., dimensions={0} | all-to-all | bytes 1048576 | tf_op jit(solution)/shard_map/all_to_all | solution.py:38
  50.0 0.5 settle.1
  50.5 14.1 %all_to_all.42.rights = bf16[32,8,128]{2,1,0:T(8,128)(2,1)S(1)} all-to-all(bf16[32,8,128]{2,1,0:T(8,128)(2,1)S(1)} %get-tuple-element.43), channel_id=1, replica_groups={{320,336,352,368,256,272,288,304,448,464,480,496,384,400,416,432,64,80,..., dimensions={0} | all-to-all | bytes 131072 | tf_op jit(solution)/shard_map/all_to_all | solution.py:38
  64.5 0.9 pair.1
  65.4 11.2 %all_to_all.43.tiles = bf16[16,16,512]{2,1,0:T(8,128)(2,1)S(1)} all-to-all(bf16[16,16,512]{2,1,0:T(8,128)(2,1)S(1)} %get-tuple-element.52), channel_id=1, replica_groups={{1,0,3,2,5,4,7,6,9,8,11,10,13,12,15,14},{17,16,19,18,21,20,23,22,25,24,..., dimensions={0} | all-to-all | bytes 524288 | tf_op jit(solution)/shard_map/all_to_all | solution.py:38
  76.6 0.5 spread.1
  77.1 21.7 %all_to_all.44 = bf16[32,24,256]{2,1,0:T(8,128)(2,1)S(1)} all-to-all(bf16[32,24,256]{2,1,0:T(8,128)(2,1)S(1)} %spread.1), channel_id=1, replica_groups={{320,336,352,368,256,272,288,304,448,464,480,496,384,400,416,432,64,80,..., dimensions={0} | all-to-all | bytes 786432 | tf_op jit(solution)/shard_map/all_to_all | solution.py:38
  98.8 0.3 fusion
  99.0 17.5 %all_to_all.45.parts = bf16[32,8,512]{2,1,0:T(8,128)(2,1)S(1)} all-to-all(bf16[32,8,512]{2,1,0:T(8,128)(2,1)S(1)} %fusion), channel_id=1, replica_groups={{320,336,352,368,256,272,288,304,448,464,480,496,384,400,416,432,64,80,..., dimensions={0} | all-to-all | bytes 524288 | tf_op jit(solution)/shard_map/all_to_all | solution.py:38
  116.5 0.3 gather.1
  116.9 11.1 %all_to_all.46 = bf16[16,8,512]{2,1,0:T(8,128)(2,1)S(1)} all-to-all(bf16[16,8,512]{2,1,0:T(8,128)(2,1)S(1)} %gather.1), channel_id=1, replica_groups={{1,0,3,2,5,4,7,6,9,8,11,10,13,12,15,14},{17,16,19,18,21,20,23,22,25,24,..., dimensions={0} | all-to-all | bytes 262144 | tf_op jit(solution)/shard_map/all_to_all | solution.py:38
  128.0 1.7 %tail.1 = (bf16[16,1024]{1,0:T(8,128)(2,1)}, bf16[512,128]{1,0:T(8,128)(2,1)}) custom-call(bf16[16,1024]{1,0:T(8,128)(2,1)S(1)} %get-tuple-element.42.sequence_near, bf16[128,512]{1,0:T(8,128)(2,1)S(1)} %bitcast.18, f32[512,128]{1,0:T(8,128)S(1)} %get-tuple-element.55.mid, f32[512,128]{1,0:T(8,128)S(1)} %get-tuple-element.56.out_gate, ...), custom_call_target="tpu_custom_call" | custom-call | tf_op jit(solution)/shard_map/tail/pallas_call | solution.py:57
  (1 shorter events, 0.0 us)
Async XLA Ops:
  2.9 22.0 %all-to-all-start = ((bf16[32,16,128]{2,1,0:T(8,128)(2,1)}), bf16[32,16,128]{2,1,0:T(8,128)(2,1)S(1)}, u32[]{:S(2)}, u32[]{:S(2)}) async-start(bf16[32,16,128]{2,1,0:T(8,128)(2,1)} %get-tuple-element.32), calls=%async_computation | async-start | bytes 262144 | tf_op jit(solution)/shard_map/all_to_all | solution.py:38

commit v8 on v7

--- a/solution.py
+++ b/solution.py
@@ -9,8 +9,12 @@
 from jax.sharding import PartitionSpec as P
 
 ROW = ("row_0", "row_1")
-ROW_TURN = 20
-COL_TURN = 1
+PAIR_AT = tuple((u // 4 + u + 3) % 4 * 4 + (u + 2) % 4 for u in range(16))
+PAIR_PLACE = tuple(PAIR_AT.index(q) for q in range(16))
+ROW_AT = tuple(2 * q + k for q in PAIR_AT for k in range(2))
+ROW_PLACE = tuple(ROW_AT.index(r) for r in range(32))
+COL_AT = tuple(p % 4 * 4 + (p // 4 ^ 1) for p in range(16))
+COL_PLACE = tuple(COL_AT.index(q) for q in range(16))
 BF16 = jnp.bfloat16
 F32 = jnp.float32
 K_PARTS = 2
@@ -32,9 +36,9 @@
 def exchange(blocks, axis):
     rows, cols = lax.axis_size(ROW), lax.axis_size("col")
     if axis == "col":
-        groups = [[r * cols + (p ^ COL_TURN) for p in range(cols)] for r in range(rows)]
+        groups = [[r * cols + q for q in COL_AT] for r in range(rows)]
     else:
-        groups = [[(p ^ ROW_TURN) * cols + q for p in range(rows)] for q in range(cols)]
+        groups = [[r * cols + q for r in ROW_AT] for q in range(cols)]
     return lax.all_to_all(
         blocks, (*ROW, "col"), split_axis=0, concat_axis=0, tiled=True, axis_index_groups=groups
     )
@@ -94,18 +98,20 @@
 
 
 def project_body(sequence, weights, key_values, query, gate, near, held, arrived):
-    halves = [pl.ds(k * LANES, LANES) for k in range(2)]
+    each = LANES // 4
+    parts = [pl.ds(k * each, each) for k in range(8)]
     first_copy, *weight_copies = fetch(
-        (sequence, *[weights.at[half] for half in halves]),
-        (near, *[held.at[half] for half in halves]),
+        (sequence, *[weights.at[part] for part in parts]),
+        (near, *[held.at[part] for part in parts]),
         arrived,
     )
     first_copy.wait()
     normed = layer_norm(near[...].astype(F32)).astype(BF16)
     projected = []
-    for half, copy in zip(halves, weight_copies):
-        copy.wait()
-        projected.append(mm(normed, held[half], 1, 1))
+    for half in range(2):
+        for copy in weight_copies[half * 4 : half * 4 + 4]:
+            copy.wait()
+        projected.append(mm(normed, held[half * LANES : (half + 1) * LANES], 1, 1))
     head, rest = projected
     rows = head.shape[0]
     first = lax.broadcasted_iota(jnp.int32, (rows, LANES), 1) < LANES // 2
@@ -144,7 +150,10 @@
 
     n = lax.broadcasted_iota(jnp.int32, pick.shape, 0)
     m = lax.broadcasted_iota(jnp.int32, pick.shape, 1)
-    pick[...] = jnp.where(m == (col[0] ^ (ROW_TURN // 2)) * pick.shape[0] + n, 1.0, 0.0).astype(BF16)
+    place = jnp.zeros(pick.shape, jnp.int32)
+    for q, u in enumerate(PAIR_PLACE):
+        place = jnp.where(col[0] == q, u, place)
+    pick[...] = jnp.where(m == place * pick.shape[0] + n, 1.0, 0.0).astype(BF16)
 
     landed["pair"].wait()
     landed["bias_in"].wait()
@@ -154,7 +163,8 @@
     heads = bias_near.shape[0]
     n = lax.broadcasted_iota(jnp.int32, (heads, heads), 0)
     m = lax.broadcasted_iota(jnp.int32, (heads, heads), 1)
-    by_place = jnp.where(m == n ^ (2 * COL_TURN), 1.0, 0.0).astype(BF16)
+    place = n // 2
+    by_place = jnp.where(m == (place % 4 * 4 + (place // 4 ^ 1)) * 2 + n % 2, 1.0, 0.0).astype(BF16)
     bias = mm(mm(by_place, bias_near[...], 1, 0).astype(BF16), normed, 1, 1)
     columns = blocks.shape[0]
     for t in range(GROUPS):
@@ -208,7 +218,7 @@
         for h in range(2):
             own = (lane >= h * (LANES // 4)) & (lane < (h + 1) * (LANES // 4))
             spread[g * eight + h * four : g * eight + (h + 1) * four, :] = jnp.where(own, taken, 0.0)
-    everyone = jnp.concatenate([key_values[r ^ ROW_TURN] for r in range(key_values.shape[0])], axis=0)
+    everyone = jnp.concatenate([key_values[p] for p in ROW_PLACE], axis=0)
     raw = mm(spread[...].astype(BF16), everyone, 1, 1)
     raw = raw * (1.0 / math.sqrt(LANES // 4))
     biases = []
@@ -217,7 +227,7 @@
         for tile in range(count // GROUPS):
             pieces.append(
                 regroup(
-                    lambda k, tile=tile, g=g: turn_lanes(blocks[(GROUPS * tile + k) ^ COL_TURN], k - g),
+                    lambda k, tile=tile, g=g: turn_lanes(blocks[COL_PLACE[GROUPS * tile + k]], k - g),
                     (eight, LANES),
                 )
             )
@@ -247,7 +257,7 @@
                 [
                     regroup(
                         lambda k, tile=tile, g=g, at=at: turn_lanes(
-                            tiles[(GROUPS * tile + k) ^ COL_TURN, :, at : at + LANES].astype(F32), k - g
+                            tiles[COL_PLACE[GROUPS * tile + k], :, at : at + LANES].astype(F32), k - g
                         ),
                         (chans, LANES),
                     )
@@ -276,7 +286,7 @@
     rows = pairs // (LANES // GROUPS)
     summed = mm(order[...], parts[...].reshape(total * few, length), 1, 0)
     for q in range(count):
-        place = q ^ COL_TURN ^ (ROW_TURN // 2)
+        place = PAIR_PLACE[COL_AT[q]]
         tile, s = place // GROUPS, place % GROUPS
         pieces = []
         for t in range(rows // GROUPS):
@@ -420,7 +430,7 @@
         "project",
         sequence,
         weights,
-        scratch=(pltpu.VMEM(weights.shape, BF16), pltpu.SemaphoreType.DMA((3,))),
+        scratch=(pltpu.VMEM(weights.shape, BF16), pltpu.SemaphoreType.DMA((9,))),
         far=True,
     )
     key_values_all = exchange(key_values, ROW)

time: 130 us -> 132 us (1.015)
  waiting for transfers between devices: 0.51 us -> 2.53 us
    all_to_all x1, waiting for transfers between devices: 0.51 us -> 2.53 us  [exchange(): lax.all_to_all(blocks, (*ROW, 'col'), split_axis=0, concat_axis=0, tiled=...]
where the time goes in v8:
time: 132 us; the launch traced here: 131 us
  blocking collectives  99.8 us (76%)
  starting transfers between devices  18.5 us (14%)
  Pallas kernels  9.57 us (7%)
  waiting for transfers between devices  2.53 us (2%)
    all_to_all x7, blocking collectives, exchange(): lax.all_to_all(blocks, (*ROW, 'col'), split_axis=0, concat_axis=0, tiled=...  99.8 us
    all_to_all x1, starting transfers between devices, exchange(): lax.all_to_all(blocks, (*ROW, 'col'), split_axis=0, concat_axis=0, tiled=...  18.5 us
    pallas_call x8, Pallas kernels, local_kernel(): pl.pallas_call(body, out_shape=out_shape, in_specs=[pl.BlockSpec(memory_s...  9.57 us
  transfers between devices with their start and end apart: 1, of which 1 were waited for; matrix products, arithmetic and copies ran while one was open for 0% of the time, Pallas kernels for 2%

profile of v8, /device:TPU:1, one launch (start us, length us, event | category | flops | bytes accessed | tf_op | source)
XLA Modules:
  0.0 131.4 jit_solution(14666326905907270677)
XLA Ops:
  0.6 2.3 %project.1 = (bf16[32,16,128]{2,1,0:T(8,128)(2,1)}, f32[16,128]{1,0:T(8,128)S(1)}, f32[16,128]{1,0:T(8,128)S(1)}, bf16[16,1024]{1,0:T(8,128)(2,1)S(1)}) custom-call(bf16[16,1024]{1,0:T(8,128)(2,1)} %sequence.1, bf16[256,1024]{1,0:T(8,128)(2,1)} %bitcast.20), custom_call_target="tpu_custom_call" | custom-call | tf_op jit(solution)/shard_map/project/pallas_call | solution.py:61
  2.9 18.5 %all-to-all-start = ((bf16[32,16,128]{2,1,0:T(8,128)(2,1)}), bf16[32,16,128]{2,1,0:T(8,128)(2,1)S(1)}, u32[]{:S(2)}, u32[]{:S(2)}) async-start(bf16[32,16,128]{2,1,0:T(8,128)(2,1)} %get-tuple-element.32), calls=%async_computation | async-start | bytes 262144 | tf_op jit(solution)/shard_map/all_to_all | solution.py:42
  21.5 2.7 %prepare.1 = (bf16[16,32,128]{2,1,0:T(8,128)(2,1)S(1)}, bf16[64,1024]{1,0:T(8,128)(2,1)S(1)}, bf16[1024,128]{1,0:T(8,128)(2,1)S(1)}, bf16[128,128]{1,0:T(8,128)(...) custom-call(s32[1]{0:T(128)} %bitcast.2.row_start, ...), custom_call_target="tpu_custom_call" | custom-call | tf_op jit(solution)/shard_map/prepare/pallas_call | solution.py:61
  24.2 2.5 %all-to-all-done.key_values = bf16[32,16,128]{2,1,0:T(8,128)(2,1)S(1)} async-done(((bf16[32,16,128]{2,1,0:T(8,128)(2,1)}), bf16[32,16,128]{2,1,0:T(8,128)(2,1)S(1)}, u32[]{:S(2)}, u32[]{:S(2)}) %all-to-all-start) | async-done | bytes 131104 | tf_op jit(solution)/shard_map/all_to_all | solution.py:42
  26.7 11.8 %all_to_all.40.blocks = f32[16,8,128]{2,1,0:T(8,128)S(1)} all-to-all(f32[16,8,128]{2,1,0:T(8,128)S(1)} %get-tuple-element.34), channel_id=1, replica_groups={{1,5,9,13,0,4,8,12,3,7,11,15,2,6,10,14},{17,21,25,29,16,20,24,28,19,23,..., dimensions={0} | all-to-all | bytes 131072 | tf_op jit(solution)/shard_map/all_to_all | solution.py:42
  38.5 0.7 attention.1
  39.2 13.2 %all_to_all.41.terms = bf16[16,16,1024]{2,1,0:T(8,128)(2,1)S(1)} all-to-all(bf16[16,16,1024]{2,1,0:T(8,128)(2,1)S(1)} %attention.1), channel_id=1, replica_groups={{1,5,9,13,0,4,8,12,3,7,11,15,2,6,10,14},{17,21,25,29,16,20,24,28,19,23,..., dimensions={0} | all-to-all | bytes 1048576 | tf_op jit(solution)/shard_map/all_to_all | solution.py:42
  52.4 0.5 settle.1
  52.9 14.9 %all_to_all.42.rights = bf16[32,8,128]{2,1,0:T(8,128)(2,1)S(1)} all-to-all(bf16[32,8,128]{2,1,0:T(8,128)(2,1)S(1)} %get-tuple-element.43), channel_id=1, replica_groups={{448,464,96,112,128,144,288,304,64,80,224,240,256,272,416,432,192,208,3..., dimensions={0} | all-to-all | bytes 131072 | tf_op jit(solution)/shard_map/all_to_all | solution.py:42
  67.8 0.9 pair.1
  68.7 10.7 %all_to_all.43.tiles = bf16[16,16,512]{2,1,0:T(8,128)(2,1)S(1)} all-to-all(bf16[16,16,512]{2,1,0:T(8,128)(2,1)S(1)} %get-tuple-element.52), channel_id=1, replica_groups={{1,5,9,13,0,4,8,12,3,7,11,15,2,6,10,14},{17,21,25,29,16,20,24,28,19,23,..., dimensions={0} | all-to-all | bytes 524288 | tf_op jit(solution)/shard_map/all_to_all | solution.py:42
  79.4 0.5 spread.1
  79.8 21.8 %all_to_all.44 = bf16[32,24,256]{2,1,0:T(8,128)(2,1)S(1)} all-to-all(bf16[32,24,256]{2,1,0:T(8,128)(2,1)S(1)} %spread.1), channel_id=1, replica_groups={{448,464,96,112,128,144,288,304,64,80,224,240,256,272,416,432,192,208,3..., dimensions={0} | all-to-all | bytes 786432 | tf_op jit(solution)/shard_map/all_to_all | solution.py:42
  101.7 0.3 fusion
  102.0 18.3 %all_to_all.45.parts = bf16[32,8,512]{2,1,0:T(8,128)(2,1)S(1)} all-to-all(bf16[32,8,512]{2,1,0:T(8,128)(2,1)S(1)} %fusion), channel_id=1, replica_groups={{448,464,96,112,128,144,288,304,64,80,224,240,256,272,416,432,192,208,3..., dimensions={0} | all-to-all | bytes 524288 | tf_op jit(solution)/shard_map/all_to_all | solution.py:42
  120.2 0.3 gather.1
  120.6 9.2 %all_to_all.46 = bf16[16,8,512]{2,1,0:T(8,128)(2,1)S(1)} all-to-all(bf16[16,8,512]{2,1,0:T(8,128)(2,1)S(1)} %gather.1), channel_id=1, replica_groups={{1,5,9,13,0,4,8,12,3,7,11,15,2,6,10,14},{17,21,25,29,16,20,24,28,19,23,..., dimensions={0} | all-to-all | bytes 262144 | tf_op jit(solution)/shard_map/all_to_all | solution.py:42
  129.7 1.7 %tail.1 = (bf16[16,1024]{1,0:T(8,128)(2,1)}, bf16[512,128]{1,0:T(8,128)(2,1)}) custom-call(bf16[16,1024]{1,0:T(8,128)(2,1)S(1)} %get-tuple-element.42.sequence_near, bf16[128,512]{1,0:T(8,128)(2,1)S(1)} %bitcast.18, f32[512,128]{1,0:T(8,128)S(1)} %get-tuple-element.55.mid, f32[512,128]{1,0:T(8,128)S(1)} %get-tuple-element.56.out_gate, ...), custom_call_target="tpu_custom_call" | custom-call | tf_op jit(solution)/shard_map/tail/pallas_call | solution.py:61
  (1 shorter events, 0.0 us)
Async XLA Ops:
  2.9 23.8 %all-to-all-start = ((bf16[32,16,128]{2,1,0:T(8,128)(2,1)}), bf16[32,16,128]{2,1,0:T(8,128)(2,1)S(1)}, u32[]{:S(2)}, u32[]{:S(2)}) async-start(bf16[32,16,128]{2,1,0:T(8,128)(2,1)} %get-tuple-element.32), calls=%async_computation | async-start | bytes 262144 | tf_op jit(solution)/shard_map/all_to_all | solution.py:42

commit v9 on v8

--- a/solution.py
+++ b/solution.py
@@ -9,7 +9,7 @@
 from jax.sharding import PartitionSpec as P
 
 ROW = ("row_0", "row_1")
-PAIR_AT = tuple((u // 4 + u + 3) % 4 * 4 + (u + 2) % 4 for u in range(16))
+PAIR_AT = tuple(u ^ 14 for u in range(16))
 PAIR_PLACE = tuple(PAIR_AT.index(q) for q in range(16))
 ROW_AT = tuple(2 * q + k for q in PAIR_AT for k in range(2))
 ROW_PLACE = tuple(ROW_AT.index(r) for r in range(32))

time: 132 us -> 132 us (level)
  no operation moved by 1% of the time
where the time goes in v9:
time: 132 us; the launch traced here: 131 us
  blocking collectives  99.7 us (76%)
  starting transfers between devices  18.5 us (14%)
  Pallas kernels  9.58 us (7%)
  waiting for transfers between devices  2.48 us (2%)
    all_to_all x7, blocking collectives, exchange(): lax.all_to_all(blocks, (*ROW, 'col'), split_axis=0, concat_axis=0, tiled=...  99.7 us
    all_to_all x1, starting transfers between devices, exchange(): lax.all_to_all(blocks, (*ROW, 'col'), split_axis=0, concat_axis=0, tiled=...  18.5 us
    pallas_call x8, Pallas kernels, local_kernel(): pl.pallas_call(body, out_shape=out_shape, in_specs=[pl.BlockSpec(memory_s...  9.58 us
  transfers between devices with their start and end apart: 1, of which 1 were waited for; matrix products, arithmetic and copies ran while one was open for 0% of the time, Pallas kernels for 2%

profile of v9, /device:TPU:1, one launch (start us, length us, event | category | flops | bytes accessed | tf_op | source)
XLA Modules:
  0.0 131.3 jit_solution(11578895936060980662)
XLA Ops:
  0.6 2.3 %project.1 = (bf16[32,16,128]{2,1,0:T(8,128)(2,1)}, f32[16,128]{1,0:T(8,128)S(1)}, f32[16,128]{1,0:T(8,128)S(1)}, bf16[16,1024]{1,0:T(8,128)(2,1)S(1)}) custom-call(bf16[16,1024]{1,0:T(8,128)(2,1)} %sequence.1, bf16[256,1024]{1,0:T(8,128)(2,1)} %bitcast.20), custom_call_target="tpu_custom_call" | custom-call | tf_op jit(solution)/shard_map/project/pallas_call | solution.py:61
  2.9 18.5 %all-to-all-start = ((bf16[32,16,128]{2,1,0:T(8,128)(2,1)}), bf16[32,16,128]{2,1,0:T(8,128)(2,1)S(1)}, u32[]{:S(2)}, u32[]{:S(2)}) async-start(bf16[32,16,128]{2,1,0:T(8,128)(2,1)} %get-tuple-element.32), calls=%async_computation | async-start | bytes 262144 | tf_op jit(solution)/shard_map/all_to_all | solution.py:42
  21.5 2.7 %prepare.1 = (bf16[16,32,128]{2,1,0:T(8,128)(2,1)S(1)}, bf16[64,1024]{1,0:T(8,128)(2,1)S(1)}, bf16[1024,128]{1,0:T(8,128)(2,1)S(1)}, bf16[128,128]{1,0:T(8,128)(...) custom-call(s32[1]{0:T(128)} %bitcast.2.row_start, ...), custom_call_target="tpu_custom_call" | custom-call | tf_op jit(solution)/shard_map/prepare/pallas_call | solution.py:61
  24.2 2.5 %all-to-all-done.key_values = bf16[32,16,128]{2,1,0:T(8,128)(2,1)S(1)} async-done(((bf16[32,16,128]{2,1,0:T(8,128)(2,1)}), bf16[32,16,128]{2,1,0:T(8,128)(2,1)S(1)}, u32[]{:S(2)}, u32[]{:S(2)}) %all-to-all-start) | async-done | bytes 131104 | tf_op jit(solution)/shard_map/all_to_all | solution.py:42
  26.7 11.8 %all_to_all.40.blocks = f32[16,8,128]{2,1,0:T(8,128)S(1)} all-to-all(f32[16,8,128]{2,1,0:T(8,128)S(1)} %get-tuple-element.34), channel_id=1, replica_groups={{1,5,9,13,0,4,8,12,3,7,11,15,2,6,10,14},{17,21,25,29,16,20,24,28,19,23,..., dimensions={0} | all-to-all | bytes 131072 | tf_op jit(solution)/shard_map/all_to_all | solution.py:42
  38.5 0.7 attention.1
  39.2 13.2 %all_to_all.41.terms = bf16[16,16,1024]{2,1,0:T(8,128)(2,1)S(1)} all-to-all(bf16[16,16,1024]{2,1,0:T(8,128)(2,1)S(1)} %attention.1), channel_id=1, replica_groups={{1,5,9,13,0,4,8,12,3,7,11,15,2,6,10,14},{17,21,25,29,16,20,24,28,19,23,..., dimensions={0} | all-to-all | bytes 1048576 | tf_op jit(solution)/shard_map/all_to_all | solution.py:42
  52.4 0.5 settle.1
  52.8 14.8 %all_to_all.42.rights = bf16[32,8,128]{2,1,0:T(8,128)(2,1)S(1)} all-to-all(bf16[32,8,128]{2,1,0:T(8,128)(2,1)S(1)} %get-tuple-element.43), channel_id=1, replica_groups={{448,464,480,496,384,400,416,432,320,336,352,368,256,272,288,304,192,20..., dimensions={0} | all-to-all | bytes 131072 | tf_op jit(solution)/shard_map/all_to_all | solution.py:42
  67.6 0.9 pair.1
  68.5 10.7 %all_to_all.43.tiles = bf16[16,16,512]{2,1,0:T(8,128)(2,1)S(1)} all-to-all(bf16[16,16,512]{2,1,0:T(8,128)(2,1)S(1)} %get-tuple-element.52), channel_id=1, replica_groups={{1,5,9,13,0,4,8,12,3,7,11,15,2,6,10,14},{17,21,25,29,16,20,24,28,19,23,..., dimensions={0} | all-to-all | bytes 524288 | tf_op jit(solution)/shard_map/all_to_all | solution.py:42
  79.2 0.5 spread.1
  79.7 21.4 %all_to_all.44 = bf16[32,24,256]{2,1,0:T(8,128)(2,1)S(1)} all-to-all(bf16[32,24,256]{2,1,0:T(8,128)(2,1)S(1)} %spread.1), channel_id=1, replica_groups={{448,464,480,496,384,400,416,432,320,336,352,368,256,272,288,304,192,20..., dimensions={0} | all-to-all | bytes 786432 | tf_op jit(solution)/shard_map/all_to_all | solution.py:42
  101.1 0.3 fusion
  101.4 17.9 %all_to_all.45.parts = bf16[32,8,512]{2,1,0:T(8,128)(2,1)S(1)} all-to-all(bf16[32,8,512]{2,1,0:T(8,128)(2,1)S(1)} %fusion), channel_id=1, replica_groups={{448,464,480,496,384,400,416,432,320,336,352,368,256,272,288,304,192,20..., dimensions={0} | all-to-all | bytes 524288 | tf_op jit(solution)/shard_map/all_to_all | solution.py:42
  119.3 0.3 gather.1
  119.6 10.0 %all_to_all.46 = bf16[16,8,512]{2,1,0:T(8,128)(2,1)S(1)} all-to-all(bf16[16,8,512]{2,1,0:T(8,128)(2,1)S(1)} %gather.1), channel_id=1, replica_groups={{1,5,9,13,0,4,8,12,3,7,11,15,2,6,10,14},{17,21,25,29,16,20,24,28,19,23,..., dimensions={0} | all-to-all | bytes 262144 | tf_op jit(solution)/shard_map/all_to_all | solution.py:42
  129.6 1.7 %tail.1 = (bf16[16,1024]{1,0:T(8,128)(2,1)}, bf16[512,128]{1,0:T(8,128)(2,1)}) custom-call(bf16[16,1024]{1,0:T(8,128)(2,1)S(1)} %get-tuple-element.42.sequence_near, bf16[128,512]{1,0:T(8,128)(2,1)S(1)} %bitcast.18, f32[512,128]{1,0:T(8,128)S(1)} %get-tuple-element.55.mid, f32[512,128]{1,0:T(8,128)S(1)} %get-tuple-element.56.out_gate, ...), custom_call_target="tpu_custom_call" | custom-call | tf_op jit(solution)/shard_map/tail/pallas_call | solution.py:61
  (1 shorter events, 0.0 us)
Async XLA Ops:
  2.9 23.8 %all-to-all-start = ((bf16[32,16,128]{2,1,0:T(8,128)(2,1)}), bf16[32,16,128]{2,1,0:T(8,128)(2,1)S(1)}, u32[]{:S(2)}, u32[]{:S(2)}) async-start(bf16[32,16,128]{2,1,0:T(8,128)(2,1)} %get-tuple-element.32), calls=%async_computation | async-start | bytes 262144 | tf_op jit(solution)/shard_map/all_to_all | solution.py:42

commit v10 on v9

--- a/solution.py
+++ b/solution.py
@@ -9,7 +9,7 @@
 from jax.sharding import PartitionSpec as P
 
 ROW = ("row_0", "row_1")
-PAIR_AT = tuple(u ^ 14 for u in range(16))
+PAIR_AT = tuple(u ^ 10 for u in range(16))
 PAIR_PLACE = tuple(PAIR_AT.index(q) for q in range(16))
 ROW_AT = tuple(2 * q + k for q in PAIR_AT for k in range(2))
 ROW_PLACE = tuple(ROW_AT.index(r) for r in range(32))
@@ -98,8 +98,7 @@
 
 
 def project_body(sequence, weights, key_values, query, gate, near, held, arrived):
-    each = LANES // 4
-    parts = [pl.ds(k * each, each) for k in range(8)]
+    parts = [pl.ds(k * LANES, LANES) for k in range(2)]
     first_copy, *weight_copies = fetch(
         (sequence, *[weights.at[part] for part in parts]),
         (near, *[held.at[part] for part in parts]),
@@ -108,10 +107,9 @@
     first_copy.wait()
     normed = layer_norm(near[...].astype(F32)).astype(BF16)
     projected = []
-    for half in range(2):
-        for copy in weight_copies[half * 4 : half * 4 + 4]:
-            copy.wait()
-        projected.append(mm(normed, held[half * LANES : (half + 1) * LANES], 1, 1))
+    for part, copy in zip(parts, weight_copies):
+        copy.wait()
+        projected.append(mm(normed, held[part], 1, 1))
     head, rest = projected
     rows = head.shape[0]
     first = lax.broadcasted_iota(jnp.int32, (rows, LANES), 1) < LANES // 2
@@ -430,7 +428,7 @@
         "project",
         sequence,
         weights,
-        scratch=(pltpu.VMEM(weights.shape, BF16), pltpu.SemaphoreType.DMA((9,))),
+        scratch=(pltpu.VMEM(weights.shape, BF16), pltpu.SemaphoreType.DMA((3,))),
         far=True,
     )
     key_values_all = exchange(key_values, ROW)

time: 132 us -> 131 us (level)
  waiting for transfers between devices: 2.48 us -> 0.51 us
    all_to_all x1, waiting for transfers between devices: 2.48 us -> 0.51 us  [exchange(): lax.all_to_all(blocks, (*ROW, 'col'), split_axis=0, concat_axis=0, tiled=...]
where the time goes in v10:
time: 131 us; the launch traced here: 130 us
  blocking collectives  100 us (76%)
  starting transfers between devices  18.7 us (14%)
  Pallas kernels  9.54 us (7%)
    all_to_all x7, blocking collectives, exchange(): lax.all_to_all(blocks, (*ROW, 'col'), split_axis=0, concat_axis=0, tiled=...  100 us
    all_to_all x1, starting transfers between devices, exchange(): lax.all_to_all(blocks, (*ROW, 'col'), split_axis=0, concat_axis=0, tiled=...  18.7 us
    pallas_call x8, Pallas kernels, local_kernel(): pl.pallas_call(body, out_shape=out_shape, in_specs=[pl.BlockSpec(memory_s...  9.54 us
  transfers between devices with their start and end apart: 1, of which 1 were waited for; matrix products, arithmetic and copies ran while one was open for 0% of the time, Pallas kernels for 2%

profile of v10, /device:TPU:1, one launch (start us, length us, event | category | flops | bytes accessed | tf_op | source)
XLA Modules:
  0.0 130.1 jit_solution(18063036672694806236)
XLA Ops:
  0.6 2.2 %project.1 = (bf16[32,16,128]{2,1,0:T(8,128)(2,1)}, f32[16,128]{1,0:T(8,128)S(1)}, f32[16,128]{1,0:T(8,128)S(1)}, bf16[16,1024]{1,0:T(8,128)(2,1)S(1)}) custom-call(bf16[16,1024]{1,0:T(8,128)(2,1)} %sequence.1, bf16[256,1024]{1,0:T(8,128)(2,1)} %bitcast.20), custom_call_target="tpu_custom_call" | custom-call | tf_op jit(solution)/shard_map/project/pallas_call | solution.py:61
  2.9 18.7 %all-to-all-start = ((bf16[32,16,128]{2,1,0:T(8,128)(2,1)}), bf16[32,16,128]{2,1,0:T(8,128)(2,1)S(1)}, u32[]{:S(2)}, u32[]{:S(2)}) async-start(bf16[32,16,128]{2,1,0:T(8,128)(2,1)} %get-tuple-element.32), calls=%async_computation | async-start | bytes 262144 | tf_op jit(solution)/shard_map/all_to_all | solution.py:42
  21.6 2.7 %prepare.1 = (bf16[16,32,128]{2,1,0:T(8,128)(2,1)S(1)}, bf16[64,1024]{1,0:T(8,128)(2,1)S(1)}, bf16[1024,128]{1,0:T(8,128)(2,1)S(1)}, bf16[128,128]{1,0:T(8,128)(...) custom-call(s32[1]{0:T(128)} %bitcast.2.row_start, ...), custom_call_target="tpu_custom_call" | custom-call | tf_op jit(solution)/shard_map/prepare/pallas_call | solution.py:61
  24.3 0.5 all-to-all-done.key_values
  24.8 12.2 %all_to_all.40.blocks = f32[16,8,128]{2,1,0:T(8,128)S(1)} all-to-all(f32[16,8,128]{2,1,0:T(8,128)S(1)} %get-tuple-element.34), channel_id=1, replica_groups={{1,5,9,13,0,4,8,12,3,7,11,15,2,6,10,14},{17,21,25,29,16,20,24,28,19,23,..., dimensions={0} | all-to-all | bytes 131072 | tf_op jit(solution)/shard_map/all_to_all | solution.py:42
  37.0 0.7 attention.1
  37.7 13.2 %all_to_all.41.terms = bf16[16,16,1024]{2,1,0:T(8,128)(2,1)S(1)} all-to-all(bf16[16,16,1024]{2,1,0:T(8,128)(2,1)S(1)} %attention.1), channel_id=1, replica_groups={{1,5,9,13,0,4,8,12,3,7,11,15,2,6,10,14},{17,21,25,29,16,20,24,28,19,23,..., dimensions={0} | all-to-all | bytes 1048576 | tf_op jit(solution)/shard_map/all_to_all | solution.py:42
  50.9 0.5 settle.1
  51.4 14.7 %all_to_all.42.rights = bf16[32,8,128]{2,1,0:T(8,128)(2,1)S(1)} all-to-all(bf16[32,8,128]{2,1,0:T(8,128)(2,1)S(1)} %get-tuple-element.43), channel_id=1, replica_groups={{320,336,352,368,256,272,288,304,448,464,480,496,384,400,416,432,64,80,..., dimensions={0} | all-to-all | bytes 131072 | tf_op jit(solution)/shard_map/all_to_all | solution.py:42
  66.1 0.9 pair.1
  67.0 10.6 %all_to_all.43.tiles = bf16[16,16,512]{2,1,0:T(8,128)(2,1)S(1)} all-to-all(bf16[16,16,512]{2,1,0:T(8,128)(2,1)S(1)} %get-tuple-element.52), channel_id=1, replica_groups={{1,5,9,13,0,4,8,12,3,7,11,15,2,6,10,14},{17,21,25,29,16,20,24,28,19,23,..., dimensions={0} | all-to-all | bytes 524288 | tf_op jit(solution)/shard_map/all_to_all | solution.py:42
  77.7 0.5 spread.1
  78.1 22.4 %all_to_all.44 = bf16[32,24,256]{2,1,0:T(8,128)(2,1)S(1)} all-to-all(bf16[32,24,256]{2,1,0:T(8,128)(2,1)S(1)} %spread.1), channel_id=1, replica_groups={{320,336,352,368,256,272,288,304,448,464,480,496,384,400,416,432,64,80,..., dimensions={0} | all-to-all | bytes 786432 | tf_op jit(solution)/shard_map/all_to_all | solution.py:42
  100.6 0.3 fusion
  100.8 17.7 %all_to_all.45.parts = bf16[32,8,512]{2,1,0:T(8,128)(2,1)S(1)} all-to-all(bf16[32,8,512]{2,1,0:T(8,128)(2,1)S(1)} %fusion), channel_id=1, replica_groups={{320,336,352,368,256,272,288,304,448,464,480,496,384,400,416,432,64,80,..., dimensions={0} | all-to-all | bytes 524288 | tf_op jit(solution)/shard_map/all_to_all | solution.py:42
  118.5 0.3 gather.1
  118.9 9.5 %all_to_all.46 = bf16[16,8,512]{2,1,0:T(8,128)(2,1)S(1)} all-to-all(bf16[16,8,512]{2,1,0:T(8,128)(2,1)S(1)} %gather.1), channel_id=1, replica_groups={{1,5,9,13,0,4,8,12,3,7,11,15,2,6,10,14},{17,21,25,29,16,20,24,28,19,23,..., dimensions={0} | all-to-all | bytes 262144 | tf_op jit(solution)/shard_map/all_to_all | solution.py:42
  128.4 1.7 %tail.1 = (bf16[16,1024]{1,0:T(8,128)(2,1)}, bf16[512,128]{1,0:T(8,128)(2,1)}) custom-call(bf16[16,1024]{1,0:T(8,128)(2,1)S(1)} %get-tuple-element.42.sequence_near, bf16[128,512]{1,0:T(8,128)(2,1)S(1)} %bitcast.18, f32[512,128]{1,0:T(8,128)S(1)} %get-tuple-element.55.mid, f32[512,128]{1,0:T(8,128)S(1)} %get-tuple-element.56.out_gate, ...), custom_call_target="tpu_custom_call" | custom-call | tf_op jit(solution)/shard_map/tail/pallas_call | solution.py:61
  (1 shorter events, 0.0 us)
Async XLA Ops:
  2.9 22.0 %all-to-all-start = ((bf16[32,16,128]{2,1,0:T(8,128)(2,1)}), bf16[32,16,128]{2,1,0:T(8,128)(2,1)S(1)}, u32[]{:S(2)}, u32[]{:S(2)}) async-start(bf16[32,16,128]{2,1,0:T(8,128)(2,1)} %get-tuple-element.32), calls=%async_computation | async-start | bytes 262144 | tf_op jit(solution)/shard_map/all_to_all | solution.py:42

commit v11 on v10

--- a/solution.py
+++ b/solution.py
@@ -9,7 +9,7 @@
 from jax.sharding import PartitionSpec as P
 
 ROW = ("row_0", "row_1")
-PAIR_AT = tuple(u ^ 10 for u in range(16))
+PAIR_AT = tuple(u ^ 4 for u in range(16))
 PAIR_PLACE = tuple(PAIR_AT.index(q) for q in range(16))
 ROW_AT = tuple(2 * q + k for q in PAIR_AT for k in range(2))
 ROW_PLACE = tuple(ROW_AT.index(r) for r in range(32))

time: 131 us -> 136 us (1.038)
  waiting for transfers between devices: 0.51 us -> 7.35 us
    all_to_all x1, waiting for transfers between devices: 0.51 us -> 7.35 us  [exchange(): lax.all_to_all(blocks, (*ROW, 'col'), split_axis=0, concat_axis=0, tiled=...]
where the time goes in v11:
time: 136 us
  blocking collectives  99.6 us (73%)
  starting transfers between devices  18.4 us (14%)
  Pallas kernels  9.53 us (7%)
  waiting for transfers between devices  7.35 us (5%)
    all_to_all x7, blocking collectives, exchange(): lax.all_to_all(blocks, (*ROW, 'col'), split_axis=0, concat_axis=0, tiled=...  99.6 us
    all_to_all x1, starting transfers between devices, exchange(): lax.all_to_all(blocks, (*ROW, 'col'), split_axis=0, concat_axis=0, tiled=...  18.4 us
    pallas_call x8, Pallas kernels, local_kernel(): pl.pallas_call(body, out_shape=out_shape, in_specs=[pl.BlockSpec(memory_s...  9.53 us
    all_to_all x1, waiting for transfers between devices, exchange(): lax.all_to_all(blocks, (*ROW, 'col'), split_axis=0, concat_axis=0, tiled=...  7.35 us
  transfers between devices with their start and end apart: 1, of which 1 were waited for; matrix products, arithmetic and copies ran while one was open for 0% of the time, Pallas kernels for 2%

profile of v11, /device:TPU:1, one launch (start us, length us, event | category | flops | bytes accessed | tf_op | source)
XLA Modules:
  0.0 135.8 jit_solution(10161463725808966140)
XLA Ops:
  0.6 2.2 %project.1 = (bf16[32,16,128]{2,1,0:T(8,128)(2,1)}, f32[16,128]{1,0:T(8,128)S(1)}, f32[16,128]{1,0:T(8,128)S(1)}, bf16[16,1024]{1,0:T(8,128)(2,1)S(1)}) custom-call(bf16[16,1024]{1,0:T(8,128)(2,1)} %sequence.1, bf16[256,1024]{1,0:T(8,128)(2,1)} %bitcast.20), custom_call_target="tpu_custom_call" | custom-call | tf_op jit(solution)/shard_map/project/pallas_call | solution.py:61
  2.9 18.4 %all-to-all-start = ((bf16[32,16,128]{2,1,0:T(8,128)(2,1)}), bf16[32,16,128]{2,1,0:T(8,128)(2,1)S(1)}, u32[]{:S(2)}, u32[]{:S(2)}) async-start(bf16[32,16,128]{2,1,0:T(8,128)(2,1)} %get-tuple-element.32), calls=%async_computation | async-start | bytes 262144 | tf_op jit(solution)/shard_map/all_to_all | solution.py:42
  21.2 2.7 %prepare.1 = (bf16[16,32,128]{2,1,0:T(8,128)(2,1)S(1)}, bf16[64,1024]{1,0:T(8,128)(2,1)S(1)}, bf16[1024,128]{1,0:T(8,128)(2,1)S(1)}, bf16[128,128]{1,0:T(8,128)(...) custom-call(s32[1]{0:T(128)} %bitcast.2.row_start, ...), custom_call_target="tpu_custom_call" | custom-call | tf_op jit(solution)/shard_map/prepare/pallas_call | solution.py:61
  24.0 7.3 %all-to-all-done.key_values = bf16[32,16,128]{2,1,0:T(8,128)(2,1)S(1)} async-done(((bf16[32,16,128]{2,1,0:T(8,128)(2,1)}), bf16[32,16,128]{2,1,0:T(8,128)(2,1)S(1)}, u32[]{:S(2)}, u32[]{:S(2)}) %all-to-all-start) | async-done | bytes 131104 | tf_op jit(solution)/shard_map/all_to_all | solution.py:42
  31.3 12.5 %all_to_all.40.blocks = f32[16,8,128]{2,1,0:T(8,128)S(1)} all-to-all(f32[16,8,128]{2,1,0:T(8,128)S(1)} %get-tuple-element.34), channel_id=1, replica_groups={{1,5,9,13,0,4,8,12,3,7,11,15,2,6,10,14},{17,21,25,29,16,20,24,28,19,23,..., dimensions={0} | all-to-all | bytes 131072 | tf_op jit(solution)/shard_map/all_to_all | solution.py:42
  43.8 0.7 attention.1
  44.5 13.2 %all_to_all.41.terms = bf16[16,16,1024]{2,1,0:T(8,128)(2,1)S(1)} all-to-all(bf16[16,16,1024]{2,1,0:T(8,128)(2,1)S(1)} %attention.1), channel_id=1, replica_groups={{1,5,9,13,0,4,8,12,3,7,11,15,2,6,10,14},{17,21,25,29,16,20,24,28,19,23,..., dimensions={0} | all-to-all | bytes 1048576 | tf_op jit(solution)/shard_map/all_to_all | solution.py:42
  57.7 0.5 settle.1
  58.1 14.7 %all_to_all.42.rights = bf16[32,8,128]{2,1,0:T(8,128)(2,1)S(1)} all-to-all(bf16[32,8,128]{2,1,0:T(8,128)(2,1)S(1)} %get-tuple-element.43), channel_id=1, replica_groups={{128,144,160,176,192,208,224,240,0,16,32,48,64,80,96,112,384,400,416,43..., dimensions={0} | all-to-all | bytes 131072 | tf_op jit(solution)/shard_map/all_to_all | solution.py:42
  72.9 0.9 pair.1
  73.8 11.1 %all_to_all.43.tiles = bf16[16,16,512]{2,1,0:T(8,128)(2,1)S(1)} all-to-all(bf16[16,16,512]{2,1,0:T(8,128)(2,1)S(1)} %get-tuple-element.52), channel_id=1, replica_groups={{1,5,9,13,0,4,8,12,3,7,11,15,2,6,10,14},{17,21,25,29,16,20,24,28,19,23,..., dimensions={0} | all-to-all | bytes 524288 | tf_op jit(solution)/shard_map/all_to_all | solution.py:42
  84.9 0.5 spread.1
  85.3 18.9 %all_to_all.44 = bf16[32,24,256]{2,1,0:T(8,128)(2,1)S(1)} all-to-all(bf16[32,24,256]{2,1,0:T(8,128)(2,1)S(1)} %spread.1), channel_id=1, replica_groups={{128,144,160,176,192,208,224,240,0,16,32,48,64,80,96,112,384,400,416,43..., dimensions={0} | all-to-all | bytes 786432 | tf_op jit(solution)/shard_map/all_to_all | solution.py:42
  104.3 0.3 fusion
  104.5 18.1 %all_to_all.45.parts = bf16[32,8,512]{2,1,0:T(8,128)(2,1)S(1)} all-to-all(bf16[32,8,512]{2,1,0:T(8,128)(2,1)S(1)} %fusion), channel_id=1, replica_groups={{128,144,160,176,192,208,224,240,0,16,32,48,64,80,96,112,384,400,416,43..., dimensions={0} | all-to-all | bytes 524288 | tf_op jit(solution)/shard_map/all_to_all | solution.py:42
  122.7 0.3 gather.1
  123.0 11.1 %all_to_all.46 = bf16[16,8,512]{2,1,0:T(8,128)(2,1)S(1)} all-to-all(bf16[16,8,512]{2,1,0:T(8,128)(2,1)S(1)} %gather.1), channel_id=1, replica_groups={{1,5,9,13,0,4,8,12,3,7,11,15,2,6,10,14},{17,21,25,29,16,20,24,28,19,23,..., dimensions={0} | all-to-all | bytes 262144 | tf_op jit(solution)/shard_map/all_to_all | solution.py:42
  134.1 1.7 %tail.1 = (bf16[16,1024]{1,0:T(8,128)(2,1)}, bf16[512,128]{1,0:T(8,128)(2,1)}) custom-call(bf16[16,1024]{1,0:T(8,128)(2,1)S(1)} %get-tuple-element.42.sequence_near, bf16[128,512]{1,0:T(8,128)(2,1)S(1)} %bitcast.18, f32[512,128]{1,0:T(8,128)S(1)} %get-tuple-element.55.mid, f32[512,128]{1,0:T(8,128)S(1)} %get-tuple-element.56.out_gate, ...), custom_call_target="tpu_custom_call" | custom-call | tf_op jit(solution)/shard_map/tail/pallas_call | solution.py:61
  (1 shorter events, 0.0 us)
Async XLA Ops:
  2.9 28.5 %all-to-all-start = ((bf16[32,16,128]{2,1,0:T(8,128)(2,1)}), bf16[32,16,128]{2,1,0:T(8,128)(2,1)S(1)}, u32[]{:S(2)}, u32[]{:S(2)}) async-start(bf16[32,16,128]{2,1,0:T(8,128)(2,1)} %get-tuple-element.32), calls=%async_computation | async-start | bytes 262144 | tf_op jit(solution)/shard_map/all_to_all | solution.py:42

commit v12 on v10

--- a/solution.py
+++ b/solution.py
@@ -13,7 +13,7 @@
 PAIR_PLACE = tuple(PAIR_AT.index(q) for q in range(16))
 ROW_AT = tuple(2 * q + k for q in PAIR_AT for k in range(2))
 ROW_PLACE = tuple(ROW_AT.index(r) for r in range(32))
-COL_AT = tuple(p % 4 * 4 + (p // 4 ^ 1) for p in range(16))
+COL_AT = tuple((p + 2) % 4 * 4 + (p // 4 ^ 1) for p in range(16))
 COL_PLACE = tuple(COL_AT.index(q) for q in range(16))
 BF16 = jnp.bfloat16
 F32 = jnp.float32
@@ -162,7 +162,7 @@
     n = lax.broadcasted_iota(jnp.int32, (heads, heads), 0)
     m = lax.broadcasted_iota(jnp.int32, (heads, heads), 1)
     place = n // 2
-    by_place = jnp.where(m == (place % 4 * 4 + (place // 4 ^ 1)) * 2 + n % 2, 1.0, 0.0).astype(BF16)
+    by_place = jnp.where(m == ((place + 2) % 4 * 4 + (place // 4 ^ 1)) * 2 + n % 2, 1.0, 0.0).astype(BF16)
     bias = mm(mm(by_place, bias_near[...], 1, 0).astype(BF16), normed, 1, 1)
     columns = blocks.shape[0]
     for t in range(GROUPS):

time: 131 us -> 128 us (0.977)
  blocking collectives: 100 us -> 98.1 us
    all_to_all x7, blocking collectives: 100 us -> 98.1 us  [exchange(): lax.all_to_all(blocks, (*ROW, 'col'), split_axis=0, concat_axis=0, tiled=...]
where the time goes in v12:
time: 128 us
  blocking collectives  98.1 us (77%)
  starting transfers between devices  18.7 us (15%)
  Pallas kernels  9.54 us (7%)
    all_to_all x7, blocking collectives, exchange(): lax.all_to_all(blocks, (*ROW, 'col'), split_axis=0, concat_axis=0, tiled=...  98.1 us
    all_to_all x1, starting transfers between devices, exchange(): lax.all_to_all(blocks, (*ROW, 'col'), split_axis=0, concat_axis=0, tiled=...  18.7 us
    pallas_call x8, Pallas kernels, local_kernel(): pl.pallas_call(body, out_shape=out_shape, in_specs=[pl.BlockSpec(memory_s...  9.54 us
  transfers between devices with their start and end apart: 1, of which 1 were waited for; matrix products, arithmetic and copies ran while one was open for 0% of the time, Pallas kernels for 2%

profile of v12, /device:TPU:1, one launch (start us, length us, event | category | flops | bytes accessed | tf_op | source)
XLA Modules:
  0.0 127.8 jit_solution(8353882825308317587)
XLA Ops:
  0.6 2.2 %project.1 = (bf16[32,16,128]{2,1,0:T(8,128)(2,1)}, f32[16,128]{1,0:T(8,128)S(1)}, f32[16,128]{1,0:T(8,128)S(1)}, bf16[16,1024]{1,0:T(8,128)(2,1)S(1)}) custom-call(bf16[16,1024]{1,0:T(8,128)(2,1)} %sequence.1, bf16[256,1024]{1,0:T(8,128)(2,1)} %bitcast.20), custom_call_target="tpu_custom_call" | custom-call | tf_op jit(solution)/shard_map/project/pallas_call | solution.py:61
  2.9 18.7 %all-to-all-start = ((bf16[32,16,128]{2,1,0:T(8,128)(2,1)}), bf16[32,16,128]{2,1,0:T(8,128)(2,1)S(1)}, u32[]{:S(2)}, u32[]{:S(2)}) async-start(bf16[32,16,128]{2,1,0:T(8,128)(2,1)} %get-tuple-element.32), calls=%async_computation | async-start | bytes 262144 | tf_op jit(solution)/shard_map/all_to_all | solution.py:42
  21.6 2.7 %prepare.1 = (bf16[16,32,128]{2,1,0:T(8,128)(2,1)S(1)}, bf16[64,1024]{1,0:T(8,128)(2,1)S(1)}, bf16[1024,128]{1,0:T(8,128)(2,1)S(1)}, bf16[128,128]{1,0:T(8,128)(...) custom-call(s32[1]{0:T(128)} %bitcast.2.row_start, ...), custom_call_target="tpu_custom_call" | custom-call | tf_op jit(solution)/shard_map/prepare/pallas_call | solution.py:61
  24.3 0.5 all-to-all-done.key_values
  24.8 10.5 %all_to_all.40.blocks = f32[16,8,128]{2,1,0:T(8,128)S(1)} all-to-all(f32[16,8,128]{2,1,0:T(8,128)S(1)} %get-tuple-element.34), channel_id=1, replica_groups={{9,13,1,5,8,12,0,4,11,15,3,7,10,14,2,6},{25,29,17,21,24,28,16,20,27,31,..., dimensions={0} | all-to-all | bytes 131072 | tf_op jit(solution)/shard_map/all_to_all | solution.py:42
  35.4 0.7 attention.1
  36.1 12.5 %all_to_all.41.terms = bf16[16,16,1024]{2,1,0:T(8,128)(2,1)S(1)} all-to-all(bf16[16,16,1024]{2,1,0:T(8,128)(2,1)S(1)} %attention.1), channel_id=1, replica_groups={{9,13,1,5,8,12,0,4,11,15,3,7,10,14,2,6},{25,29,17,21,24,28,16,20,27,31,..., dimensions={0} | all-to-all | bytes 1048576 | tf_op jit(solution)/shard_map/all_to_all | solution.py:42
  48.6 0.5 settle.1
  49.1 14.1 %all_to_all.42.rights = bf16[32,8,128]{2,1,0:T(8,128)(2,1)S(1)} all-to-all(bf16[32,8,128]{2,1,0:T(8,128)(2,1)S(1)} %get-tuple-element.43), channel_id=1, replica_groups={{320,336,352,368,256,272,288,304,448,464,480,496,384,400,416,432,64,80,..., dimensions={0} | all-to-all | bytes 131072 | tf_op jit(solution)/shard_map/all_to_all | solution.py:42
  63.1 0.9 pair.1
  64.0 11.3 %all_to_all.43.tiles = bf16[16,16,512]{2,1,0:T(8,128)(2,1)S(1)} all-to-all(bf16[16,16,512]{2,1,0:T(8,128)(2,1)S(1)} %get-tuple-element.52), channel_id=1, replica_groups={{9,13,1,5,8,12,0,4,11,15,3,7,10,14,2,6},{25,29,17,21,24,28,16,20,27,31,..., dimensions={0} | all-to-all | bytes 524288 | tf_op jit(solution)/shard_map/all_to_all | solution.py:42
  75.3 0.5 spread.1
  75.8 21.8 %all_to_all.44 = bf16[32,24,256]{2,1,0:T(8,128)(2,1)S(1)} all-to-all(bf16[32,24,256]{2,1,0:T(8,128)(2,1)S(1)} %spread.1), channel_id=1, replica_groups={{320,336,352,368,256,272,288,304,448,464,480,496,384,400,416,432,64,80,..., dimensions={0} | all-to-all | bytes 786432 | tf_op jit(solution)/shard_map/all_to_all | solution.py:42
  97.6 0.3 fusion
  97.9 17.7 %all_to_all.45.parts = bf16[32,8,512]{2,1,0:T(8,128)(2,1)S(1)} all-to-all(bf16[32,8,512]{2,1,0:T(8,128)(2,1)S(1)} %fusion), channel_id=1, replica_groups={{320,336,352,368,256,272,288,304,448,464,480,496,384,400,416,432,64,80,..., dimensions={0} | all-to-all | bytes 524288 | tf_op jit(solution)/shard_map/all_to_all | solution.py:42
  115.6 0.3 gather.1
  115.9 10.2 %all_to_all.46 = bf16[16,8,512]{2,1,0:T(8,128)(2,1)S(1)} all-to-all(bf16[16,8,512]{2,1,0:T(8,128)(2,1)S(1)} %gather.1), channel_id=1, replica_groups={{9,13,1,5,8,12,0,4,11,15,3,7,10,14,2,6},{25,29,17,21,24,28,16,20,27,31,..., dimensions={0} | all-to-all | bytes 262144 | tf_op jit(solution)/shard_map/all_to_all | solution.py:42
  126.1 1.7 %tail.1 = (bf16[16,1024]{1,0:T(8,128)(2,1)}, bf16[512,128]{1,0:T(8,128)(2,1)}) custom-call(bf16[16,1024]{1,0:T(8,128)(2,1)S(1)} %get-tuple-element.42.sequence_near, bf16[128,512]{1,0:T(8,128)(2,1)S(1)} %bitcast.18, f32[512,128]{1,0:T(8,128)S(1)} %get-tuple-element.55.mid, f32[512,128]{1,0:T(8,128)S(1)} %get-tuple-element.56.out_gate, ...), custom_call_target="tpu_custom_call" | custom-call | tf_op jit(solution)/shard_map/tail/pallas_call | solution.py:61
  (1 shorter events, 0.0 us)
Async XLA Ops:
  2.9 22.0 %all-to-all-start = ((bf16[32,16,128]{2,1,0:T(8,128)(2,1)}), bf16[32,16,128]{2,1,0:T(8,128)(2,1)S(1)}, u32[]{:S(2)}, u32[]{:S(2)}) async-start(bf16[32,16,128]{2,1,0:T(8,128)(2,1)} %get-tuple-element.32), calls=%async_computation | async-start | bytes 262144 | tf_op jit(solution)/shard_map/all_to_all | solution.py:42
